TPU v7x, 256 devices: a whole 4x4x8 slice. The times are simulated.
256 devices in a mesh: fsdp: 256 (over z, y, x, core).
Axes of the slice: x: 4, y: 4, z: 8, core: 2. Of those that a mesh axis runs over, the one named last changes fastest.
Arguments:
- x: bfloat16 [512, 512, 512], P('fsdp')
- lengths: int32 [512], P('fsdp')
- d_y: bfloat16 [512, 512, 512], P('fsdp')
- w_attn: bfloat16 [2, 4, 512, 512], P(None, None, 'fsdp')
- b_attn: bfloat16 [2, 4, 512], P(None, None, 'fsdp')
- ln_par: bfloat16 [2, 4, 512], P(None, None, 'fsdp')
- w_up: bfloat16 [2, 512, 2048], P(None, 'fsdp')
- b_up: bfloat16 [2, 2048], P(None, 'fsdp')
- w_down: bfloat16 [2, 2048, 512], P(None, 'fsdp')
- b_down: bfloat16 [2, 512], P(None, 'fsdp')
Outputs:
- output 1: bfloat16 [512, 512, 512], P('fsdp')
- output 2: float32 [2, 4, 512, 512], P(None, None, 'fsdp')
- output 3: float32 [2, 4, 512], P(None, None, 'fsdp')
- output 4: float32 [2, 4, 512], P(None, None, 'fsdp')
- output 5: float32 [2, 512, 2048], P(None, 'fsdp')
- output 6: float32 [2, 2048], P(None, 'fsdp')
- output 7: float32 [2, 2048, 512], P(None, 'fsdp')
- output 8: float32 [2, 512], P(None, 'fsdp')
All inputs are finite; a program needn't handle non-finite values.
Results may differ from a plain program's by a relative error of at most 0.0133472.
Values are sent between devices in bfloat16 or wider.
A program may use at most 768 MiB of HBM per device.

v0:
```python
import math
import functools
import jax
import jax.numpy as jnp
from jax import lax
from jax.sharding import PartitionSpec as P

HEAD_DIM = 64
EPS = 1e-5
THETA = 10000.0
NEG_BIG = -1e30


def rotary_tables(seq_len):
    half_dim = HEAD_DIM // 2
    inv_freq = 1.0 / (THETA ** (jnp.arange(half_dim, dtype=jnp.float32) * (2.0 / HEAD_DIM)))
    angles = jnp.arange(seq_len, dtype=jnp.float32)[:, None] * inv_freq[None, :]
    return jnp.cos(angles)[:, None, :], jnp.sin(angles)[:, None, :]


def rotate(tensor, cos_tab, sin_tab):
    half_dim = HEAD_DIM // 2
    first_half = tensor[..., :half_dim]
    second_half = tensor[..., half_dim:]
    return jnp.concatenate([first_half * cos_tab - second_half * sin_tab, second_half * cos_tab + first_half * sin_tab], axis=-1)


def rotate_back(tensor, cos_tab, sin_tab):
    half_dim = HEAD_DIM // 2
    first_half = tensor[..., :half_dim]
    second_half = tensor[..., half_dim:]
    return jnp.concatenate([first_half * cos_tab + second_half * sin_tab, second_half * cos_tab - first_half * sin_tab], axis=-1)


def norm_fwd(x_in, gain, shift):
    row_mean = jnp.mean(x_in, axis=-1, keepdims=True)
    centered = x_in - row_mean
    variance = jnp.mean(centered * centered, axis=-1, keepdims=True)
    return centered * lax.rsqrt(variance + EPS) * gain + shift


def gelu_slope(pre_act):
    normal_cdf = 0.5 * (1.0 + lax.erf(pre_act * (1.0 / math.sqrt(2.0))))
    density = jnp.exp(-0.5 * pre_act * pre_act) * (1.0 / math.sqrt(2.0 * math.pi))
    return normal_cdf + pre_act * density


def layer_forward(x, weights, lengths, tables):
    w_attn, b_attn, ln_par, w_up, b_up, w_down, b_down = weights
    cos_tab, sin_tab = tables
    num_seq, seq_len, model_dim = x.shape
    num_heads = model_dim // HEAD_DIM
    x_f32 = x.astype(jnp.float32)
    h_one = norm_fwd(x_f32, ln_par[0].astype(jnp.float32), ln_par[1].astype(jnp.float32)).astype(jnp.bfloat16)
    projected = jnp.einsum('bld,kde->kble', h_one, w_attn[:3], preferred_element_type=jnp.float32)
    projected = (projected + b_attn[:3, None, None, :].astype(jnp.float32)).reshape(3, num_seq, seq_len, num_heads, HEAD_DIM)
    query_rot = rotate(projected[0] * (HEAD_DIM ** -0.5), cos_tab, sin_tab).astype(jnp.bfloat16)
    key_rot = rotate(projected[1], cos_tab, sin_tab).astype(jnp.bfloat16)
    values = projected[2].astype(jnp.bfloat16)
    scores = jnp.einsum('bqhd,bkhd->bhqk', query_rot, key_rot, preferred_element_type=jnp.float32)
    key_valid = jnp.arange(seq_len)[None, None, None, :] < lengths[:, None, None, None]
    probs_bf = jax.nn.softmax(jnp.where(key_valid, scores, NEG_BIG), axis=-1).astype(jnp.bfloat16)
    context = jnp.einsum('bhqk,bkhd->bqhd', probs_bf, values, preferred_element_type=jnp.float32)
    context = context.astype(jnp.bfloat16).reshape(num_seq, seq_len, model_dim)
    attn_out = jnp.einsum('bld,de->ble', context, w_attn[3], preferred_element_type=jnp.float32)
    x_mid = (x_f32 + attn_out + b_attn[3].astype(jnp.float32)).astype(jnp.bfloat16)
    mid_f32 = x_mid.astype(jnp.float32)
    h_two = norm_fwd(mid_f32, ln_par[2].astype(jnp.float32), ln_par[3].astype(jnp.float32)).astype(jnp.bfloat16)
    pre_act = jnp.einsum('bld,df->blf', h_two, w_up, preferred_element_type=jnp.float32) + b_up.astype(jnp.float32)
    act_bf = jax.nn.gelu(pre_act, approximate=False).astype(jnp.bfloat16)
    mlp_out = jnp.einsum('blf,fd->bld', act_bf, w_down, preferred_element_type=jnp.float32)
    y_out = (mid_f32 + mlp_out + b_down.astype(jnp.float32)).astype(jnp.bfloat16)
    saved_acts = (x, h_one, query_rot, key_rot, values, probs_bf, context, x_mid, h_two, pre_act, act_bf)
    return y_out, saved_acts


def layer_backward(d_out, saved_acts, weights, tables):
    w_attn, ln_par, w_up, w_down = weights[0], weights[2], weights[3], weights[5]
    cos_tab, sin_tab = tables
    x, h_one, query_rot, key_rot, values, probs_bf, context, x_mid, h_two, pre_act, act_bf = saved_acts
    num_seq, seq_len, model_dim = x.shape
    num_heads = model_dim // HEAD_DIM
    gb_down = jnp.sum(d_out, axis=(0, 1), dtype=jnp.float32)
    gw_down = jnp.einsum('blf,bld->fd', act_bf, d_out, preferred_element_type=jnp.float32)
    d_act = jnp.einsum('bld,fd->blf', d_out, w_down, preferred_element_type=jnp.float32)
    d_pre = d_act * gelu_slope(pre_act)
    gb_up = jnp.sum(d_pre, axis=(0, 1))
    d_pre_bf = d_pre.astype(jnp.bfloat16)
    gw_up = jnp.einsum('bld,blf->df', h_two, d_pre_bf, preferred_element_type=jnp.float32)
    d_h_two = jnp.einsum('blf,df->bld', d_pre_bf, w_up, preferred_element_type=jnp.float32)
    _, norm_pull_two = jax.vjp(norm_fwd, x_mid.astype(jnp.float32), ln_par[2].astype(jnp.float32), ln_par[3].astype(jnp.float32))
    d_mid_norm, g_gain_two, g_shift_two = norm_pull_two(d_h_two)
    d_mid = (d_out.astype(jnp.float32) + d_mid_norm).astype(jnp.bfloat16)
    gb_out = jnp.sum(d_mid, axis=(0, 1), dtype=jnp.float32)
    gw_out = jnp.einsum('bld,ble->de', context, d_mid, preferred_element_type=jnp.float32)
    d_context = jnp.einsum('ble,de->bld', d_mid, w_attn[3], preferred_element_type=jnp.float32)
    d_context = d_context.astype(jnp.bfloat16).reshape(num_seq, seq_len, num_heads, HEAD_DIM)
    d_probs = jnp.einsum('bqhd,bkhd->bhqk', d_context, values, preferred_element_type=jnp.float32)
    d_values = jnp.einsum('bhqk,bqhd->bkhd', probs_bf, d_context, preferred_element_type=jnp.float32)
    probs_f32 = probs_bf.astype(jnp.float32)
    d_scores = (probs_f32 * (d_probs - jnp.sum(d_probs * probs_f32, axis=-1, keepdims=True))).astype(jnp.bfloat16)
    d_query = jnp.einsum('bhqk,bkhd->bqhd', d_scores, key_rot, preferred_element_type=jnp.float32)
    d_key = jnp.einsum('bhqk,bqhd->bkhd', d_scores, query_rot, preferred_element_type=jnp.float32)
    d_proj = jnp.stack([
        (rotate_back(d_query, cos_tab, sin_tab) * (HEAD_DIM ** -0.5)).astype(jnp.bfloat16),
        rotate_back(d_key, cos_tab, sin_tab).astype(jnp.bfloat16),
        d_values.astype(jnp.bfloat16)]).reshape(3, num_seq, seq_len, model_dim)
    gb_qkv = jnp.sum(d_proj, axis=(1, 2), dtype=jnp.float32)
    gw_qkv = jnp.einsum('bld,kble->kde', h_one, d_proj, preferred_element_type=jnp.float32)
    d_h_one = jnp.einsum('kble,kde->bld', d_proj, w_attn[:3], preferred_element_type=jnp.float32)
    _, norm_pull_one = jax.vjp(norm_fwd, x.astype(jnp.float32), ln_par[0].astype(jnp.float32), ln_par[1].astype(jnp.float32))
    d_x_norm, g_gain_one, g_shift_one = norm_pull_one(d_h_one)
    d_x = (d_mid.astype(jnp.float32) + d_x_norm).astype(jnp.bfloat16)
    gb_attn = jnp.concatenate([gb_qkv, gb_out[None]], axis=0)
    g_ln = jnp.stack([g_gain_one, g_shift_one, g_gain_two, g_shift_two])
    return d_x, (gw_qkv, gw_out, gb_attn, g_ln, gw_up, gb_up, gw_down, gb_down)


def gather_layer(layer_shards, axis_name):
    w_attn, b_attn, ln_par, w_up, b_up, w_down, b_down = layer_shards
    return (lax.all_gather(w_attn, axis_name, axis=1, tiled=True),
            lax.all_gather(b_attn, axis_name, axis=1, tiled=True),
            lax.all_gather(ln_par, axis_name, axis=1, tiled=True),
            lax.all_gather(w_up, axis_name, axis=0, tiled=True),
            lax.all_gather(b_up, axis_name, axis=0, tiled=True),
            lax.all_gather(w_down, axis_name, axis=0, tiled=True),
            lax.all_gather(b_down, axis_name, axis=0, tiled=True))


def scatter_grads(layer_grads, axis_name):
    gw_qkv, gw_out, gb_attn, g_ln, gw_up, gb_up, gw_down, gb_down = layer_grads
    reduce_rows = functools.partial(lax.psum_scatter, axis_name=axis_name, tiled=True)
    attn_part = jnp.concatenate([reduce_rows(gw_qkv, scatter_dimension=1), reduce_rows(gw_out, scatter_dimension=0)[None]], axis=0)
    return (attn_part,
            reduce_rows(gb_attn, scatter_dimension=1),
            reduce_rows(g_ln, scatter_dimension=1),
            reduce_rows(gw_up, scatter_dimension=0),
            reduce_rows(gb_up, scatter_dimension=0),
            reduce_rows(gw_down, scatter_dimension=0),
            reduce_rows(gb_down, scatter_dimension=0))


def solution(mesh):
    axis_name = mesh.axis_names[0]
    batch_spec = P(axis_name)
    weight_specs = (P(None, None, axis_name, None), P(None, None, axis_name), P(None, None, axis_name),
                    P(None, axis_name, None), P(None, axis_name), P(None, axis_name, None), P(None, axis_name))

    def device_step(x, lengths, d_y, w_attn, b_attn, ln_par, w_up, b_up, w_down, b_down):
        shards = (w_attn, b_attn, ln_par, w_up, b_up, w_down, b_down)
        num_layers = w_attn.shape[0]
        tables = rotary_tables(x.shape[1])
        hidden = x
        saved_list = []
        for layer_idx in range(num_layers):
            full_wts = gather_layer(tuple(shard[layer_idx] for shard in shards), axis_name)
            hidden, saved_acts = layer_forward(hidden, full_wts, lengths, tables)
            saved_list.append(saved_acts)
        grad_x = d_y
        grads_list = [None] * num_layers
        for layer_idx in reversed(range(num_layers)):
            layer_shards, grad_x = lax.optimization_barrier((tuple(shard[layer_idx] for shard in shards), grad_x))
            full_wts = gather_layer(layer_shards, axis_name)
            grad_x, layer_grads = layer_backward(grad_x, saved_list[layer_idx], full_wts, tables)
            grads_list[layer_idx] = scatter_grads(layer_grads, axis_name)
        stacked = tuple(jnp.stack([grads_list[layer_pos][field_pos] for layer_pos in range(num_layers)]) for field_pos in range(7))
        return (grad_x,) + stacked

    return jax.shard_map(device_step, mesh=mesh,
                         in_specs=(batch_spec, batch_spec, batch_spec) + weight_specs,
                         out_specs=(batch_spec,) + weight_specs,
                         check_vma=False)
```

profile of v0, /device:TPU:1, one launch (start us, length us, event | category | flops | bytes accessed | tf_op | source)
XLA Modules:
  0.0 4161.3 jit_solution(4317722402157341286)
XLA Ops:
  17.0 79.1 %all-gather.2 = bf16[1,4,512]{1,0,2:T(2,128)(2,1)S(1)} all-gather(bf16[1,4,2]{1,0,2:T(2,128)(2,1)S(1)} %copy.346), channel_id=4, replica_groups=mesh['fsdp'=256] {'fsdp'}, dimensions={2}, use_global_device_ids=true | all-gather | bytes 4112 | tf_op jit(solution)/shard_map/all_gather | solution.py:122
  100.3 71.8 %all-gather.9 = bf16[1,4,512]{1,0,2:T(2,128)(2,1)S(1)} all-gather(bf16[1,4,2]{1,0,2:T(2,128)(2,1)S(1)} %copy.349), channel_id=11, replica_groups=mesh['fsdp'=256] {'fsdp'}, dimensions={2}, use_global_device_ids=true | all-gather | bytes 4112 | tf_op jit(solution)/shard_map/all_gather | solution.py:122
  179.1 74.9 %all-reduce.19 = (bf16[2048]{0:T(1024)(128)(2,1)S(1)}, bf16[512]{0:T(512)(128)(2,1)S(1)}, bf16[2048]{0:T(1024)(128)(2,1)S(1)}) all-reduce(bf16[2048]{0:T(1024)(128)(2,1)S(1)} %dynamic-update-slice, bf16[512]{0:T(512)(128)(2,1)S(1)} %dynamic-update-slice.1, bf16[2048]{0:T(1024)(128)(2,1)S(1)} %dynamic-update-slice.2), channel_id=6, replica_groups=mesh['fsdp'=256] {'fsdp'}, use_global_device_ids=true, to_apply=%add | all-reduce | flops 4608 | bytes 18432
  254.4 72.4 %all-gather.13 = bf16[256,2,4]{2,1,0:T(2,128)(2,1)S(1)} all-gather(bf16[1,2,4]{2,1,0:T(2,128)(2,1)S(1)} %bitcast.352), channel_id=1, replica_groups=mesh['fsdp'=256] {'fsdp'}, dimensions={0}, use_global_device_ids=true | all-gather | bytes 4112 | tf_op jit(solution)/shard_map/all_gather | solution.py:123
  327.7 71.9 %all-gather = bf16[1,4,512]{1,0,2:T(2,128)(2,1)S(1)} all-gather(bf16[1,4,2]{1,0,2:T(2,128)(2,1)S(1)} %copy.338), channel_id=2, replica_groups=mesh['fsdp'=256] {'fsdp'}, dimensions={2}, use_global_device_ids=true | all-gather | bytes 4112 | tf_op jit(solution)/shard_map/all_gather | solution.py:123
  399.6 7.1 fusion.159
  406.8 71.8 %all-gather.7 = bf16[1,4,512]{1,0,2:T(2,128)(2,1)S(1)} all-gather(bf16[1,4,2]{1,0,2:T(2,128)(2,1)S(1)} %copy.340), channel_id=9, replica_groups=mesh['fsdp'=256] {'fsdp'}, dimensions={2}, use_global_device_ids=true | all-gather | bytes 4112 | tf_op jit(solution)/shard_map/all_gather | solution.py:123
  478.6 7.1 fusion.154
  499.9 4.1 copy.348
  507.9 10.9 fusion.229
  518.9 6.9 divide_convert_fusion.1
  530.4 8.1 fusion.123
  541.7 20.7 fusion.14
  562.4 5.4 convert_reduce_fusion.2
  580.4 11.0 fusion.230
  591.4 7.1 divide_convert_fusion
  602.9 4.1 reshape.533
  607.0 69.6 %all-gather.44.cloned.1.call-done = bf16[1,512,2048]{2,0,1:T(2,128)(2,1)} async-done(((bf16[1,2,2048]{2,0,1:T(2,128)(2,1)}), bf16[1,512,2048]{2,0,1:T(2,128)(2,1)}) %all-gather.44.cloned.1.call-update) | async-done | bytes 2097168 | tf_op jit(solution)/shard_map/all_gather | solution.py:124
  676.6 12.6 fusion.124
  689.3 92.5 %all-gather.28.cloned.1.call-done = bf16[2048,512]{1,0:T(8,128)(2,1)} async-done(((bf16[8,512]{1,0:T(8,128)(2,1)}), bf16[2048,512]{1,0:T(8,128)(2,1)}) %all-gather.28.cloned.1.call-update) | async-done | bytes 2097168 | tf_op jit(solution)/shard_map/all_gather | solution.py:126
  781.7 8.5 fusion.235
  790.2 4.3 fusion.231
  802.6 86.0 %all-gather.30.cloned.1.call-done = bf16[4,512,512]{2,0,1:T(4,128)(2,1)} async-done(((bf16[4,2,512]{2,0,1:T(4,128)(2,1)}), bf16[4,512,512]{2,0,1:T(4,128)(2,1)}) %all-gather.30.cloned.1.call-update) | async-done | bytes 2097168 | tf_op jit(solution)/shard_map/all_gather | solution.py:121
  893.4 7.2 convolution_convert_fusion.1
  900.6 7.1 fusion.2
  907.7 11.8 fusion.3
  938.8 5.7 fusion.232
  951.5 24.1 fusion.46
  977.1 4.9 convolution_bitcast_fusion.3
  982.0 5.5 copy.269
  987.5 74.2 %all-gather.15 = bf16[256,2,4]{2,1,0:T(2,128)(2,1)S(1)} all-gather(bf16[1,2,4]{2,1,0:T(2,128)(2,1)S(1)} %bitcast.351), channel_id=1, replica_groups=mesh['fsdp'=256] {'fsdp'}, dimensions={0}, use_global_device_ids=true | all-gather | bytes 4112 | tf_op jit(solution)/shard_map/all_gather | solution.py:123
  1063.6 6.6 convolution_bitcast_fusion
  1070.2 6.7 convolution_bitcast_fusion.1
  1081.1 79.3 %all-gather.32.cloned.1.call-done = bf16[2048,512]{1,0:T(8,128)(2,1)} async-done(((bf16[8,512]{1,0:T(8,128)(2,1)}), bf16[2048,512]{1,0:T(8,128)(2,1)}) %all-gather.32.cloned.1.call-update) | async-done | bytes 2097168 | tf_op jit(solution)/shard_map/all_gather | solution.py:126
  1160.4 8.6 fusion.236
  1169.0 4.2 fusion.233
  1175.7 91.6 %all-gather.34.cloned.1.call-done = bf16[4,512,512]{2,0,1:T(4,128)(2,1)} async-done(((bf16[4,2,512]{2,0,1:T(4,128)(2,1)}), bf16[4,512,512]{2,0,1:T(4,128)(2,1)}) %all-gather.34.cloned.1.call-update) | async-done | bytes 2097168 | tf_op jit(solution)/shard_map/all_gather | solution.py:121
  1274.4 6.4 convolution_convert_fusion
  1282.3 6.4 fusion.4
  1288.8 8.0 fusion.5
  1311.8 4.9 convolution_bitcast_fusion.4
  1316.7 5.4 copy.263
  1325.2 6.7 convolution_bitcast_fusion.2
  1338.7 5.1 fusion.234
  1347.1 81.2 %all-reduce.17 = (f32[4,512]{0,1:T(8,128)}, f32[4,512]{0,1:T(8,128)}, f32[4,512]{1,0:T(4,128)S(1)}, f32[4,512]{1,0:T(4,128)S(1)}, f32[2048]{0:T(1024)S(1)}, /*in...) all-reduce(f32[4,512]{0,1:T(8,128)S(1)} %copy.274, ...), channel_id=19, replica_groups=mesh['fsdp'=256] {'fsdp'}, use_global_device_ids=true, to_apply=%region_31.32.clone | all-reduce | flops 13312 | bytes 106496
  1437.0 1114.0 %reduce-scatter.9.cloned.1.call-done = f32[8,512]{1,0:T(8,128)} async-done(((f32[2048,512]{1,0:T(8,128)}), f32[8,512]{1,0:T(8,128)}) %reduce-scatter.9.cloned.1.call-update) | async-done | bytes 16400 | tf_op jit(solution)/shard_map/reduce_scatter | solution.py:139
  2551.0 1288.3 %reduce-scatter.7.cloned.1.call-done = f32[8,512]{1,0:T(8,128)} async-done(((f32[2048,512]{1,0:T(8,128)}), f32[8,512]{1,0:T(8,128)}) %reduce-scatter.7.cloned.1.call-update) | async-done | bytes 16400 | tf_op jit(solution)/shard_map/reduce_scatter | solution.py:139
  3840.7 309.2 %all-reduce.22.cloned.1.call-done = (f32[512,512]{0,1:T(8,128)}, f32[3,512,512]{2,0,1:T(4,128)}, f32[512,512]{0,1:T(8,128)}, f32[3,512,512]{2,0,1:T(4,128)}, f32[512,2048]{1,0:T(8,128)}, /*index=5*/f32[512,2048]{1,0:T(8,128)}) async-done(((f32[512,512]{0,1:T(8,128)}, f32[3,512,512]{2,0,1:T(4,128)}, f32[512,512]{0,1:T(8,128)}, f32[3,512,512]{2,0,1:T(4,128)}, f32[512,2048]{1,0:T(8,128)}, ...) | async-done | bytes 16777232
  (399 shorter events, 164.3 us)
Async XLA Ops:
  7.2 478.6 %copy-start.55 = (bf16[2,512,512]{2,1,0:T(8,128)(2,1)S(1)}, bf16[2,512,512]{2,1,0:T(8,128)(2,1)}, u32[]{:S(2)}) copy-start(bf16[2,512,512]{2,1,0:T(8,128)(2,1)} %param.10) | copy-start | bytes 3145732
  7.2 481.4 %all-gather.36.cloned.1.call-start = ((), (), s32[]{:S(2)}) async-start(), calls=%async_computation.8 | async-start | bytes 2105344 | tf_op jit(solution)/shard_map/all_gather | solution.py:121
  8.7 491.2 %all-gather.42.cloned.1.call-start = ((), (), s32[]{:S(2)}) async-start(), calls=%async_computation.11 | async-start | bytes 2105344 | tf_op jit(solution)/shard_map/all_gather | solution.py:121
  9.4 521.0 %all-gather.38.cloned.1.call-start = ((), (), s32[]{:S(2)}) async-start(), calls=%async_computation.9 | async-start | bytes 4210688 | tf_op jit(solution)/shard_map/all_gather | solution.py:124
  11.4 551.0 %all-gather.40.cloned.1.call-start = ((), (), s32[]{:S(2)}) async-start(), calls=%async_computation.10 | async-start | bytes 2105344 | tf_op jit(solution)/shard_map/all_gather | solution.py:126
  12.8 590.1 %all-gather.46.cloned.1.call-start = ((), (), s32[]{:S(2)}) async-start(), calls=%async_computation.13 | async-start | bytes 2105344 | tf_op jit(solution)/shard_map/all_gather | solution.py:124
  14.1 662.5 %all-gather.44.cloned.1.call-start = ((), (), s32[]{:S(2)}) async-start(), calls=%async_computation.12 | async-start | bytes 4210688 | tf_op jit(solution)/shard_map/all_gather | solution.py:124
  14.8 766.9 %all-gather.28.cloned.1.call-start = ((), (), s32[]{:S(2)}) async-start(), calls=%async_computation.2 | async-start | bytes 2105344 | tf_op jit(solution)/shard_map/all_gather | solution.py:126
  15.5 873.0 %all-gather.30.cloned.1.call-start = ((), (), s32[]{:S(2)}) async-start(), calls=%async_computation.3 | async-start | bytes 2105344 | tf_op jit(solution)/shard_map/all_gather | solution.py:121
  16.3 1060.7 %all-gather.48.cloned.1.call-start = ((), (), s32[]{:S(2)}) async-start(), calls=%async_computation.14 | async-start | bytes 2105344 | tf_op jit(solution)/shard_map/all_gather | solution.py:124
  254.0 284.5 %copy-start.74 = (f32[2048]{0:T(1024)}, f32[2048]{0:T(1024)S(1)}, u32[]{:S(2)}) copy-start(f32[2048]{0:T(1024)S(1)} %convert_element_type.463) | copy-start | bytes 24580
  254.3 673.1 %copy-start.50 = (f32[512,32]{0,1:T(8,128)}, f32[512,32]{0,1:T(8,128)S(1)}, u32[]{:S(2)}) copy-start(f32[512,32]{0,1:T(8,128)S(1)} %get-tuple-element.156) | copy-start | bytes 196612
  254.3 673.0 %copy-start.52 = (f32[512,32]{0,1:T(8,128)}, f32[512,32]{0,1:T(8,128)S(1)}, u32[]{:S(2)}) copy-start(f32[512,32]{0,1:T(8,128)S(1)} %get-tuple-element.157) | copy-start | bytes 196612
  399.6 87.6 %copy-start.56 = (bf16[2,512,512]{2,1,0:T(8,128)(2,1)S(1)}, bf16[2,512,512]{2,1,0:T(8,128)(2,1)}, u32[]{:S(2)}) copy-start(bf16[2,512,512]{2,1,0:T(8,128)(2,1)} %param.12) | copy-start | bytes 3145732
  406.8 84.7 %copy-start.89 = (f32[512]{0:T(512)}, f32[512]{0:T(512)S(1)}, u32[]{:S(2)}) copy-start(f32[512]{0:T(512)S(1)} %get-tuple-element.77) | copy-start | bytes 6148
  406.8 84.7 %copy-start.91 = (f32[512]{0:T(512)}, f32[512]{0:T(512)S(1)}, u32[]{:S(2)}) copy-start(f32[512]{0:T(512)S(1)} %get-tuple-element.78) | copy-start | bytes 6148
  406.8 123.6 %copy-start.85 = (f32[512]{0:T(512)}, f32[512]{0:T(512)S(1)}, u32[]{:S(2)}) copy-start(f32[512]{0:T(512)S(1)} %get-tuple-element.76) | copy-start | bytes 6148
  406.8 123.6 %copy-start.87 = (f32[512]{0:T(512)}, f32[512]{0:T(512)S(1)}, u32[]{:S(2)}) copy-start(f32[512]{0:T(512)S(1)} %get-tuple-element.79) | copy-start | bytes 6148
  485.7 82.4 %copy-start.97 = (f32[512]{0:T(512)}, f32[512]{0:T(512)S(1)}, u32[]{:S(2)}) copy-start(f32[512]{0:T(512)S(1)} %get-tuple-element.73) | copy-start | bytes 6148
  485.7 82.4 %copy-start.99 = (f32[512]{0:T(512)}, f32[512]{0:T(512)S(1)}, u32[]{:S(2)}) copy-start(f32[512]{0:T(512)S(1)} %get-tuple-element.74) | copy-start | bytes 6148
  485.7 190.9 %copy-start.93 = (f32[512]{0:T(512)}, f32[512]{0:T(512)S(1)}, u32[]{:S(2)}) copy-start(f32[512]{0:T(512)S(1)} %get-tuple-element.72) | copy-start | bytes 6148
  485.8 190.9 %copy-start.95 = (f32[512]{0:T(512)}, f32[512]{0:T(512)S(1)}, u32[]{:S(2)}) copy-start(f32[512]{0:T(512)S(1)} %get-tuple-element.75) | copy-start | bytes 6148
  486.7 42.3 %copy-start.2 = (bf16[2,512,512]{1,2,0:T(8,128)(2,1)}, bf16[2,512,512]{1,2,0:T(8,128)(2,1)S(1)}, u32[]{:S(2)}) copy-start(bf16[2,512,512]{1,2,0:T(8,128)(2,1)S(1)} %copy.218) | copy-start | bytes 3145732
  493.6 32.2 copy-start.10
  507.9 11.0 copy-start.37
  507.9 11.0 copy-start.39
  530.0 32.4 copy-start.4
  570.3 28.2 copy-start.11
  580.4 11.0 copy-start.42
  580.4 11.0 copy-start.44
  602.5 86.7 %copy-start.7 = (bf16[2,512,512]{1,2,0:T(8,128)(2,1)}, bf16[2,512,512]{1,2,0:T(8,128)(2,1)S(1)}, u32[]{:S(2)}) copy-start(bf16[2,512,512]{1,2,0:T(8,128)(2,1)S(1)} %get-tuple-element.168) | copy-start | bytes 3145732
  676.6 105.1 %copy-start.57 = (bf16[2,512,512]{2,1,0:T(8,128)(2,1)S(1)}, bf16[2,512,512]{2,1,0:T(8,128)(2,1)}, u32[]{:S(2)}) copy-start(bf16[2,512,512]{2,1,0:T(8,128)(2,1)} %param.12) | copy-start | bytes 3145732
  888.6 12.0 slice-start
  907.7 11.9 copy-start.46
  907.7 11.9 copy-start.47
  933.5 11.0 copy-start.19
  950.1 210.3 %all-gather.32.cloned.1.call-start = ((), (), s32[]{:S(2)}) async-start(), calls=%async_computation.4 | async-start | bytes 2105344 | tf_op jit(solution)/shard_map/all_gather | solution.py:126
  950.7 316.6 %all-gather.34.cloned.1.call-start = ((), (), s32[]{:S(2)}) async-start(), calls=%async_computation.5 | async-start | bytes 2105344 | tf_op jit(solution)/shard_map/all_gather | solution.py:121
  951.4 1599.6 %reduce-scatter.9.cloned.1.call-start = ((), (), s32[]{:S(2)}) async-start(), calls=%async_computation.7 | async-start | bytes 4210688 | tf_op jit(solution)/shard_map/reduce_scatter | solution.py:139
  975.6 2863.8 %reduce-scatter.7.cloned.1.call-start = ((), (), s32[]{:S(2)}) async-start(), calls=%async_computation.6 | async-start | bytes 4210688 | tf_op jit(solution)/shard_map/reduce_scatter | solution.py:139
  982.0 79.8 %copy-start.29 = (bf16[2,512,512]{1,2,0:T(8,128)(2,1)S(1)}, bf16[2,512,512]{1,2,0:T(8,128)(2,1)}, u32[]{:S(2)}) copy-start(bf16[2,512,512]{1,2,0:T(8,128)(2,1)} %get-tuple-element.100) | copy-start | bytes 3145732
  982.0 79.8 %copy-start.36 = (bf16[2,8,64,512]{3,2,1,0:T(8,128)(2,1)S(1)}, bf16[2,8,64,512]{3,2,1,0:T(8,128)(2,1)}, u32[]{:S(2)}) copy-start(bf16[2,8,64,512]{3,2,1,0:T(8,128)(2,1)} %copy-done.35) | copy-start | bytes 3145732
  987.5 76.1 %copy-start.30 = (bf16[2,512,512]{1,2,0:T(8,128)(2,1)S(1)}, bf16[2,512,512]{1,2,0:T(8,128)(2,1)}, u32[]{:S(2)}) copy-start(bf16[2,512,512]{1,2,0:T(8,128)(2,1)} %fusion.88) | copy-start | bytes 3145732
  1076.9 83.5 %copy-start.75 = (f32[2048]{0:T(1024)S(1)}, f32[2048]{0:T(1024)}, u32[]{:S(2)}) copy-start(f32[2048]{0:T(1024)} %copy-done.74) | copy-start | bytes 24580
  1076.9 3073.0 %all-reduce.22.cloned.1.call-start = ((), (), s32[]{:S(2)}) async-start(), calls=%async_computation.15 | async-start | bytes 37748736
  1175.3 94.8 %copy-start.71 = (f32[2,512]{1,0:T(2,128)S(1)}, f32[2,512]{1,0:T(2,128)}, u32[]{:S(2)}) copy-start(f32[2,512]{1,0:T(2,128)} %copy-done.70) | copy-start | bytes 12292
  1175.3 94.9 %copy-start.73 = (f32[2,512]{1,0:T(2,128)S(1)}, f32[2,512]{1,0:T(2,128)}, u32[]{:S(2)}) copy-start(f32[2,512]{1,0:T(2,128)} %copy-done.72) | copy-start | bytes 12292
  1306.8 9.9 copy-start.24
  (75 other events, 308.3 us)
Sparse Core Ops, SparseCore 0:
  11.7 108.2 all-gather.35
  123.7 103.2 all-gather.41
  231.1 114.8 all-gather.37
  349.6 101.3 all-gather.39
  454.6 103.1 all-gather.45
  561.8 114.8 all-gather.43
  680.3 101.3 all-gather.27
  785.5 103.0 all-gather.29
  950.2 103.1 all-gather.47
  1057.0 103.4 all-gather.31
  1164.2 103.0 all-gather.33
  1269.6 1281.3 reduce-scatter.8
  2553.5 1285.7 reduce-scatter.6
  3845.7 304.2 all-reduce.21
where the time goes:
time: 4170 us; the launch traced here: 4160 us
  waiting for transfers between devices  3130 us (75%)
  blocking collectives  597 us (14%)
  matrix products  192 us (5%)
  other arithmetic  132 us (3%)
  local copies, waits for them, and re-layouts  90.1 us (2%)
    reduce_scatter x2, waiting for transfers between devices, scatter_grads(): reduce_rows(gw_down, scatter_dimension=0)  2400 us
    unnamed x15, waiting for transfers between devices  312 us
    all_gather x4, blocking collectives, gather_layer(): lax.all_gather(ln_par, axis_name, axis=1, tiled=True)  290 us
    all_gather x4, waiting for transfers between devices, gather_layer(): lax.all_gather(w_attn, axis_name, axis=1, tiled=True)  178 us
    all_gather x3, waiting for transfers between devices, gather_layer(): lax.all_gather(w_down, axis_name, axis=0, tiled=True)  172 us
    unnamed x2, blocking collectives  156 us
    all_gather x2, blocking collectives, gather_layer(): lax.all_gather(b_attn, axis_name, axis=1, tiled=True)  151 us
  transfers between devices with their start and end apart: 14, of which 8 were waited for; matrix products, arithmetic and copies ran while one was open for 8% of the time, Pallas kernels for 0%

commit v1 on v0

v1 whole, which is shorter than its diff:
```python
import functools
import math
import jax
import jax.numpy as jnp
import numpy as np
from jax import lax
from jax.experimental import pallas as pl
from jax.experimental.pallas import tpu as pltpu
from jax.sharding import Mesh, PartitionSpec as P

F32, BF = jnp.float32, jnp.bfloat16
AXES = ('z', 'y', 'x', 'c')
SIZES = dict(z=8, y=4, x=4, c=2, k=2, h=2, l=2, r=2)
TILE = (8, 128)
TILED = dict(attn='kzyht', up='zyht', down='zyxct')
FINE = dict(attn='kzyhtlcr', up='zyhtlcr', down='zyxct')
LANE_TILES = dict(attn=4, up=8, down=2)
HALVED = dict(attn='k', up='t', down='t')
ALL = slice(None)


class Place:
    def __init__(self, send, recv):
        self.me = {a: lax.axis_index(a) for a in AXES}
        self.send, self.recv, self.used = send, recv, 0

    def shifted(self, axis, s):
        at = dict(self.me)
        if axis:
            at[axis] = lax.rem(at[axis] + s, SIZES[axis])
        return at

    def peers(self, axis):
        n = SIZES[axis]
        return sorted(range(1, n), key=lambda s: min(s, n - s))

    def greet(self, axes):
        bar = pltpu.get_barrier_semaphore()
        everyone = [(a, s) for a in axes for s in self.peers(a)]
        for a, s in everyone:
            pl.semaphore_signal(bar, inc=1, device_id=self.device(a, s), device_id_type=pl.DeviceIdType.MESH)
        pl.semaphore_wait(bar, len(everyone))

    def device(self, axis, s):
        at = self.shifted(axis, s)
        return tuple(at[a] for a in AXES)

    def copy(self, axis, s, refs):
        i, self.used = self.used, self.used + 1

        def build():
            src, dst = refs()
            return pltpu.make_async_remote_copy(src, dst, self.send.at[i], self.recv.at[i], device_id=self.device(axis, s), device_id_type=pl.DeviceIdType.MESH)
        build().start()
        return lambda: build().wait()

    def local(self, refs):
        i, self.used = self.used, self.used + 1

        def build():
            return pltpu.make_async_copy(*refs(), self.send.at[i])
        build().start()
        return lambda: build().wait()


def spot(at):
    return dict(at, h=lax.div(at['x'], SIZES['l']), l=lax.rem(at['x'], SIZES['l']))


def half(kind, core):
    n = SIZES['k'] if HALVED[kind] == 'k' else LANE_TILES[kind]
    return {HALVED[kind]: pl.ds(core * n, n)}


def view(ref, names, pick):
    return ref.at[tuple(pick.get(n, ALL) for n in names)]


def only(at, names):
    return {n: v for n, v in spot(at).items() if n in names}


OWNER = dict(x='xhl', y='y', z='z')


def gather_unit(place, kind, full, shard, order):
    names = FINE[kind]
    mine = [n for n in names if n not in 'tkr']

    def block(core, fixed, at):
        return view(full, names, dict(half(kind, core(at)), **only(at, fixed)))
    own, other = (lambda at: at['c']), (lambda at: 1 - at['c'])
    rows = [n for n in names if n in 'tk'] + ['r'] * 2

    def piece(core):
        return view(shard, rows, half(kind, core(place.me)))
    waits = [place.local(lambda: (piece(own), block(own, mine, place.me))),
             place.copy('c', 1, lambda: (piece(other), block(other, mine, place.me)))]
    yield
    for w in waits:
        w()
    left = list(order)
    while left:
        fixed = ''.join(OWNER[a] for a in left)
        axis = left.pop(0)
        same = lambda fixed=fixed: (block(own, fixed, place.me),) * 2
        waits = [(s, place.copy(axis, s, same)) for s in place.peers(axis)]
        if left:
            yield
            for _, w in waits:
                w()
    last = [place.copy('c', 1, same)]
    for s, w in waits:
        yield
        w()
        came = lambda s=s: (block(own, fixed, place.shifted(axis, SIZES[axis] - s)),) * 2
        last.append(place.copy('c', 1, came))
    yield
    for w in last:
        w()


def unravel(i, shape):
    idx = []
    for n in reversed(shape):
        idx.append(lax.rem(i, n))
        i = lax.div(i, n)
    return tuple(reversed(idx))


def each(shape, body):
    def step(i, carry):
        body(unravel(i, shape))
        return carry
    lax.fori_loop(0, math.prod(shape), step, 0)


def sizes(kind, names):
    return tuple(LANE_TILES[kind] if n == 't' else SIZES[n] for n in names) + TILE


def phases(kind, order):
    names = TILED[kind]
    for a in order:
        d = a if a in names else 'h'
        yield a, d, names, names.replace(d, '')
        names = names.replace(d, '')


def scatter_buffers(kind, order):
    shapes = [sizes(kind, TILED[kind])] * 2
    for a, _, _, after in phases(kind, order):
        shapes += [(SIZES[a] - 1,) + sizes(kind, after), sizes(kind, after)]
    shapes.append(sizes(kind, after.replace('c', '')))
    return [pltpu.VMEM(s, F32) for s in shapes]


def scatter_unit(place, kind, order, grad, out, bufs):
    me = place.me
    own, got, *bufs = bufs
    names = TILED[kind]
    waits = [place.copy('c', 1, lambda: (view(grad, names, half(kind, 1 - me['c'])), got)),
             place.local(lambda: (view(grad, names, half(kind, me['c'])), own))]
    yield
    for w in waits:
        w()

    def add(idx):
        own[idx] = own[idx] + got[idx]
    each(own.shape[:-4], add)
    src = own
    for a, d, before, after in phases(kind, order):
        slots, total, *bufs = bufs
        at = before.index(d)
        waits = [place.copy(a, s, lambda s=s, src=src: (view(src, before, only(place.shifted(a, s), d)), slots.at[s - 1])) for s in place.peers(a)]
        yield
        for w in waits:
            w()
        lead = total.shape[:-4]

        def reduce(idx):
            loop = dict(zip(after, idx))
            v = src[tuple(spot(me)[n] if n == d else loop.get(n, ALL) for n in before)]
            for s in range(SIZES[a] - 1):
                v = v + slots[(s,) + idx]
            total[idx if idx else ...] = v
        each(lead, reduce) if lead else reduce(())
        src = total
    other, = bufs
    mine = lambda core: view(src, after, dict(c=core)) if 'c' in after else src
    wait = place.copy('c', 1, lambda: (mine(1 - me['c']), other))
    yield
    wait()
    for core, ref in ((me['c'], mine(me['c'])), (1 - me['c'], other)):
        rows = ALL if kind == 'down' else pl.ds((spot(me)['l'] * 2 + me['c']) * 2, 2)
        out[half(kind, core)[HALVED[kind]]] = ref[..., rows, :]


def total_unit(place, value, out, slots):
    me = place.me
    keep, *slots = slots
    wait = place.copy('c', 1, lambda: (value.at[1 - me['c']], slots[0].at[0]))
    yield
    wait()
    keep[...] = value[me['c']] + slots[0][0]
    for axis, slot in zip('xyz', slots[1:]):
        slot[SIZES[axis] - 1] = keep[...]
        waits = [place.copy(axis, s, lambda s=s: (slot.at[SIZES[axis] - 1], slot.at[s - 1])) for s in place.peers(axis)]
        yield
        for w in waits:
            w()
        v = slot[0]
        for s in range(1, SIZES[axis]):
            v = v + slot[s]
        keep[...] = v
    out[me['c']] = keep[...]
    wait = place.copy('c', 1, lambda: (keep, out.at[me['c']]))
    yield
    wait()


def total_buffers(n):
    return [pltpu.VMEM((n, 512), F32)] + [pltpu.VMEM((SIZES[a], n, 512), F32) for a in 'cxyz']


def run(units):
    units = list(units)
    while units:
        units = [u for u in units if next(u, units) is not units]


def semaphores(n):
    return [pltpu.SemaphoreType.DMA((n,))] * 2


def any_space(n):
    return [pl.BlockSpec(memory_space=pl.ANY)] * n


def in_vmem(n):
    return [pl.BlockSpec(memory_space=pltpu.VMEM)] * n


SD = jax.ShapeDtypeStruct
GATHER_ORDER = dict(attn='xzy', up='xzy', down='yzx')
SCATTER_ORDER = dict(attn='yzx', up='yzx', down='xzy')
KINDS = tuple(TILED)


def gather_kernel(*refs):
    n = 2 * len(KINDS)
    shards, small, full, total, slots, sems = refs[:n], refs[n], refs[n + 1:2 * n + 1], refs[2 * n + 1], refs[2 * n + 2:-2], refs[-2:]
    place = Place(*sems)
    place.greet(AXES)
    run([total_unit(place, small, total, slots)] + [gather_unit(place, kind, f, s, GATHER_ORDER[kind]) for kind, f, s in zip(KINDS * 2, full, shards)])


def fine_shape(kind):
    n = 2 * LANE_TILES[kind] if HALVED[kind] == 't' else LANE_TILES[kind]
    dims = dict(SIZES, t=n, k=4)
    tail = (128,) if 'r' in FINE[kind] else TILE
    return tuple(dims[d] for d in FINE[kind]) + tail


def gather(attn, up, down, small):
    shards = []
    for l in range(2):
        shards += [attn[l].reshape(4, 2, 4, 128).swapaxes(1, 2), up[l].reshape(2, 16, 128).swapaxes(0, 1), down[l].reshape(8, 4, 128).swapaxes(0, 1)]
    *full, total = pl.pallas_call(
        gather_kernel, name='gather',
        in_specs=in_vmem(len(shards) + 1), out_specs=any_space(len(shards)) + in_vmem(1),
        out_shape=[SD(fine_shape(k), BF) for k in KINDS * 2] + [SD(small.shape, F32)],
        scratch_shapes=total_buffers(16) + semaphores(180),
        compiler_params=pltpu.CompilerParams(collective_id=1, has_side_effects=True),
    )(*shards, small)
    whole = []
    for l in range(2):
        a, u, d = full[3 * l:3 * l + 3]
        whole.append((tiles_to_rows(a.reshape(4, 64, 4, *TILE)), tiles_to_rows(u.reshape(64, 16, *TILE)), tiles_to_rows(d.reshape(256, 4, *TILE))))
    return whole, total


def tiles_to_rows(t):
    *lead, r, n, s, w = t.shape
    return t.swapaxes(-3, -2).reshape(*lead, r * s, n * w)


def rows_to_tiles(g):
    *lead, r, w = g.shape
    return g.reshape(*lead, r // TILE[0], TILE[0], w // TILE[1], TILE[1]).swapaxes(-3, -2)


def tiled_shape(kind):
    return fine_shape(kind)[:-3 if kind != 'down' else -2][:len(TILED[kind])] + TILE


def scatter_kernel(*refs):
    n = 2 * len(KINDS)
    grads, small, outs, total = refs[:n], refs[n:n + 4], refs[n + 4:2 * n + 4], refs[2 * n + 4]
    scratch = list(refs[2 * n + 5:-2])
    value, *scratch = scratch
    for i in range(4):
        value[i // 2, pl.ds(8 * (i % 2), 8)] = small[i][...]
    place = Place(*refs[-2:])
    place.greet(AXES)
    count = len(total_buffers(16))
    units = [total_unit(place, value, total, scratch[:count])]
    scratch = scratch[count:]
    for kind, g, o in zip(KINDS * 2, grads, outs):
        count = len(scatter_buffers(kind, SCATTER_ORDER[kind]))
        units.append(scatter_unit(place, kind, SCATTER_ORDER[kind], g, o, scratch[:count]))
        scratch = scratch[count:]
    run(units)


def scatter(grads, small):
    tiled = [rows_to_tiles(g).reshape(tiled_shape(k)) for k, g in zip(KINDS * 2, grads)]
    out = dict(attn=(4, 4, 2, 128), up=(16, 2, 128), down=(4, 8, 128))
    bufs = [b for k in KINDS * 2 for b in scatter_buffers(k, SCATTER_ORDER[k])]
    *res, total = pl.pallas_call(
        scatter_kernel, name='scatter',
        in_specs=any_space(len(tiled)) + in_vmem(4), out_specs=in_vmem(len(tiled) + 1),
        out_shape=[SD(out[k], F32) for k in KINDS * 2] + [SD((2, 16, 512), F32)],
        scratch_shapes=[pltpu.VMEM((2, 16, 512), F32)] + total_buffers(16) + bufs + semaphores(180),
        compiler_params=pltpu.CompilerParams(collective_id=2, has_side_effects=True, vmem_limit_bytes=63 << 20),
    )(*tiled, *small)
    stack = lambda i: jnp.stack([tiles_to_rows(res[j][..., None, :, :, :]) for j in (i, i + 3)])
    return stack(0), stack(1), stack(2), total


HEAD_DIM = 64
EPS = 1e-5
THETA = 10000.0
NEG_BIG = -1e30
SEQ, DIM, FFN, TOKENS, CHUNK, BLOCK, WIDE = 512, 512, 2048, 1024, 512, 256, 128


def blocks(n):
    return range(0, n, BLOCK)


def dot(a, b, ca=1, cb=0):
    return lax.dot_general(a, b, (((ca,), (cb,)), ((), ())), preferred_element_type=F32)


def rotary_tables():
    half = HEAD_DIM // 2
    inv = (1.0 / (THETA ** (np.arange(half, dtype=np.float32) * np.float32(2.0 / HEAD_DIM)))).astype(np.float32)
    ang = np.arange(SEQ, dtype=np.float32)[:, None] * inv[None, :]
    cos, sin = np.cos(ang), np.sin(ang)
    return np.tile(cos, (1, 4)).astype(np.float32), np.concatenate([-sin, sin, -sin, sin], axis=1).astype(np.float32)


def swap_halves(t):
    lane = lax.broadcasted_iota(jnp.int32, t.shape, 1)
    return jnp.where(lax.rem(lane, HEAD_DIM) < HEAD_DIM // 2, pltpu.roll(t, 128 - HEAD_DIM // 2, 1), pltpu.roll(t, HEAD_DIM // 2, 1))


def normed(t):
    mean = jnp.mean(t, axis=-1, keepdims=True)
    cent = t - mean
    var = jnp.mean(cent * cent, axis=-1, keepdims=True)
    rstd = lax.rsqrt(var + EPS)
    return cent * rstd, rstd


def norm_back(dh, gain, xhat, rstd):
    dn = dh * gain
    return rstd * (dn - jnp.mean(dn, axis=-1, keepdims=True) - xhat * jnp.mean(dn * xhat, axis=-1, keepdims=True))


def half_mask(shape, axis, h):
    i = lax.broadcasted_iota(jnp.int32, shape, axis)
    return (i < HEAD_DIM) if h == 0 else (i >= HEAD_DIM)


def attn_fwd_kernel(len_ref, x_ref, w_ref, s_ref, cos_ref, sin_ref, h_ref, q_ref, k_ref, v_ref, p_ref, ctx_ref, x1_ref):
    seq = pl.program_id(0)
    limit = len_ref[seq]
    for r in blocks(SEQ):
        rows = pl.ds(r, BLOCK)
        xhat, _ = normed(x_ref[0, rows].astype(F32))
        h_ref[0, rows] = (xhat * s_ref[0, 4:5] + s_ref[0, 5:6]).astype(BF)
        h = h_ref[0, rows]
        cos, sin = cos_ref[rows], sin_ref[rows]
        for j in range(2):
            cols = slice(BLOCK * j, BLOCK * j + BLOCK)
            for kind, dst in enumerate((q_ref, k_ref, v_ref)):
                t = dot(h, w_ref[kind, :, cols]) + s_ref[0, kind:kind + 1, cols]
                if kind == 0:
                    t = t * (HEAD_DIM ** -0.5)
                for i in range(2):
                    u = t[:, WIDE * i:WIDE * i + WIDE]
                    if kind < 2:
                        u = u * cos + swap_halves(u) * sin
                    dst[0, rows, BLOCK * j + WIDE * i:BLOCK * j + WIDE * i + WIDE] = u.astype(BF)
    valid = lax.broadcasted_iota(jnp.int32, (1, SEQ), 1) < limit

    def pair(j, _):
        lanes = pl.ds(pl.multiple_of(j * WIDE, WIDE), WIDE)
        k, v = k_ref[0, :, lanes], v_ref[0, :, lanes]
        for r in blocks(SEQ):
            rows = pl.ds(r, BLOCK)
            q = q_ref[0, rows, lanes]
            ctx = None
            for h in range(2):
                m = half_mask((SEQ, WIDE), 1, h)
                kh, vh = jnp.where(m, k, 0), jnp.where(m, v, 0)
                s = jnp.where(valid, dot(q, kh, 1, 1), NEG_BIG)
                e = jnp.exp(s - jnp.max(s, axis=-1, keepdims=True))
                p = (e * (1.0 / jnp.sum(e, axis=-1, keepdims=True))).astype(BF)
                p_ref[0, 2 * j + h, rows] = p
                part = dot(p, vh)
                ctx = part if ctx is None else ctx + part
            ctx_ref[0, rows, lanes] = ctx.astype(BF)
        return 0

    lax.fori_loop(0, 4, pair, 0)
    for r in blocks(SEQ):
        rows = pl.ds(r, BLOCK)
        out = dot(ctx_ref[0, rows], w_ref[3])
        x1_ref[0, rows] = (x_ref[0, rows].astype(F32) + out + s_ref[0, 3:4]).astype(BF)


def mlp_fwd_kernel(x_ref, w1_ref, w2_ref, s_ref, h_ref, a_ref, g_ref, y_ref):
    x = x_ref[0].astype(F32)
    xhat, _ = normed(x)
    h = (xhat * s_ref[0, 6:7] + s_ref[0, 7:8]).astype(BF)
    h_ref[0] = h
    acc = x + s_ref[0, 12:13]
    for j in range(4):
        cols = slice(CHUNK * j, CHUNK * j + CHUNK)
        pre = dot(h, w1_ref[:, cols]) + s_ref[0, 8 + j:9 + j]
        cdf = 0.5 * (1.0 + lax.erf(pre * (1.0 / math.sqrt(2.0))))
        pdf = jnp.exp(-0.5 * pre * pre) * (1.0 / math.sqrt(2.0 * math.pi))
        g_ref[0, :, cols] = cdf + pre * pdf
        a = (pre * cdf).astype(BF)
        a_ref[0, :, cols] = a
        acc = acc + dot(a, w2_ref[cols, :])
    y_ref[0] = acc.astype(BF)


def mlp_bwd_kernel(dy_ref, a_ref, g_ref, h_ref, x1_ref, w1_ref, w2_ref, s_ref, gw1_ref, gw2_ref, dmid_ref, gs_ref, acc_ref):
    j = pl.program_id(0)
    dy = dy_ref[...]
    gw2_ref[...] = dot(a_ref[...], dy, 0, 0)
    bias = jnp.zeros((1, DIM), F32)
    for r in blocks(TOKENS):
        rows = pl.ds(r, BLOCK)
        dpre = dot(dy_ref[rows], w2_ref[...], 1, 1) * g_ref[rows]
        bias = bias + jnp.sum(dpre, axis=0, keepdims=True)
        a_ref[rows] = dpre.astype(BF)
        part = dot(a_ref[rows], w1_ref[...], 1, 1)

        @pl.when(j == 0)
        def _():
            acc_ref[rows] = part

        @pl.when(j > 0)
        def _():
            acc_ref[rows] = acc_ref[rows] + part
    gs_ref[pl.ds(4 + j, 1)] = bias
    gw1_ref[...] = dot(h_ref[...], a_ref[...], 0, 0)

    @pl.when(j == 3)
    def _():
        sums = [jnp.zeros((1, DIM), F32) for _ in range(4)]
        for r in blocks(TOKENS):
            rows = pl.ds(r, BLOCK)
            dh = acc_ref[rows]
            xhat, rstd = normed(x1_ref[rows].astype(F32))
            d = dy_ref[rows].astype(F32)
            dmid = (d + norm_back(dh, s_ref[0, 6:7], xhat, rstd)).astype(BF)
            dmid_ref[rows] = dmid
            for i, t in enumerate((d, dh * xhat, dh, dmid.astype(F32))):
                sums[i] = sums[i] + jnp.sum(t, axis=0, keepdims=True)
        for i in range(4):
            gs_ref[i:i + 1] = sums[i]


def attn_bwd_kernel(dmid_ref, x_ref, h_ref, q_ref, k_ref, v_ref, p_ref, ctx_ref, w_ref, s_ref, cos_ref, sin_ref,
                    gw_ref, dx_ref, gs_ref, dctx_ref, dproj_ref):
    seq = pl.program_id(0)

    def put(dst, value):
        @pl.when(seq == 0)
        def _():
            dst[...] = value

        @pl.when(seq > 0)
        def _():
            dst[...] = dst[...] + value

    dmid = dmid_ref[0]
    for r in blocks(SEQ):
        rows = pl.ds(r, BLOCK)
        dctx_ref[rows] = dot(dmid_ref[0, rows], w_ref[3], 1, 1).astype(BF)
    put(gw_ref.at[3], dot(ctx_ref[0], dmid, 0, 0))

    def pair(j, _):
        lanes = pl.ds(pl.multiple_of(j * WIDE, WIDE), WIDE)
        q, k, v, dc = q_ref[0, :, lanes], k_ref[0, :, lanes], v_ref[0, :, lanes], dctx_ref[:, lanes]
        qt, dct = q.T, dc.T
        dq, dkt, dvt = None, None, None
        for h in range(2):
            m = half_mask((SEQ, WIDE), 1, h)
            mt = half_mask((WIDE, SEQ), 0, h)
            kh, vh = jnp.where(m, k, 0), jnp.where(m, v, 0)
            qh, dch = jnp.where(mt, qt, 0), jnp.where(mt, dct, 0)
            p = p_ref[0, 2 * j + h]
            part = dot(dch, p)
            dvt = part if dvt is None else dvt + part
            ds = []
            for r in blocks(SEQ):
                pf = p[r:r + BLOCK].astype(F32)
                dp = dot(dc[r:r + BLOCK], vh, 1, 1)
                ds.append((pf * (dp - jnp.sum(dp * pf, axis=-1, keepdims=True))).astype(BF))
            ds = jnp.concatenate(ds, axis=0)
            part = dot(ds, kh)
            dq = part if dq is None else dq + part
            part = dot(qh, ds)
            dkt = part if dkt is None else dkt + part
        cos, sin = cos_ref[...], sin_ref[...]
        dq = (dq * cos - swap_halves(dq) * sin) * (HEAD_DIM ** -0.5)
        dk = dkt.T
        dk = dk * cos - swap_halves(dk) * sin
        dv = dvt.T
        for i, t in enumerate((dq, dk, dv)):
            t = t.astype(BF)
            dproj_ref[i, :, lanes] = t
        return 0

    lax.fori_loop(0, 4, pair, 0)
    dh = None
    rowsums = []
    for i in range(3):
        d = dproj_ref[i]
        put(gw_ref.at[i], dot(h_ref[0], d, 0, 0))
        rowsums.append(jnp.sum(d.astype(F32), axis=0, keepdims=True))
        part = dot(d, w_ref[i], 1, 1)
        dh = part if dh is None else dh + part
    xhat, rstd = normed(x_ref[0].astype(F32))
    dx_ref[0] = (dmid.astype(F32) + norm_back(dh, s_ref[0, 4:5], xhat, rstd)).astype(BF)
    rowsums.append(jnp.sum(dh * xhat, axis=0, keepdims=True))
    rowsums.append(jnp.sum(dh, axis=0, keepdims=True))
    put(gs_ref, jnp.concatenate(rowsums + [jnp.zeros((3, DIM), F32)], axis=0))


VM = 56 * 2 ** 20


def whole(shape):
    n = len(shape)
    return pl.BlockSpec(shape, lambda *_: (0,) * n)


def per_seq(shape):
    n = len(shape)
    return pl.BlockSpec((1,) + shape, lambda i: (i,) + (0,) * n)


def at_layer(layer, shape):
    n = len(shape)
    return pl.BlockSpec((1,) + shape, lambda *_: (layer,) + (0,) * n)


def attn_fwd(layer, lengths, x, w, s, cos, sin):
    t = per_seq((SEQ, DIM))
    b = SD((2, SEQ, DIM), BF)
    return pl.pallas_call(
        attn_fwd_kernel, grid=(2,), name='attn_fwd',
        in_specs=[pl.BlockSpec(memory_space=pltpu.SMEM), t, whole((4, DIM, DIM)), at_layer(layer, (16, DIM)), whole((SEQ, WIDE)), whole((SEQ, WIDE))],
        out_specs=[t, t, t, t, per_seq((8, SEQ, SEQ)), t, t],
        out_shape=[b, b, b, b, SD((2, 8, SEQ, SEQ), BF), b, b],
        compiler_params=pltpu.CompilerParams(vmem_limit_bytes=VM),
    )(lengths, x, w, s, cos, sin)


def mlp_fwd(layer, x1, w1, w2, s):
    R = 256
    row = lambda n: pl.BlockSpec((1, R, n), lambda i: (i // 2, i % 2, 0))
    return pl.pallas_call(
        mlp_fwd_kernel, grid=(4,), name='mlp_fwd',
        in_specs=[row(DIM), whole((DIM, FFN)), whole((FFN, DIM)), at_layer(layer, (16, DIM))],
        out_specs=[row(DIM), row(FFN), row(FFN), row(DIM)],
        out_shape=[SD((2, SEQ, DIM), BF), SD((2, SEQ, FFN), BF), SD((2, SEQ, FFN), F32), SD((2, SEQ, DIM), BF)],
        compiler_params=pltpu.CompilerParams(vmem_limit_bytes=VM),
    )(x1, w1, w2, s)


def mlp_bwd(layer, dy, a, g, h, x1, w1, w2, s):
    flat = lambda t: t.reshape(TOKENS, t.shape[-1])
    full = whole((TOKENS, DIM))
    return pl.pallas_call(
        mlp_bwd_kernel, grid=(4,), name='mlp_bwd',
        in_specs=[full, pl.BlockSpec((TOKENS, CHUNK), lambda j: (0, j)), pl.BlockSpec((TOKENS, CHUNK), lambda j: (0, j)), full, full,
                  pl.BlockSpec((DIM, CHUNK), lambda j: (0, j)), pl.BlockSpec((CHUNK, DIM), lambda j: (j, 0)), at_layer(layer, (16, DIM))],
        out_specs=[pl.BlockSpec((DIM, CHUNK), lambda j: (0, j)), pl.BlockSpec((CHUNK, DIM), lambda j: (j, 0)), full, whole((8, DIM))],
        out_shape=[SD((DIM, FFN), F32), SD((FFN, DIM), F32), SD((TOKENS, DIM), BF), SD((8, DIM), F32)],
        scratch_shapes=[pltpu.VMEM((TOKENS, DIM), F32)],
        compiler_params=pltpu.CompilerParams(vmem_limit_bytes=VM),
    )(flat(dy), flat(a), flat(g), flat(h), flat(x1), w1, w2, s)


def attn_bwd(layer, dmid, x, h, q, k, v, p, ctx, w, s, cos, sin):
    t = per_seq((SEQ, DIM))
    return pl.pallas_call(
        attn_bwd_kernel, grid=(2,), name='attn_bwd',
        in_specs=[t, t, t, t, t, t, per_seq((8, SEQ, SEQ)), t, whole((4, DIM, DIM)), at_layer(layer, (16, DIM)), whole((SEQ, WIDE)), whole((SEQ, WIDE))],
        out_specs=[whole((4, DIM, DIM)), t, whole((8, DIM))],
        out_shape=[SD((4, DIM, DIM), F32), SD((2, SEQ, DIM), BF), SD((8, DIM), F32)],
        scratch_shapes=[pltpu.VMEM((SEQ, DIM), BF), pltpu.VMEM((3, SEQ, DIM), BF)],
        compiler_params=pltpu.CompilerParams(vmem_limit_bytes=VM),
    )(dmid.reshape(2, SEQ, DIM), x, h, q, k, v, p, ctx, w, s, cos, sin)


def compute(x, lengths, d_y, whole_wts, small):
    cos, sin = (jnp.asarray(t) for t in rotary_tables())
    saved, y = [], x
    for l in range(2):
        fa, fu, fd = whole_wts[l]
        h1, q, k, v, p, ctx, x1 = attn_fwd(l, lengths, y, fa, small, cos, sin)
        h2, a, g, y2 = mlp_fwd(l, x1, fu, fd, small)
        saved.append((y, h1, q, k, v, p, ctx, x1, h2, a, g))
        y = y2
    d, grads = d_y, [None, None]
    for l in (1, 0):
        x_in, h1, q, k, v, p, ctx, x1, h2, a, g = saved[l]
        fa, fu, fd = whole_wts[l]
        gu, gd, dmid, s_mlp = mlp_bwd(l, d, a, g, h2, x1, fu, fd, small)
        ga, d, s_attn = attn_bwd(l, dmid, x_in, h1, q, k, v, p, ctx, fa, small, cos, sin)
        grads[l] = (ga, gu, gd, s_mlp, s_attn)
    return d, grads


def pack_small(b_attn, ln_par, b_up, b_down, index):
    rows = jnp.concatenate([b_attn, ln_par, b_down[:, None]], axis=1).astype(F32)
    rows = lax.dynamic_update_slice(jnp.zeros((2, 9, DIM), F32), rows, (0, 0, 2 * index))
    ups = lax.dynamic_update_slice(jnp.zeros((2, FFN), F32), b_up.astype(F32), (0, 8 * index))
    return jnp.concatenate([rows[:, :8], ups.reshape(2, 4, DIM), rows[:, 8:], jnp.zeros((2, 3, DIM), F32)], axis=1)


def solution(mesh):
    grid = Mesh(mesh.devices.reshape([SIZES[a] for a in AXES]), AXES)
    first, second, third = P(AXES), P(None, AXES), P(None, None, AXES)
    weight_specs = (third, third, third, second, second, second, second)

    def device_step(x, lengths, d_y, w_attn, b_attn, ln_par, w_up, b_up, w_down, b_down):
        index = lax.axis_index(AXES)
        whole_wts, small = gather(w_attn, w_up, w_down, pack_small(b_attn, ln_par, b_up, b_down, index))
        d_x, grads = compute(x, lengths, d_y, whole_wts, small)
        o_attn, o_up, o_down, sums = scatter([g for layer in grads for g in layer[:3]], [s for layer in grads for s in layer[3:]])
        pick = lax.dynamic_slice(sums, (0, 0, 2 * index), (2, 16, 2))
        ups = lax.dynamic_slice(sums[:, 4:8].reshape(2, FFN), (0, 8 * index), (2, 8))
        rows = lambda *ids: jnp.stack([pick[:, i] for i in ids], axis=1)
        return d_x, o_attn, rows(8, 9, 10, 3), rows(11, 12, 1, 2), o_up, ups, o_down, pick[:, 0]

    return jax.shard_map(device_step, mesh=grid, in_specs=(first,) * 3 + weight_specs, out_specs=(first,) + weight_specs, check_vma=False)
```

time: 4170 us -> 407 us (0.10)
  waiting for transfers between devices: 3130 us -> 0 us
  blocking collectives: 597 us -> 0 us
  Pallas kernels: 0 us -> 387 us
  matrix products: 192 us -> 0 us
  other arithmetic: 132 us -> 6.24 us
  local copies, waits for them, and re-layouts: 90.1 us -> 11.4 us
    reduce_scatter x2 -> x0, waiting for transfers between devices: 2400 us -> none  [scatter_grads(): reduce_rows(gw_down, scatter_dimension=0)]
    all_gather x6 -> x0, blocking collectives: 441 us -> none  [the longest x4 290 us: gather_layer(): lax.all_gather(ln_par, axis_name, axis=1, tiled=True)]
    all_gather x11 -> x0, waiting for transfers between devices: 419 us -> none  [the longest x4 178 us: gather_layer(): lax.all_gather(w_attn, axis_name, axis=1, tiled=True)]
    pallas_call x0 -> x10, Pallas kernels: none -> 387 us  [the longest x1 141 us: scatter(): pl.pallas_call(scatter_kernel, name='scatter', in_specs=any_space(len(til...]
    unnamed x15 -> x0, waiting for transfers between devices: 312 us -> none
    dot_general x33 -> x0, matrix products: 170 us -> none  [the longest x2 30.7 us: layer_backward(): jnp.einsum('blf,bld->fd', act_bf, d_out, preferred_element_type=jnp.float32)]
    unnamed x2 -> x0, blocking collectives: 156 us -> none
    convert_element_type x20 -> x2, other arithmetic: 85.1 us -> 1.43 us  [the longest x1 0.77 us: pack_small(): jnp.concatenate([b_attn, ln_par, b_down[:, None]], axis=1).astype(F32)]
  transfers between devices with their start and end apart: 14 -> 0, of which waited for: 8 -> 0; matrix products, arithmetic and copies ran while one was open for 8% -> 0% of each run, Pallas kernels for 0% -> 0%
where the time goes in v1:
time: 407 us; the launch traced here: 406 us
  Pallas kernels  387 us (95%)
  local copies, waits for them, and re-layouts  11.4 us (3%)
  other arithmetic  6.24 us (2%)
    pallas_call x1, Pallas kernels, scatter(): pl.pallas_call(scatter_kernel, name='scatter', in_specs=any_space(len(til...  141 us
    pallas_call x1, Pallas kernels, gather(): pl.pallas_call(gather_kernel, name='gather', in_specs=in_vmem(len(shards)...  78 us
    pallas_call x2, Pallas kernels, attn_bwd(): pl.pallas_call(attn_bwd_kernel, grid=(2,), name='attn_bwd', in_specs=[t,...  56.5 us
    pallas_call x2, Pallas kernels, mlp_bwd(): pl.pallas_call(mlp_bwd_kernel, grid=(4,), name='mlp_bwd', in_specs=[full,...  44.2 us
    pallas_call x2, Pallas kernels, attn_fwd(): pl.pallas_call(attn_fwd_kernel, grid=(2,), name='attn_fwd', in_specs=[pl....  41.5 us
    pallas_call x2, Pallas kernels, mlp_fwd(): pl.pallas_call(mlp_fwd_kernel, grid=(4,), name='mlp_fwd', in_specs=[row(D...  26.3 us

profile of v1, /device:TPU:1, one launch (start us, length us, event | category | flops | bytes accessed | tf_op | source)
XLA Modules:
  0.0 405.7 jit_solution(7100170787918089703)
XLA Ops:
  0.6 0.8 copy.25
  1.4 0.8 maximum_convert_fusion
  2.2 0.1 copy.26
  2.3 0.5 dynamic_update_slice.6
  2.8 0.7 convert_element_type.7
  3.5 0.2 dynamic_update_slice.7
  3.7 0.1 pad.13.clone
  3.8 0.7 maximum_maximum_fusion.refs_6_
  4.5 1.3 slice_bitcast_fusion.1
  5.8 1.3 slice_bitcast_fusion.2
  7.2 1.3 slice_bitcast_fusion.3
  8.5 78.0 %gather.1 = (bf16[4,8,4,2,4,2,2,2,128]{8,7,6,5,4,3,2,1,0:T(2,128)(2,1)}, bf16[8,4,2,16,2,2,2,128]{7,6,5,4,3,2,1,0:T(2,128)(2,1)}, bf16[8,4,4,2,4,8,128]{6,5,4,3,...) custom-call(bf16[4,4,2,128]{3,2,1,0:T(2,128)(2,1)} %get-tuple-elemen, ...), custom_call_target="tpu_custom_call" | custom-call | tf_op jit(solution)/shard_map/gather/pallas_call | solution.py:269
  86.5 20.8 %attn_fwd.2 = (bf16[2,512,512]{2,1,0:T(8,128)(2,1)}, bf16[2,512,512]{2,1,0:T(8,128)(2,1)}, bf16[2,512,512]{2,1,0:T(8,128)(2,1)}, bf16[2,512,512]{2,1,0:T(8,128)(...) custom-call(s32[2]{0:T(128)} %len_ref.3, ...), custom_call_target="tpu_custom_call" | custom-call | tf_op jit(solution)/shard_map/attn_fwd/pallas_call | solution.py:570
  107.3 13.1 %mlp_fwd.2 = (bf16[2,512,512]{2,1,0:T(8,128)(2,1)}, bf16[2,512,2048]{2,1,0:T(8,128)(2,1)}, f32[2,512,2048]{2,1,0:T(8,128)}, bf16[2,512,512]{2,1,0:T(8,128)(2,1)}) custom-call(bf16[2,512,512]{2,1,0:T(8,128)(2,1)} %get-tuple-element.59.x_ref, bf16[512,2048]{1,0:T(8,128)(2,1)} %bitcast.137, bf16[2048,512]{1,0:T(8,128)(2,1)} %bitcast.139, ...), custom_call_target="tpu_custom_call" | custom-call | tf_op jit(solution)/shard_map/mlp_fwd/pallas_call | solution.py:582
  120.4 20.7 %attn_fwd.3 = (bf16[2,512,512]{2,1,0:T(8,128)(2,1)}, bf16[2,512,512]{2,1,0:T(8,128)(2,1)}, bf16[2,512,512]{2,1,0:T(8,128)(2,1)}, bf16[2,512,512]{2,1,0:T(8,128)(...) custom-call(s32[2]{0:T(128)} %len_ref.3, ...), custom_call_target="tpu_custom_call" | custom-call | tf_op jit(solution)/shard_map/attn_fwd/pallas_call | solution.py:570
  141.1 13.2 %mlp_fwd.3 = (bf16[2,512,512]{2,1,0:T(8,128)(2,1)}, bf16[2,512,2048]{2,1,0:T(8,128)(2,1)}, f32[2,512,2048]{2,1,0:T(8,128)}, bf16[2,512,512]{2,1,0:T(8,128)(2,1)}) custom-call(bf16[2,512,512]{2,1,0:T(8,128)(2,1)} %get-tuple-element.64.x_ref, bf16[512,2048]{1,0:T(8,128)(2,1)} %bitcast.141, bf16[2048,512]{1,0:T(8,128)(2,1)} %bitcast.143, ...), custom_call_target="tpu_custom_call" | custom-call | tf_op jit(solution)/shard_map/mlp_fwd/pallas_call | solution.py:582
  154.3 22.0 %mlp_bwd.2 = (f32[512,2048]{1,0:T(8,128)}, f32[2048,512]{1,0:T(8,128)}, bf16[1024,512]{1,0:T(8,128)(2,1)}, f32[8,512]{1,0:T(8,128)}) custom-call(bf16[1024,512]{1,0:T(8,128)(2,1)} %bitcast.155, bf16[1024,2048]{1,0:T(8,128)(2,1)} %bitcast.146, f32[1024,2048]{1,0:T(8,128)} %bitcast.136, bf16[1024,512]{1,0:T(8,128)(2,1)} %bitcast.160, ...), custom_call_target="tpu_custom_call" | custom-call | tf_op jit(solution)/shard_map/mlp_bwd/pallas_call | solution.py:594
  176.3 28.3 %attn_bwd.2 = (f32[4,512,512]{2,1,0:T(8,128)}, bf16[2,512,512]{2,1,0:T(8,128)(2,1)}, f32[8,512]{1,0:T(8,128)}) custom-call(bf16[2,512,512]{2,1,0:T(8,128)(2,1)} %bitcast.159, bf16[2,512,512]{2,1,0:T(8,128)(2,1)} %get-tuple-element.62.x_ref, bf16[2,512,512]{2,1,0:T(8,128)(2,1)} %get-tuple-element.71.h_ref, bf16[2,512,512]{2,1,0:T(8,128)(2,1)} %get-tuple-element.72.q_ref, ...), custom_call_target="tpu_custom_call" | custom-call | tf_op jit(solution)/shard_map/attn_bwd/pallas_call | solution.py:607
  204.6 22.2 %mlp_bwd.3 = (f32[512,2048]{1,0:T(8,128)}, f32[2048,512]{1,0:T(8,128)}, bf16[1024,512]{1,0:T(8,128)(2,1)}, f32[8,512]{1,0:T(8,128)}) custom-call(bf16[1024,512]{1,0:T(8,128)(2,1)} %bitcast.158, bf16[1024,2048]{1,0:T(8,128)(2,1)} %bitcast.145, f32[1024,2048]{1,0:T(8,128)} %bitcast.135, bf16[1024,512]{1,0:T(8,128)(2,1)} %bitcast.156, ...), custom_call_target="tpu_custom_call" | custom-call | tf_op jit(solution)/shard_map/mlp_bwd/pallas_call | solution.py:594
  226.8 28.2 %attn_bwd.3 = (f32[4,512,512]{2,1,0:T(8,128)}, bf16[2,512,512]{2,1,0:T(8,128)(2,1)}, f32[8,512]{1,0:T(8,128)}) custom-call(bf16[2,512,512]{2,1,0:T(8,128)(2,1)} %bitcast.157, bf16[2,512,512]{2,1,0:T(8,128)(2,1)} %x_ref.3, bf16[2,512,512]{2,1,0:T(8,128)(2,1)} %get-tuple-element.82.h_ref, bf16[2,512,512]{2,1,0:T(8,128)(2,1)} %get-tuple-element.83.q_ref, ...), custom_call_target="tpu_custom_call" | custom-call | tf_op jit(solution)/shard_map/attn_bwd/pallas_call | solution.py:607
  255.0 140.9 %scatter.1 = (f32[4,4,2,128]{3,2,1,0:T(2,128)}, f32[16,2,128]{2,1,0:T(2,128)}, f32[4,8,128]{2,1,0:T(8,128)}, f32[4,4,2,128]{3,2,1,0:T(2,128)}, f32[16,2,128]{2,1...) custom-call(f32[4,8,4,2,4,8,128]{6,5,4,3,2,1,0:T(8,128)} %bitcast.154, f32[8,4,2,16,8,128]{5,4,3,2,1,0:T(8,128)} %bitcast.152, ...), custom_call_target="tpu_custom_call" | custom-call | tf_op jit(solution)/shard_map/scatter/pallas_call | solution.py:320
  395.9 1.4 pad_maximum_fusion.2
  397.3 1.4 pad_maximum_fusion.1
  398.6 0.8 slice_bitcast_fusion
  399.4 0.6 constant_dynamic-slice_fusion.4
  400.0 0.8 constant_dynamic-slice_fusion.1
  400.8 0.7 copy.28
  401.5 0.8 constant_dynamic-slice_fusion.3
  402.3 1.4 constant_dynamic-slice_fusion.5
  403.7 0.7 copy.27
  404.4 1.4 pad_maximum_fusion
  (9 shorter events, 0.1 us)

commit v2 on v0

v2 whole, which is shorter than its diff:
```python
import math
import jax
import jax.numpy as jnp
import numpy as np
from jax import lax
from jax.experimental import pallas as pl
from jax.experimental.pallas import tpu as pltpu
from jax.sharding import Mesh, PartitionSpec as P

HEAD_DIM, EPS, THETA, NEG_BIG = 64, 1e-5, 10000.0, -1e30
SEQ, DIM, FFN, TOKENS, CHUNK, BLOCK, WIDE = 512, 512, 2048, 1024, 512, 256, 128
LAYERS = CORES = SEQS = PAIR = 2
MATRICES = CHUNKS = QUAD = 4
HEADS = OCT = 8
SMALL = 16
F32, BF = jnp.float32, jnp.bfloat16
SD = jax.ShapeDtypeStruct
AXES = ('z', 'y', 'x', 'c')
SIZES = dict(z=OCT, y=QUAD, x=QUAD, c=PAIR, k=PAIR, h=PAIR, l=PAIR, r=PAIR)
TILE = (OCT, WIDE)
ALL = slice(None)
BIAS_OUT, GAIN1, SHIFT1, GAIN2, SHIFT2, BIAS_UP, BIAS_DOWN = 3, 4, 5, 6, 7, 8, 12
TILED = dict(part='kzyht', slim='zyht', pair='zyht', up='zyht', down='zyxct')
FINE = dict(attn='kzyhtlcr', up='zyhtlcr', down='zyxct')
LANE_TILES = dict(attn=QUAD, part=PAIR, slim=PAIR, pair=PAIR, up=OCT, down=PAIR)
OWNER = dict(x='xhl', y='y', z='z')
UNITS = dict(up='yzx', down='xyz', part='hyzl', slim='yzx', pair='hyzl')
MLP_STEPS, ATTN_STEPS = CHUNKS, 8
LAYER_STEPS = MLP_STEPS + ATTN_STEPS
STEPS = LAYERS * LAYER_STEPS
SETS = (('up', 'up', ('t', PAIR, CHUNKS)), ('down', 'down', ('z', PAIR, CHUNKS)), ('first', 'part', ('z', OCT, 1)), ('second', 'slim', ('z', OCT, 1)), ('third', 'pair', ('z', OCT, 1)))
SCHEDULE = {(1, 'up'): 'ABCDEKNOP', (1, 'down'): 'ABCDEKNOP', (1, 'first'): 'HLNOPTU', (1, 'second'): 'LMPQSV', (1, 'third'): 'LMPQSTV',
            (0, 'up'): 'MNOPQVcd', (0, 'down'): 'MNOPQVcd', (0, 'first'): 'TUX', (0, 'second'): 'Xa', (0, 'third'): 'Xa'}
ENDING = 'mstfmudstfmstfmstftmm'
VM = 56 << 20


def spot(at):
    return dict(at, h=lax.div(at['x'], SIZES['l']), l=lax.rem(at['x'], SIZES['l']))


def only(at, names):
    return {n: at[n] for n in names if n in at}


def view(ref, names, pick):
    return ref.at[tuple(pick.get(n, ALL) for n in names)]


class Place:
    def __init__(self, send, recv):
        self.me = spot({a: lax.axis_index(a) for a in AXES})
        self.send, self.recv, self.used = send, recv, 0

    def shifted(self, axis, s):
        at = dict(self.me, **{axis: lax.rem(self.me[axis] + s, SIZES[axis])})
        if axis in 'hl':
            at['x'] = SIZES['l'] * at['h'] + at['l']
        return spot(at)

    def device(self, axis, s):
        at = self.shifted(axis, s)
        return tuple(at[a] for a in AXES)

    def peers(self, axis):
        n = SIZES[axis]
        return sorted(range(1, n), key=lambda s: min(s, n - s))

    def signal(self, sem, axis, s):
        pl.semaphore_signal(sem, inc=1, device_id=self.device(axis, s), device_id_type=pl.DeviceIdType.MESH)

    def greet(self):
        bar = pltpu.get_barrier_semaphore()
        everyone = [(a, s) for a in AXES for s in self.peers(a)]
        for a, s in everyone:
            self.signal(bar, a, s)
        pl.semaphore_wait(bar, len(everyone))

    def begin(self, build):
        self.used += 1
        assert self.used <= self.send.shape[0]
        build().start()
        return lambda: build().wait()

    def copy(self, axis, s, refs):
        i = self.used

        def build():
            src, dst = refs()
            return pltpu.make_async_remote_copy(src, dst, self.send.at[i], self.recv.at[i], device_id=self.device(axis, s), device_id_type=pl.DeviceIdType.MESH)
        return self.begin(build)

    def local(self, refs):
        i = self.used
        return self.begin(lambda: pltpu.make_async_copy(*refs(), self.send.at[i]))


def half(kind, core, part):
    if kind == 'attn':
        return dict(k=pl.ds(core * CORES + part, 1))
    return dict(t=pl.ds(core * LANE_TILES[kind], LANE_TILES[kind]))


def gathered(kind, full, part):
    names = FINE[kind]
    return lambda core, fixed, at: view(full, names, dict(half(kind, core(at), part), **only(at, fixed)))


def own(at):
    return at['c']


def other(at):
    return 1 - at['c']


def gather_early(place, kind, part, order, full, shard):
    block = gathered(kind, full, part)
    names = FINE[kind]
    mine = [n for n in names if n not in 'tkr']
    rows = [n for n in names if n in 'tk'] + ['r', 'r']

    def piece(core):
        return view(shard, rows, half(kind, core(place.me), part))
    waits = [place.local(lambda: (piece(own), block(own, mine, place.me))),
             place.copy('c', 1, lambda: (piece(other), block(other, mine, place.me)))]
    for i in range(len(order) - 1):
        yield
        for w in waits:
            w()
        fixed = ''.join(OWNER[a] for a in order[i:])
        waits = [place.copy(order[i], s, lambda: (block(own, fixed, place.me),) * PAIR) for s in place.peers(order[i])]
    yield
    for w in waits:
        w()


def gather_late(place, kind, part, order, full):
    block = gathered(kind, full, part)
    axis = order[-1]
    fixed = OWNER[axis]
    same = lambda at: (block(own, fixed, at),) * PAIR
    waits = [(s, place.copy(axis, s, lambda: same(place.me))) for s in place.peers(axis)]
    last = [place.copy('c', 1, lambda: same(place.me))]
    for s, w in waits:
        yield
        w()
        last.append(place.copy('c', 1, lambda s=s: same(place.shifted(axis, SIZES[axis] - s))))
    yield
    for w in last:
        w()


def gather_whole(*args):
    yield from gather_early(*args)
    yield from gather_late(*args[:-1])


def unravel(i, shape):
    idx = []
    for n in reversed(shape):
        idx.append(lax.rem(i, n))
        i = lax.div(i, n)
    return tuple(reversed(idx))


def each(shape, body):
    def step(i, carry):
        body(unravel(i, shape))
        return carry
    lax.fori_loop(0, math.prod(shape), step, 0)


def total_unit(place, value, out, slots):
    me = place.me
    keep, slot, *slots = slots
    wait = place.copy('c', 1, lambda: (value.at[other(me)], slot.at[0]))
    yield
    wait()
    keep[...] = value[me['c']] + slot[0]
    for axis, slot in zip('xyz', slots):
        last = SIZES[axis] - 1
        slot[last] = keep[...]
        waits = [place.copy(axis, s, lambda s=s: (slot.at[last], slot.at[s - 1])) for s in place.peers(axis)]
        yield
        for w in waits:
            w()
        v = slot[0]
        for s in range(1, SIZES[axis]):
            v = v + slot[s]
        keep[...] = v
    out[me['c']] = keep[...]
    wait = place.copy('c', 1, lambda: (keep, out.at[me['c']]))
    yield
    wait()


def total_buffers():
    return [pltpu.VMEM((SMALL, DIM), F32)] + [pltpu.VMEM((SIZES[a], SMALL, DIM), F32) for a in 'cxyz']


def run(units):
    units = list(units)
    while units:
        units = [u for u in units if next(u, units) is not units]


def free_sizes(kind, names):
    return tuple(LANE_TILES[kind] if n == 't' else SIZES[n] for n in names) + TILE


def plan(kind):
    left = TILED[kind]
    for axis in UNITS[kind]:
        d = axis if axis in left else 'h' if axis == 'x' else ''
        left = left.replace(d, '')
        yield axis, d, left


def unit_buffers(kind, layers):
    slots = [pltpu.VMEM((SIZES[axis] - 1,) + free_sizes(kind, left), F32) for axis, _, left in plan(kind)]
    *_, (_, _, left) = plan(kind)
    _, _, first = next(plan(kind))
    shapes = [(PAIR,) + free_sizes(kind, TILED[kind]), free_sizes(kind, TILED[kind]), free_sizes(kind, first)]
    return [pltpu.VMEM(s, F32) for s in shapes] + slots[:1] + (slots[1:] + [pltpu.VMEM(free_sizes(kind, left.replace('c', '')), F32)]) * layers


def reduce_unit(place, kind, bufs, finish, pieces, give, take):
    grad, got, first, slots, *rest = bufs
    me = place.me
    whole_grad, whole_names = grad, 'g' + TILED[kind]
    names, pick = whole_names, dict(g=me['c'])
    dim, size, count = pieces

    def cut(i, n=1):
        return {dim: pl.ds(size * i, size * n)}

    def accumulate(terms, fixed, into, piece=None):
        left = [n for n in names if n not in fixed]
        lead = left[:-3]
        sizes_of = dict(SIZES, t=LANE_TILES[kind])
        if piece is not None:
            sizes_of[dim] = size

        def body(idx):
            loop = dict(zip(lead, idx))
            if piece is not None:
                loop[dim] = loop[dim] + size * piece if dim in loop else pl.ds(size * piece, size)
            mine = tuple(fixed.get(n, loop.get(n, ALL)) for n in names)
            at = tuple(loop.get(n, ALL) for n in left)
            v = grad[mine]
            for ref in terms:
                v = v + ref[at]
            into[mine if into is grad else at] = v
        if lead:
            each([sizes_of[n] for n in lead], body)
        else:
            body(())

    (axis, d, left), *later = plan(kind)
    arrived, waits = [], []

    def begin(start, n):
        if not waits:
            take(1)
        for i in range(start, start + n):
            arrived[i]()
            accumulate([got], pick, grad, i)
        for s in place.peers(axis):
            waits.append(place.copy(axis, s, lambda s=s: (view(whole_grad, whole_names, dict(only(place.shifted(axis, s), d), g=me['c'], **cut(start, n))),
                                                          view(slots, 's' + TILED[kind].replace(d, ''), dict(cut(start, n), s=s - 1)))))
    take(0)
    for i in range(count):
        arrived.append(place.copy('c', 1, lambda i=i: (view(whole_grad, whole_names, dict(cut(i), g=other(me))), view(got, TILED[kind], cut(i)))))
        if i and count == PAIR * i:
            begin(0, i)
        yield
    begin(count // PAIR, count - count // PAIR)
    give(0)
    yield
    for w in waits:
        w()
    pick = dict(pick, **only(me, d))
    accumulate([slots.at[s] for s in range(SIZES[axis] - 1)], pick, first)
    give(1)
    grad, names, pick = first, left, {}
    for axis, d, left in later:
        slots, *rest = rest
        waits = [place.copy(axis, s, lambda s=s: (view(first, names, dict(pick, **only(place.shifted(axis, s), d))), slots.at[s - 1])) for s in place.peers(axis)]
        yield
        for w in waits:
            w()
        pick = dict(pick, **only(me, d))
        accumulate([slots.at[s] for s in range(SIZES[axis] - 1)], pick, first)
    away, = rest
    last = (lambda core: dict(pick, c=core(me))) if 'c' in left else (lambda core: pick)
    wait = place.copy('c', 1, lambda: (view(first, names, last(other)), away))
    yield
    wait()
    rows = ALL if kind == 'down' else pl.ds((me['l'] * PAIR + me['c']) * PAIR, PAIR)
    finish(own(me), first[tuple(last(own).get(n, ALL) for n in names) + (rows,)])
    finish(other(me), away[..., rows, :])


def blocks(n):
    return range(0, n, BLOCK)


def lane(i):
    return slice(WIDE * i, WIDE * i + WIDE)


def dot(a, b, ca=1, cb=0):
    return lax.dot_general(a, b, (((ca,), (cb,)), ((), ())), preferred_element_type=F32)


def rotary_tables():
    half_dim = HEAD_DIM // PAIR
    inv = (1.0 / (THETA ** (np.arange(half_dim, dtype=np.float32) * np.float32(2.0 / HEAD_DIM)))).astype(np.float32)
    ang = np.arange(SEQ, dtype=np.float32)[:, None] * inv[None, :]
    cos, sin = np.cos(ang), np.sin(ang)
    return np.tile(cos, (1, QUAD)), np.concatenate([-sin, sin] * PAIR, axis=1)


def swap_halves(t):
    n = HEAD_DIM // PAIR
    lanes = lax.broadcasted_iota(jnp.int32, t.shape, 1)
    return jnp.where(lax.rem(lanes, HEAD_DIM) < n, pltpu.roll(t, WIDE - n, 1), pltpu.roll(t, n, 1))


def normed(t):
    cent = t - jnp.mean(t, axis=-1, keepdims=True)
    rstd = lax.rsqrt(jnp.mean(cent * cent, axis=-1, keepdims=True) + EPS)
    return cent * rstd, rstd


def norm_back(dh, gain, xhat, rstd):
    dn = dh * gain
    return rstd * (dn - jnp.mean(dn, axis=-1, keepdims=True) - xhat * jnp.mean(dn * xhat, axis=-1, keepdims=True))


def row(ref, i):
    return ref[i:i + 1]


def half_mask(shape, axis, h):
    i = lax.broadcasted_iota(jnp.int32, shape, axis)
    return i >= HEAD_DIM if h else i < HEAD_DIM


def any_space(n):
    return [pl.BlockSpec(memory_space=pl.ANY)] * n


def in_vmem(n):
    return [pl.BlockSpec(memory_space=pltpu.VMEM)] * n


def semaphores(n):
    return [pltpu.SemaphoreType.DMA((n,))] * PAIR


def whole(shape, **kw):
    return pl.BlockSpec(shape, lambda *_: (0,) * len(shape), **kw)


def tiles_to_rows(t):
    *lead, r, n, s, w = t.shape
    return t.swapaxes(-3, -2).reshape(*lead, r * s, n * w)


def natural(kind, full):
    n = full.shape[FINE[kind].index('t')]
    lead = (MATRICES,) if kind == 'attn' else ()
    return tiles_to_rows(full.reshape(*lead, -1, n, *TILE))


def fine_shape(kind):
    n = LANE_TILES[kind] if kind == 'attn' else PAIR * LANE_TILES[kind]
    dims = dict(SIZES, t=n, k=MATRICES)
    return tuple(dims[d] for d in FINE[kind]) + ((WIDE,) if 'r' in FINE[kind] else TILE)


GATHERS = (('attn', 0, 0, 'zxy'), ('attn', 0, 1, 'zyx'), ('up', 0, 0, 'zxy'), ('down', 0, 0, 'zyx'),
           ('attn', 1, 0, 'zxy'), ('attn', 1, 1, 'zyx'), ('up', 1, 0, 'zxy'), ('down', 1, 0, 'zyx'))
LATE = (GATHERS[2:6], GATHERS[6:])
KINDS = tuple(FINE)


def gather_kernel(sa, su, sd, b_attn, ln, b_up, b_down, *refs):
    n = LAYERS * len(KINDS)
    full, total, value, slots, sems = refs[:n], refs[n], refs[n + 1], refs[n + 2:-2], refs[-2:]
    place = Place(*sems)
    place.greet()
    shards, full = dict(zip(KINDS, (sa, su, sd))), dict(zip([(k, l) for l in range(LAYERS) for k in KINDS], full))
    me = place.me
    index = ((me['z'] * SIZES['y'] + me['y']) * SIZES['x'] + me['x']) * CORES + me['c']

    def spread(v, rows):
        n = v.shape[1]
        at = lax.broadcasted_iota(jnp.int32, (rows, DIM), 1) - n * index
        if v.shape[0] < rows:
            at = at + DIM * lax.broadcasted_iota(jnp.int32, (rows, DIM), 0)
        return sum(jnp.where(at == i, v[:, i:i + 1], 0.0) for i in range(n))
    value[...] = jnp.zeros_like(value)
    for l in range(LAYERS):
        value[l, :GAIN1] = spread(b_attn[l].astype(F32), QUAD)
        value[l, GAIN1:BIAS_UP] = spread(ln[l].astype(F32), QUAD)
        value[l, BIAS_UP:BIAS_DOWN] = spread(b_up[l:l + 1].astype(F32), QUAD)
        value[l, BIAS_DOWN:BIAS_DOWN + 1] = spread(b_down[l:l + 1].astype(F32), 1)
    units = [(gather_early if g in sum(LATE, ()) else gather_whole)(place, g[0], *g[2:], full[g[:2]], shards[g[0]].at[g[1]]) for g in GATHERS]
    run([units[0], units[1], total_unit(place, value, total, slots)] + units[2:])


def gather(attn, up, down, *small):
    shards = [attn.reshape(LAYERS, MATRICES, PAIR, -1, WIDE).swapaxes(-3, -2), up.reshape(LAYERS, PAIR, -1, WIDE).swapaxes(-3, -2),
              down.reshape(LAYERS, OCT, -1, WIDE).swapaxes(-3, -2)]
    keys = [(k, l) for l in range(LAYERS) for k in KINDS]
    *full, total = pl.pallas_call(
        gather_kernel, name='gather',
        in_specs=in_vmem(len(shards) + len(small)), out_specs=any_space(len(keys)) + in_vmem(1),
        out_shape=[SD(fine_shape(k), BF) for k, _ in keys] + [SD((LAYERS, SMALL, DIM), F32)],
        scratch_shapes=[pltpu.VMEM((LAYERS, SMALL, DIM), F32)] + total_buffers() + semaphores(200),
        compiler_params=pltpu.CompilerParams(collective_id=1, has_side_effects=True),
    )(*shards, *small)
    return dict(zip(keys, full)), total


def attn_fwd_kernel(late, len_ref, x_ref, w_ref, s_ref, cos_ref, sin_ref, *refs):
    h_ref, q_ref, k_ref, v_ref, ctx_ref, x1_ref, p_ref, *full = refs[:-2]
    t = pl.program_id(0)
    seq, j = lax.div(t, QUAD), lax.rem(t, QUAD)
    place = Place(*refs[-2:])
    full = dict(zip(sorted({g[:2] for g in late}), full))
    gens = []

    @pl.when(t == 0)
    def _():
        place.greet()
        for g in late:
            gens.append(gather_late(place, g[0], *g[2:], full[g[:2]]))
            next(gens[-1])

    @pl.when(j == 0)
    def _():
        for r in blocks(SEQ):
            rows = pl.ds(r, BLOCK)
            xhat, _ = normed(x_ref[0, rows].astype(F32))
            h_ref[0, rows] = (xhat * row(s_ref, GAIN1) + row(s_ref, SHIFT1)).astype(BF)
            h = h_ref[0, rows]
            cos, sin = cos_ref[rows], sin_ref[rows]
            for c in blocks(DIM):
                cols = slice(c, c + BLOCK)
                for kind, dst in enumerate((q_ref, k_ref, v_ref)):
                    u = dot(h, w_ref[kind, :, cols]) + s_ref[kind:kind + 1, cols]
                    if dst is q_ref:
                        u = u * (HEAD_DIM ** -0.5)
                    for i in range(PAIR):
                        e = u[:, lane(i)]
                        if dst is not v_ref:
                            e = e * cos + swap_halves(e) * sin
                        dst[0, rows, c + WIDE * i:c + WIDE * i + WIDE] = e.astype(BF)

    valid = lax.broadcasted_iota(jnp.int32, (1, SEQ), 1) < len_ref[seq]
    lanes = pl.ds(pl.multiple_of(j * WIDE, WIDE), WIDE)
    masks = [half_mask((SEQ, WIDE), 1, h) for h in range(PAIR)]
    ks = [jnp.where(m, k_ref[0, :, lanes], 0) for m in masks]
    vs = [jnp.where(m, v_ref[0, :, lanes], 0) for m in masks]
    chains = [(r, h) for r in blocks(SEQ) for h in range(PAIR)]

    def score(r, h):
        return dot(q_ref[0, pl.ds(r, BLOCK), lanes], ks[h], 1, 1)
    ahead, ctx = score(*chains[0]), 0
    for i, (r, h) in enumerate(chains):
        s = jnp.where(valid, ahead, NEG_BIG)
        if i + 1 < len(chains):
            ahead = score(*chains[i + 1])
        e = jnp.exp(s - jnp.max(s, axis=-1, keepdims=True))
        p = (e * (1.0 / jnp.sum(e, axis=-1, keepdims=True))).astype(BF)
        p_ref[0, h, pl.ds(r, BLOCK)] = p
        ctx = ctx + dot(p, vs[h]) if h else dot(p, vs[h])
        if h:
            ctx_ref[0, pl.ds(r, BLOCK), lanes] = ctx.astype(BF)

    @pl.when(j == QUAD - 1)
    def _():
        for r in blocks(SEQ):
            rows = pl.ds(r, BLOCK)
            x1_ref[0, rows] = (x_ref[0, rows].astype(F32) + dot(ctx_ref[0, rows], w_ref[BIAS_OUT]) + row(s_ref, BIAS_OUT)).astype(BF)

    for step, count in ((4, PAIR), (6, 1), (7, OCT)):
        @pl.when(t == step)
        def _():
            for gen in gens if step == 7 else gens[:PAIR]:
                for _ in range(count):
                    next(gen, 0)


def mlp_fwd_kernel(x_ref, w1_ref, w2_ref, s_ref, h_ref, a_ref, g_ref, *y_ref):
    x = x_ref[0].astype(F32)
    xhat, _ = normed(x)
    h = (xhat * row(s_ref, GAIN2) + row(s_ref, SHIFT2)).astype(BF)
    h_ref[0] = h
    acc = x + row(s_ref, BIAS_DOWN)
    for j in range(CHUNKS):
        cols = slice(CHUNK * j, CHUNK * j + CHUNK)
        pre = dot(h, w1_ref[:, cols]) + row(s_ref, BIAS_UP + j)
        cdf = 0.5 * (1.0 + lax.erf(pre * (1.0 / math.sqrt(2.0))))
        pdf = jnp.exp(-0.5 * pre * pre) * (1.0 / math.sqrt(2.0 * math.pi))
        g_ref[0, :, cols] = cdf + pre * pdf
        a = (pre * cdf).astype(BF)
        a_ref[0, :, cols] = a
        if y_ref:
            acc = acc + dot(a, w2_ref[cols, :])
    for ref in y_ref:
        ref[0] = acc.astype(BF)


def layer_small(layer):
    return pl.BlockSpec((None, SMALL, DIM), lambda *_: (layer, 0, 0))


def attn_fwd(layer, lengths, x, w, s, cos, sin, prev, late):
    seq = lambda t: (lax.div(t, QUAD), 0, 0)
    t = pl.BlockSpec((1, SEQ, DIM), seq)
    saved = [pl.BlockSpec((None, 1, SEQ, DIM), lambda t: (layer,) + seq(t))] * 6
    saved.append(pl.BlockSpec((None, 1, PAIR, SEQ, SEQ), lambda t: (layer, lax.div(t, QUAD), lax.rem(t, QUAD), 0, 0)))
    inputs = [lengths, x, w, s, cos, sin]
    n, m = len(inputs), len(prev)

    def body(*refs):
        attn_fwd_kernel(LATE[layer], *refs[:n], *refs[n + m + len(late):])
    res = pl.pallas_call(
        body, name='attn_fwd', grid=(OCT,),
        in_specs=[pl.BlockSpec(memory_space=pltpu.SMEM), t, whole((MATRICES, DIM, DIM)), layer_small(layer), whole((SEQ, WIDE)), whole((SEQ, WIDE))] + any_space(m + len(late)),
        out_specs=saved + any_space(len(late)),
        out_shape=[SD((LAYERS, SEQS, SEQ, DIM), BF)] * 6 + [SD((LAYERS, SEQS, HEADS, SEQ, SEQ), BF)] + [SD(e.shape, BF) for e in late],
        input_output_aliases=dict([(n + i, i) for i in range(m)] + [(n + m + i, len(saved) + i) for i in range(len(late))]),
        scratch_shapes=semaphores(40),
        compiler_params=pltpu.CompilerParams(collective_id=2 + layer, has_side_effects=True, vmem_limit_bytes=VM),
    )(*inputs, *prev, *late)
    return res[:len(saved)], res[len(saved):]


def mlp_fwd(layer, x1, w1, w2, s, prev):
    place = lambda t: (layer, lax.div(t, PAIR), lax.rem(t, PAIR), 0)
    block = lambda n: pl.BlockSpec((None, 1, BLOCK, n), place)
    widths = [(DIM, BF), (FFN, BF), (FFN, F32)]
    outs = [block(w) for w, _ in widths] + [pl.BlockSpec((1, BLOCK, DIM), lambda t: place(t)[1:])] * (1 - layer)
    shapes = [SD((LAYERS, SEQS, SEQ, w), d) for w, d in widths] + [SD((SEQS, SEQ, DIM), BF)] * (1 - layer)
    inputs = [x1, w1, w2, s]
    n, m = len(inputs), len(prev)
    return pl.pallas_call(
        lambda *refs: mlp_fwd_kernel(*refs[:n], *refs[n + m:]), name='mlp_fwd', grid=(QUAD,),
        in_specs=[block(DIM), whole((DIM, FFN)), whole((FFN, DIM)), layer_small(layer)] + any_space(m),
        out_specs=outs, out_shape=shapes,
        input_output_aliases={n + i: i for i in range(m)},
        compiler_params=pltpu.CompilerParams(vmem_limit_bytes=VM),
    )(*inputs, *prev)


def backward_kernel(dy, a, g, q, k, v, p, s, cos_ref, sin_ref, h2, x1, h1, ctx, x0, y0, w1_0, w1_1, w2_0, w2_1, wa_0, wa_1,
                    d_x, g_attn, g_up, g_down, gb_attn, g_ln, gb_up, gb_down, dx, dmid, dproj, dpre, acc, value, total, w1, w2, wa, h2s, h1s, late, *refs):
    credits, fetched, *sems = refs[-4:]
    t = pl.program_id(0)
    layer, r = 1 - lax.div(t, LAYER_STEPS), lax.rem(t, LAYER_STEPS)
    place = Place(*sems)
    me = place.me
    slots, refs = refs[:len(total_buffers())], refs[len(total_buffers()):-4]

    def finish_of(name, l):
        def finish(core, part):
            if name == 'down':
                for i in range(PAIR):
                    g_down[l, :, pl.ds(pl.multiple_of((PAIR * core + i) * WIDE, WIDE), WIDE)] = part[i]
            elif name == 'up':
                for i in range(OCT):
                    at = i // PAIR * QUAD + PAIR * core + i % PAIR
                    g_up[l, :, pl.ds(pl.multiple_of(at * WIDE, WIDE), WIDE)] = part[i]
            elif name == 'first':
                for i in range(QUAD):
                    g_attn[l, PAIR * core + i // PAIR, :, lane(i % PAIR)] = part[i // PAIR, i % PAIR]
            else:
                for i in range(PAIR):
                    g_attn[l, PAIR * core + (name == 'third'), :, lane(PAIR + i)] = part[i]
        return finish

    gens, grads = {}, {}
    for i, (name, kind, pieces) in enumerate(SETS):
        m = len(unit_buffers(kind, 1)) - QUAD
        shared, later, refs = refs[:QUAD], refs[QUAD:QUAD + LAYERS * m], refs[QUAD + LAYERS * m:]
        grads[name] = shared[0]
        axis = UNITS[kind][0]
        groups = [[('c', 1)], [(axis, e) for e in place.peers(axis)]]

        def give(which, groups=groups, i=i):
            for e in groups[which]:
                place.signal(credits.at[PAIR * i + which], *e)

        def take(which, groups=groups, i=i):
            pl.semaphore_wait(credits.at[PAIR * i + which], len(groups[which]))
        nothing = lambda which: None
        for l in (1, 0):
            gens[l, name] = reduce_unit(place, kind, [*shared, *later[m * l:m * l + m]], finish_of(name, l), pieces, give if l else nothing, nothing if l else take)

    loads = dict(w2=(w2_0, w2_1, w2), w1=(w1_0, w1_1, w1), h2=(h2.at[0], h2.at[1], h2s), x1=(x1.at[0], x1.at[1], late), h1=(h1.at[0], h1.at[1], h1s),
                 wa=(wa_0, wa_1, wa), ctx=(ctx.at[0], ctx.at[1], late), xin=(x0, y0, late))
    starts = {(1, 'w2'): 'A', (1, 'w1'): 'A', (1, 'h2'): 'A', (1, 'x1'): 'A', (1, 'h1'): 'B', (1, 'wa'): 'B', (1, 'ctx'): 'E', (1, 'xin'): 'I',
              (0, 'w2'): 'E', (0, 'w1'): 'E', (0, 'h2'): 'E', (0, 'x1'): 'M', (0, 'h1'): 'M', (0, 'wa'): 'M', (0, 'ctx'): 'Q', (0, 'xin'): 'U'}

    def load(name, l):
        return pltpu.make_async_copy(loads[name][l], loads[name][-1], fetched.at[list(loads).index(name)])

    @pl.when(t == 0)
    def _():
        place.greet()
        dx[...] = dy[...]
        value[...] = jnp.zeros_like(value)

    for step in range(STEPS):
        due = [key for key, letter in starts.items() if ord(letter) - ord('A') == step]
        if due:
            @pl.when(t == step)
            def _():
                for l, name in due:
                    load(name, l).start()

    def put(ref, where, part, shape):
        ref[where] = part.reshape(shape + TILE)

    def add_sums(rows, terms):
        for i, e in zip(rows, terms):
            value[layer, i:i + 1] += jnp.sum(e, axis=0, keepdims=True)

    @pl.when(r == 0)
    def _():
        for name in ('w2', 'w1', 'h2'):
            load(name, 0).wait()

    @pl.when(r < MLP_STEPS)
    def _():
        gw = dot(a[...], dx[...], 0, 0)
        for i in range(QUAD):
            put(grads['down'], (i // PAIR, pl.ds(PAIR * r, PAIR), ALL, ALL, ALL, i % PAIR), gw[:, lane(i)], (PAIR, QUAD, QUAD, CORES))
        chunk = pl.ds(pl.multiple_of(r * CHUNK, CHUNK), CHUNK)
        bias = jnp.zeros((1, DIM), F32)
        for e in blocks(TOKENS):
            rows = pl.ds(e, BLOCK)
            d = dot(dx[rows], w2[chunk], 1, 1) * g[rows]
            bias = bias + jnp.sum(d, axis=0, keepdims=True)
            dpre[rows] = d.astype(BF)
            part = dot(dpre[rows], w1[:, chunk], 1, 1)

            @pl.when(r == 0)
            def _():
                acc[rows] = part

            @pl.when(r > 0)
            def _():
                acc[rows] = acc[rows] + part
        value[layer, pl.ds(BIAS_UP + r, 1)] = bias
        gw = dot(h2s[...], dpre[...], 0, 0)
        for i in range(QUAD):
            put(grads['up'], (i // PAIR, ALL, ALL, ALL, PAIR * r + i % PAIR), gw[:, lane(i)], (OCT, QUAD, PAIR))

    @pl.when(r == MLP_STEPS - 1)
    def _():
        load('x1', 0).wait()
        for e in blocks(TOKENS):
            rows = pl.ds(e, BLOCK)
            dh = acc[rows]
            xhat, rstd = normed(late[rows].astype(F32))
            d = dx[rows].astype(F32)
            dmid[rows] = (d + norm_back(dh, row(s, GAIN2), xhat, rstd)).astype(BF)
            add_sums((BIAS_DOWN, GAIN2, SHIFT2, BIAS_OUT), (d, dh * xhat, dh, dmid[rows].astype(F32)))

    @pl.when(r == MLP_STEPS)
    def _():
        load('wa', 0).wait()

    @pl.when(r >= MLP_STEPS)
    def _():
        e = r - MLP_STEPS
        rows = pl.ds(pl.multiple_of(lax.rem(e, SEQS) * SEQ, SEQ), SEQ)
        lanes = pl.ds(pl.multiple_of(lax.div(e, SEQS) * WIDE, WIDE), WIDE)
        qv, kv, vv = q[...], k[...], v[...]
        dc = dot(dmid[rows], wa[BIAS_OUT, lanes], 1, 1).astype(BF)
        qt, dct = qv.T, dc.T
        dq, dkt, dvt = 0, 0, 0
        for h in range(PAIR):
            m = half_mask((SEQ, WIDE), 1, h)
            mt = half_mask((WIDE, SEQ), 0, h)
            kh, vh = jnp.where(m, kv, 0), jnp.where(m, vv, 0)
            dvt = dvt + dot(jnp.where(mt, dct, 0), p[h])
            ds = []
            for b in blocks(SEQ):
                pf = p[h, pl.ds(b, BLOCK)].astype(F32)
                dp = dot(dc[b:b + BLOCK], vh, 1, 1)
                ds.append((pf * (dp - jnp.sum(dp * pf, axis=-1, keepdims=True))).astype(BF))
            ds = jnp.concatenate(ds, axis=0)
            dq = dq + dot(ds, kh)
            dkt = dkt + dot(jnp.where(mt, qt, 0), ds)
        cos, sin = cos_ref[...], sin_ref[...]
        dk = dkt.T
        dproj[0, rows, lanes] = ((dq * cos - swap_halves(dq) * sin) * (HEAD_DIM ** -0.5)).astype(BF)
        dproj[1, rows, lanes] = (dk * cos - swap_halves(dk) * sin).astype(BF)
        dproj[PAIR, rows, lanes] = dvt.T.astype(BF)

    for which in range(PAIR):
        @pl.when(r == MLP_STEPS + ATTN_STEPS // PAIR * (1 + which) - 1)
        def _():
            if which == 0:
                load('h1', 0).wait()
                load('ctx', 0).wait()
                gw_out = dot(late[...], dmid[...], 0, 0)
                for j in range(QUAD):
                    name, at = (('third', (1, ALL, ALL, ALL, j % PAIR)) if j >= PAIR else ('first', (1, 1, ALL, ALL, ALL, j)))
                    put(grads[name], at, gw_out[:, lane(j)], (OCT, QUAD, PAIR))
            cols = slice(BLOCK * which, BLOCK * which + BLOCK)
            for i in range(MATRICES - 1):
                gw = dot(h1s[...], dproj[i, :, cols], 0, 0)
                for j in range(PAIR):
                    name, at = (('second', 'third')[i % PAIR], (i // PAIR,)) if which else ('first', (i // PAIR, i % PAIR))
                    put(grads[name], at + (ALL, ALL, ALL, j), gw[:, lane(j)], (OCT, QUAD, PAIR))

    def advance(when, cond):
        for l in (1, 0):
            due = [gens[l, name] for (n, name), letters in SCHEDULE.items() if n == l and when in letters]
            if due:
                @pl.when(cond)
                def _():
                    for gen in due:
                        next(gen, 0)

    for step in range(STEPS):
        advance(chr(ord('A') + step), t == step)

    def result(i):
        e = pl.ds(i * BLOCK, BLOCK)
        return pltpu.make_async_copy(dx.at[e], d_x.at[e], fetched.at[len(loads) + i])

    @pl.when(r == LAYER_STEPS - 1)
    def _():
        load('xin', 0).wait()
        for i, e in enumerate(blocks(TOKENS)):
            rows = pl.ds(e, BLOCK)
            parts = [dproj[j, rows] for j in range(MATRICES - 1)]
            dh = sum(dot(part, wa[j], 1, 1) for j, part in enumerate(parts))
            xhat, rstd = normed(late[rows].astype(F32))
            add_sums((0, 1, PAIR, GAIN1, SHIFT1), [part.astype(F32) for part in parts] + [dh * xhat, dh])
            dx[rows] = (dmid[rows].astype(F32) + norm_back(dh, row(s, GAIN1), xhat, rstd)).astype(BF)
            advance('abcd'[i], layer == 0)

    @pl.when(t == STEPS - 1)
    def _():
        for i in range(QUAD):
            result(i).start()
        left = {name[0]: gens[0, name] for name, _, _ in SETS}
        left['m'] = total_unit(place, value, total, slots)
        for letter in ENDING:
            next(left[letter], 0)
        run(left.values())
        index = ((me['z'] * SIZES['y'] + me['y']) * SIZES['x'] + me['x']) * CORES + me['c']
        lanes = lax.broadcasted_iota(jnp.int32, (QUAD, DIM), 1)
        flat = lanes + DIM * lax.broadcasted_iota(jnp.int32, (QUAD, DIM), 0)
        for l in range(LAYERS):
            for i in range(PAIR):
                here = lanes == PAIR * index + i
                pick = lambda e: jnp.sum(jnp.where(here[:e.shape[0]], e, 0.0), axis=-1, keepdims=True)
                gb_attn[l, :, i:i + 1] = pick(total[l, :GAIN1])
                g_ln[l, :, i:i + 1] = pick(total[l, GAIN1:BIAS_UP])
                gb_down[l:l + 1, i:i + 1] = pick(total[l, BIAS_DOWN:BIAS_DOWN + 1])
            for i in range(OCT):
                e = jnp.where(flat == OCT * index + i, total[l, BIAS_UP:BIAS_DOWN], 0.0)
                gb_up[l:l + 1, i:i + 1] = jnp.sum(jnp.sum(e, axis=0, keepdims=True), axis=-1, keepdims=True)
        for i in range(QUAD):
            result(i).wait()


def backward(dy, saved, x0, y0, wts, s, cos, sin):
    h1, q, k, v, ctx, x1, p, h2, a, g = saved
    once = dict(pipeline_mode=pl.Buffered(1))
    layer = lambda t: 1 - lax.div(t, LAYER_STEPS)
    chunk = lambda t: jnp.minimum(lax.rem(t, LAYER_STEPS), CHUNKS - 1)
    head_of = lambda t: jnp.maximum(lax.rem(t, LAYER_STEPS) - MLP_STEPS, 0)
    seq = lambda t: lax.rem(head_of(t), SEQS)
    pair = lambda t: lax.div(head_of(t), SEQS)
    flat = lambda e: e.reshape(*e.shape[:-3], TOKENS, e.shape[-1])
    cols = pl.BlockSpec((None, TOKENS, CHUNK), lambda t: (layer(t), 0, chunk(t)))
    head = pl.BlockSpec((None, None, SEQ, WIDE), lambda t: (layer(t), seq(t), 0, pair(t)))
    late = [flat(e) for e in (h2, x1, h1, ctx, x0, y0)] + [w for pair_of in wts for w in pair_of]
    act, small = pltpu.VMEM((TOKENS, DIM), BF), pltpu.VMEM((LAYERS, SMALL, DIM), F32)
    bufs = [e for _, kind, _ in SETS for e in unit_buffers(kind, LAYERS)]
    shapes = [(LAYERS, MATRICES, PAIR, DIM), (LAYERS, PAIR, FFN), (LAYERS, OCT, DIM), (LAYERS, QUAD, PAIR), (LAYERS, QUAD, PAIR), (LAYERS, OCT), (LAYERS, PAIR)]
    return pl.pallas_call(
        backward_kernel, name='backward', grid=(STEPS,),
        in_specs=[whole((TOKENS, DIM), **once), cols, cols, head, head, head,
                  pl.BlockSpec((None, None, PAIR, SEQ, SEQ), lambda t: (layer(t), seq(t), pair(t), 0, 0)),
                  pl.BlockSpec((None, SMALL, DIM), lambda t: (layer(t), 0, 0)), whole((SEQ, WIDE), **once), whole((SEQ, WIDE), **once)] + any_space(len(late)),
        out_specs=any_space(1) + in_vmem(len(shapes)),
        out_shape=[SD((TOKENS, DIM), BF)] + [SD(e, F32) for e in shapes],
        scratch_shapes=[act, act, pltpu.VMEM((MATRICES - 1, TOKENS, DIM), BF), act, pltpu.VMEM((TOKENS, DIM), F32), small, small,
                        pltpu.VMEM((DIM, FFN), BF), pltpu.VMEM((FFN, DIM), BF), pltpu.VMEM((MATRICES, DIM, DIM), BF), act, act, act]
        + total_buffers() + bufs + [pltpu.SemaphoreType.REGULAR((PAIR * len(SETS),)), pltpu.SemaphoreType.DMA((SMALL,))] + semaphores(200),
        compiler_params=pltpu.CompilerParams(collective_id=SMALL, has_side_effects=True, vmem_limit_bytes=67043328),
    )(flat(dy), flat(a), flat(g), q, k, v, p, s, cos, sin, *late)


def solution(mesh):
    grid = Mesh(mesh.devices.reshape([SIZES[a] for a in AXES]), AXES)
    first, second, third = P(AXES), P(None, AXES), P(None, None, AXES)
    weight_specs = (third, third, third, second, second, second, second)

    def device_step(x, lengths, d_y, w_attn, b_attn, ln_par, w_up, b_up, w_down, b_down):
        full, small = gather(w_attn, w_up, w_down, b_attn, ln_par, b_up, b_down)
        cos, sin = (jnp.asarray(t) for t in rotary_tables())
        attn_saved, mlp_saved, y, wts = [], [], x, {}
        for layer in range(LAYERS):
            inner = y
            late = sorted({g[:2] for g in LATE[layer]})
            wts['attn', layer] = natural('attn', full['attn', layer])
            attn_saved, done = attn_fwd(layer, lengths, inner, wts['attn', layer], small, cos, sin, attn_saved, [full[e] for e in late])
            full.update(zip(late, done))
            for kind in ('up', 'down'):
                wts[kind, layer] = natural(kind, full[kind, layer])
            *mlp_saved, y = list(mlp_fwd(layer, attn_saved[5], wts['up', layer], wts['down', layer], small, mlp_saved)) + [x] * layer
        by_layer = [[wts[kind, layer] for layer in range(LAYERS)] for kind in ('up', 'down', 'attn')]
        d_x, *grads = backward(d_y, list(attn_saved) + mlp_saved, x, inner, by_layer, small, cos, sin)
        g_attn, g_up, g_down, gb_attn, g_ln, gb_up, gb_down = grads
        return d_x.reshape(x.shape), g_attn, gb_attn, g_ln, g_up, gb_up, g_down, gb_down

    return jax.shard_map(device_step, mesh=grid, in_specs=(first,) * 3 + weight_specs, out_specs=(first,) + weight_specs, check_vma=False)
```

time: 4170 us -> 287 us (0.07)
  waiting for transfers between devices: 3130 us -> 0 us
  blocking collectives: 597 us -> 0 us
  Pallas kernels: 0 us -> 276 us
  matrix products: 192 us -> 0 us
  other arithmetic: 132 us -> 0 us
  local copies, waits for them, and re-layouts: 90.1 us -> 10.6 us
    reduce_scatter x2 -> x0, waiting for transfers between devices: 2400 us -> none  [scatter_grads(): reduce_rows(gw_down, scatter_dimension=0)]
    all_gather x6 -> x0, blocking collectives: 441 us -> none  [the longest x4 290 us: gather_layer(): lax.all_gather(ln_par, axis_name, axis=1, tiled=True)]
    all_gather x11 -> x0, waiting for transfers between devices: 419 us -> none  [the longest x4 178 us: gather_layer(): lax.all_gather(w_attn, axis_name, axis=1, tiled=True)]
    unnamed x15 -> x0, waiting for transfers between devices: 312 us -> none
    pallas_call x0 -> x6, Pallas kernels: none -> 276 us  [the longest x1 158 us: backward(): pl.pallas_call(backward_kernel, name='backward', grid=(STEPS,), in_specs=...]
    dot_general x33 -> x0, matrix products: 170 us -> none  [the longest x2 30.7 us: layer_backward(): jnp.einsum('blf,bld->fd', act_bf, d_out, preferred_element_type=jnp.float32)]
    unnamed x2 -> x0, blocking collectives: 156 us -> none
    convert_element_type x20 -> x0, other arithmetic: 85.1 us -> none  [the longest x1 20.7 us: layer_forward(): act_bf = jax.nn.gelu(pre_act, approximate=False).astype(jnp.bfloat16)]
  transfers between devices with their start and end apart: 14 -> 0, of which waited for: 8 -> 0; matrix products, arithmetic and copies ran while one was open for 8% -> 0% of each run, Pallas kernels for 0% -> 0%
where the time goes in v2:
time: 287 us
  Pallas kernels  276 us (96%)
  local copies, waits for them, and re-layouts  10.6 us (4%)
    pallas_call x1, Pallas kernels, backward(): pl.pallas_call(backward_kernel, name='backward', grid=(STEPS,), in_specs=...  158 us
    pallas_call x2, Pallas kernels, attn_fwd(): pl.pallas_call(body, name='attn_fwd', grid=(OCT,), in_specs=[pl.BlockSpec...  54.4 us
    pallas_call x1, Pallas kernels, gather(): pl.pallas_call(gather_kernel, name='gather', in_specs=in_vmem(len(shards)...  40.5 us
    pallas_call x2, Pallas kernels, mlp_fwd(): pl.pallas_call(lambda *refs: mlp_fwd_kernel(*refs[:n], *refs[n + m:]), na...  23.1 us
    unnamed x20, local copies, waits for them, and re-layouts  10.6 us

profile of v2, /device:TPU:1, one launch (start us, length us, event | category | flops | bytes accessed | tf_op | source)
XLA Modules:
  0.0 287.0 jit_solution(13567767205683048120)
XLA Ops:
  0.6 1.4 copy.35.b_attn
  2.0 1.4 copy.36.ln
  3.3 40.5 %gather.1 = (bf16[4,8,4,2,4,2,2,2,128]{8,7,6,5,4,3,2,1,0:T(2,128)(2,1)}, bf16[8,4,2,16,2,2,2,128]{7,6,5,4,3,2,1,0:T(2,128)(2,1)}, bf16[8,4,4,2,4,8,128]{6,5,4,3,...) custom-call(bf16[2,4,4,2,128]{4,3,2,1,0:T(2,128)(2,1)} %bitcast.71, ...), custom_call_target="tpu_custom_call" | custom-call | tf_op jit(solution)/shard_map/gather/pallas_call | solution.py:419
  43.9 31.2 %attn_fwd.2 = (bf16[2,2,512,512]{3,2,1,0:T(8,128)(2,1)}, bf16[2,2,512,512]{3,2,1,0:T(8,128)(2,1)}, bf16[2,2,512,512]{3,2,1,0:T(8,128)(2,1)}, bf16[2,2,512,512]{3...) custom-call(s32[2]{0:T(128)} %refs_0_.3, ...), custom_call_target="tpu_custom_call", output_to_operand_aliasing={{7}: (6, {}), {8}: (7, {}), {9}: (8, {})} | custom-call | tf_op jit(solution)/shard_map/attn_fwd/pallas_call | solution.py:533
  75.1 13.1 %mlp_fwd.2 = (bf16[2,2,512,512]{3,2,1,0:T(8,128)(2,1)}, bf16[2,2,512,2048]{3,2,1,0:T(8,128)(2,1)}, f32[2,2,512,2048]{3,2,1,0:T(8,128)}, bf16[2,512,512]{2,1,0:T(8,128)(2,1)}) custom-call(bf16[2,2,512,512]{3,2,1,0:T(8,128)(2,1)} %get-tuple-element.54.refs_0_.refs_11_, bf16[512,2048]{1,0:T(8,128)(2,1)} %bitcast.56, bf16[2048,512]{1,0:T(8,128)(2,1)} %bitcast.58, ...), custom_call_target="tpu_custom_call" | custom-call | tf_op jit(solution)/shard_map/mlp_fwd/pallas_call | solution.py:553
  88.1 23.2 %attn_fwd.3 = (bf16[2,2,512,512]{3,2,1,0:T(8,128)(2,1)}, bf16[2,2,512,512]{3,2,1,0:T(8,128)(2,1)}, bf16[2,2,512,512]{3,2,1,0:T(8,128)(2,1)}, bf16[2,2,512,512]{3...) custom-call(s32[2]{0:T(128)} %refs_0_.3, ...), custom_call_target="tpu_custom_call", output_to_operand_aliasing={{0}: (6, {}), {1}: (7, {}), {2}: (8, {}), {3}: (9, {}), {4}... | custom-call | tf_op jit(solution)/shard_map/attn_fwd/pallas_call | solution.py:533
  111.4 10.1 %mlp_fwd.3 = (bf16[2,2,512,512]{3,2,1,0:T(8,128)(2,1)}, bf16[2,2,512,2048]{3,2,1,0:T(8,128)(2,1)}, f32[2,2,512,2048]{3,2,1,0:T(8,128)}) custom-call(bf16[2,2,512,512]{3,2,1,0:T(8,128)(2,1)} %get-tuple-element.67.refs_0_, bf16[512,2048]{1,0:T(8,128)(2,1)} %bitcast.52, ...), custom_call_target="tpu_custom_call", output_to_operand_aliasing={{0}: (4, {}), {1}: (5, {}), {2}: (6, {})} | custom-call | tf_op jit(solution)/shard_map/mlp_fwd/pallas_call | solution.py:553
  121.5 157.5 %backward.1 = (bf16[1024,512]{1,0:T(8,128)(2,1)}, f32[2,4,2,512]{3,2,1,0:T(2,128)}, f32[2,2,2048]{2,1,0:T(2,128)}, f32[2,8,512]{2,1,0:T(8,128)}, f32[2,4,2]{2,1,...) custom-call(bf16[1024,512]{1,0:T(8,128)(2,1)} %bitcast.70, bf16[2,1024,2048]{2,1,0:T(8,128)(2,1)} %bitcast.50, ...), custom_call_target="tpu_custom_call" | custom-call | tf_op jit(solution)/shard_map/backward/pallas_call | solution.py:795
  279.0 0.0 copy-start.2
  279.0 0.0 copy-start.1
  279.0 0.0 copy-start.4
  279.0 0.0 copy-start
  279.1 0.0 copy-start.3
  279.1 1.4 copy.37
  280.4 1.3 copy.38
  281.8 2.3 copy.60
  284.0 0.0 copy-done.2
  284.0 0.6 copy.61
  284.6 0.0 copy-done.1
  284.6 0.6 copy.62
  285.2 0.0 copy-done.4
  285.3 0.6 copy.63
  285.8 0.0 copy-done
  285.8 0.6 copy.64
  286.4 0.0 copy-done.3
  286.4 0.6 copy.65
Async XLA Ops:
  279.0 5.0 %copy-start.2 = (f32[2,4,2,512]{3,2,1,0:T(2,128)S(1)}, f32[2,4,2,512]{3,2,1,0:T(2,128)}, u32[]{:S(2)}) copy-start(f32[2,4,2,512]{3,2,1,0:T(2,128)} %get-tuple-element.107) | copy-start | bytes 98308
  279.0 5.6 %copy-start.1 = (f32[2,2,2048]{2,1,0:T(2,128)S(1)}, f32[2,2,2048]{2,1,0:T(2,128)}, u32[]{:S(2)}) copy-start(f32[2,2,2048]{2,1,0:T(2,128)} %get-tuple-element.110) | copy-start | bytes 98308
  279.0 6.2 %copy-start.4 = (f32[2,8]{1,0:T(2,128)S(1)}, f32[2,8]{1,0:T(2,128)}, u32[]{:S(2)}) copy-start(f32[2,8]{1,0:T(2,128)} %get-tuple-element.111) | copy-start | bytes 196
  279.0 6.8 %copy-start = (f32[2,8,512]{2,1,0:T(8,128)S(1)}, f32[2,8,512]{2,1,0:T(8,128)}, u32[]{:S(2)}) copy-start(f32[2,8,512]{2,1,0:T(8,128)} %get-tuple-element.112) | copy-start | bytes 98308
  279.1 7.4 %copy-start.3 = (f32[2,2]{1,0:T(2,128)S(1)}, f32[2,2]{1,0:T(2,128)}, u32[]{:S(2)}) copy-start(f32[2,2]{1,0:T(2,128)} %get-tuple-element.113) | copy-start | bytes 52

commit v3 on v2

--- a/solution.py
+++ b/solution.py
@@ -24,14 +24,14 @@
 FINE = dict(attn='kzyhtlcr', up='zyhtlcr', down='zyxct')
 LANE_TILES = dict(attn=QUAD, part=PAIR, slim=PAIR, pair=PAIR, up=OCT, down=PAIR)
 OWNER = dict(x='xhl', y='y', z='z')
-UNITS = dict(up='yzx', down='xyz', part='hyzl', slim='yzx', pair='hyzl')
+UNITS = dict(up=('yzx', 'yzx'), down=('xyz', 'xyz'), part=('hyzl', 'hzyl'), slim=('yzx', 'yzx'), pair=('hyzl', 'hzyl'))
 MLP_STEPS, ATTN_STEPS = CHUNKS, 8
 LAYER_STEPS = MLP_STEPS + ATTN_STEPS
 STEPS = LAYERS * LAYER_STEPS
 SETS = (('up', 'up', ('t', PAIR, CHUNKS)), ('down', 'down', ('z', PAIR, CHUNKS)), ('first', 'part', ('z', OCT, 1)), ('second', 'slim', ('z', OCT, 1)), ('third', 'pair', ('z', OCT, 1)))
-SCHEDULE = {(1, 'up'): 'ABCDEKNOP', (1, 'down'): 'ABCDEKNOP', (1, 'first'): 'HLNOPTU', (1, 'second'): 'LMPQSV', (1, 'third'): 'LMPQSTV',
-            (0, 'up'): 'MNOPQVcd', (0, 'down'): 'MNOPQVcd', (0, 'first'): 'TUX', (0, 'second'): 'Xa', (0, 'third'): 'Xa'}
-ENDING = 'mstfmudstfmstfmstftmm'
+SCHEDULE = {(1, 'small'): 'MNOPST', (1, 'second'): 'LMQUXb', (1, 'third'): 'LMPTWac', (1, 'first'): 'HJNSUWX', (1, 'up'): 'ABCDEJNQU', (1, 'down'): 'ABCDEJMOP',
+            (0, 'up'): 'MNOPQVb', (0, 'down'): 'MNOPQVXc', (0, 'first'): 'TVb', (0, 'second'): 'Xa', (0, 'third'): 'Xa'}
+ENDING = 'lsdltufsldtsfltsftlft'
 VM = 56 << 20
 
 
@@ -195,8 +195,8 @@
     wait()
 
 
-def total_buffers():
-    return [pltpu.VMEM((SMALL, DIM), F32)] + [pltpu.VMEM((SIZES[a], SMALL, DIM), F32) for a in 'cxyz']
+def total_buffers(n):
+    return [pltpu.VMEM((n, DIM), F32)] + [pltpu.VMEM((SIZES[a], n, DIM), F32) for a in 'cxyz']
 
 
 def run(units):
@@ -209,31 +209,34 @@
     return tuple(LANE_TILES[kind] if n == 't' else SIZES[n] for n in names) + TILE
 
 
-def plan(kind):
+def plan(kind, layer=0):
     left = TILED[kind]
-    for axis in UNITS[kind]:
+    for axis in UNITS[kind][layer]:
         d = axis if axis in left else 'h' if axis == 'x' else ''
         left = left.replace(d, '')
         yield axis, d, left
 
 
-def unit_buffers(kind, layers):
-    slots = [pltpu.VMEM((SIZES[axis] - 1,) + free_sizes(kind, left), F32) for axis, _, left in plan(kind)]
-    *_, (_, _, left) = plan(kind)
+def unit_buffers(kind):
     _, _, first = next(plan(kind))
     shapes = [(PAIR,) + free_sizes(kind, TILED[kind]), free_sizes(kind, TILED[kind]), free_sizes(kind, first)]
-    return [pltpu.VMEM(s, F32) for s in shapes] + slots[:1] + (slots[1:] + [pltpu.VMEM(free_sizes(kind, left.replace('c', '')), F32)]) * layers
-
-
-def reduce_unit(place, kind, bufs, finish, pieces, give, take):
+    later = []
+    for layer in range(LAYERS):
+        slots = [(SIZES[axis] - 1,) + free_sizes(kind, left) for axis, _, left in plan(kind, layer)]
+        *_, (_, _, left) = plan(kind, layer)
+        later.append([pltpu.VMEM(s, F32) for s in slots[1:] + [free_sizes(kind, left.replace('c', ''))]])
+    return [pltpu.VMEM(s, F32) for s in shapes + slots[:1]], later
+
+
+def reduce_unit(place, kind, layer, bufs, finish, pieces, give, take):
     grad, got, first, slots, *rest = bufs
     me = place.me
     whole_grad, whole_names = grad, 'g' + TILED[kind]
     names, pick = whole_names, dict(g=me['c'])
     dim, size, count = pieces
 
-    def cut(i, n=1):
-        return {dim: pl.ds(size * i, size * n)}
+    def cut(i):
+        return {dim: pl.ds(size * i, size)}
 
     def accumulate(terms, fixed, into, piece=None):
         left = [n for n in names if n not in fixed]
@@ -257,25 +260,24 @@
         else:
             body(())
 
-    (axis, d, left), *later = plan(kind)
+    (axis, d, left), *later = plan(kind, layer)
     arrived, waits = [], []
 
-    def begin(start, n):
-        if not waits:
+    def begin(i):
+        if i == 0:
             take(1)
-        for i in range(start, start + n):
-            arrived[i]()
-            accumulate([got], pick, grad, i)
+        arrived[i]()
+        accumulate([got], pick, grad, i)
         for s in place.peers(axis):
-            waits.append(place.copy(axis, s, lambda s=s: (view(whole_grad, whole_names, dict(only(place.shifted(axis, s), d), g=me['c'], **cut(start, n))),
-                                                          view(slots, 's' + TILED[kind].replace(d, ''), dict(cut(start, n), s=s - 1)))))
+            waits.append(place.copy(axis, s, lambda s=s: (view(whole_grad, whole_names, dict(only(place.shifted(axis, s), d), g=me['c'], **cut(i))),
+                                                          view(slots, 's' + TILED[kind].replace(d, ''), dict(cut(i), s=s - 1)))))
     take(0)
     for i in range(count):
         arrived.append(place.copy('c', 1, lambda i=i: (view(whole_grad, whole_names, dict(cut(i), g=other(me))), view(got, TILED[kind], cut(i)))))
-        if i and count == PAIR * i:
-            begin(0, i)
+        if i:
+            begin(i - 1)
         yield
-    begin(count // PAIR, count - count // PAIR)
+    begin(count - 1)
     give(0)
     yield
     for w in waits:
@@ -381,18 +383,55 @@
     return tuple(dims[d] for d in FINE[kind]) + ((WIDE,) if 'r' in FINE[kind] else TILE)
 
 
-GATHERS = (('attn', 0, 0, 'zxy'), ('attn', 0, 1, 'zyx'), ('up', 0, 0, 'zxy'), ('down', 0, 0, 'zyx'),
-           ('attn', 1, 0, 'zxy'), ('attn', 1, 1, 'zyx'), ('up', 1, 0, 'zxy'), ('down', 1, 0, 'zyx'))
-LATE = (GATHERS[2:6], GATHERS[6:])
+ATTN0, ATTN1 = ((('attn', l, 0, 'zxy'), ('attn', l, 1, 'zyx')) for l in range(LAYERS))
+MLP0, MLP1 = ((('up', l, 0, 'zxy'), ('down', l, 0, 'zyx')) for l in range(LAYERS))
+JOBS = dict(gather=[(gather_whole, g) for g in ATTN0] + [(gather_early, g) for g in MLP0 + ATTN1 + MLP1],
+            attn0=[(gather_late, g) for g in MLP0 + ATTN1], attn1=[(gather_late, g) for g in MLP1])
+HOST_STEPS = dict(attn0=((5, '0101'), (6, '01')), attn1=((5, '0101'), (6, '01')))
 KINDS = tuple(FINE)
 
 
+def keys(name):
+    return sorted({g[:2] for _, g in JOBS[name]})
+
+
+def units_of(name, place, full, shards):
+    units = []
+    for make, (kind, layer, part, order) in JOBS[name]:
+        args = [place, kind, part, order, full[kind, layer]]
+        units.append(make(*args) if make is gather_late else make(*args, shards[kind, layer]))
+    return units
+
+
+def host(name, place, t, full, shards):
+    units = []
+
+    @pl.when(t == 0)
+    def _():
+        place.greet()
+        units.extend(units_of(name, place, full, shards))
+        for u in units:
+            next(u)
+
+    def proceed():
+        for step, digits in HOST_STEPS[name]:
+            @pl.when(t == step)
+            def _():
+                for i in digits:
+                    next(units[int(i)], 0)
+
+        @pl.when(t == pl.num_programs(0) - 1)
+        def _():
+            run(units)
+    return proceed
+
+
 def gather_kernel(sa, su, sd, b_attn, ln, b_up, b_down, *refs):
-    n = LAYERS * len(KINDS)
+    n = len(keys('gather'))
     full, total, value, slots, sems = refs[:n], refs[n], refs[n + 1], refs[n + 2:-2], refs[-2:]
     place = Place(*sems)
     place.greet()
-    shards, full = dict(zip(KINDS, (sa, su, sd))), dict(zip([(k, l) for l in range(LAYERS) for k in KINDS], full))
+    shards = {(kind, l): ref.at[l] for kind, ref in zip(KINDS, (sa, su, sd)) for l in range(LAYERS)}
     me = place.me
     index = ((me['z'] * SIZES['y'] + me['y']) * SIZES['x'] + me['x']) * CORES + me['c']
 
@@ -403,43 +442,40 @@
             at = at + DIM * lax.broadcasted_iota(jnp.int32, (rows, DIM), 0)
         return sum(jnp.where(at == i, v[:, i:i + 1], 0.0) for i in range(n))
     value[...] = jnp.zeros_like(value)
+    shape = (PAIR, DIM)
+    two = (lax.broadcasted_iota(jnp.int32, shape, 1) == PAIR * index + lax.broadcasted_iota(jnp.int32, shape, 0)).astype(F32).astype(BF)
     for l in range(LAYERS):
-        value[l, :GAIN1] = spread(b_attn[l].astype(F32), QUAD)
-        value[l, GAIN1:BIAS_UP] = spread(ln[l].astype(F32), QUAD)
+        value[l, :GAIN1] = dot(b_attn[l], two, 0, 0)
+        value[l, GAIN1:BIAS_UP] = dot(ln[l], two, 0, 0)
         value[l, BIAS_UP:BIAS_DOWN] = spread(b_up[l:l + 1].astype(F32), QUAD)
         value[l, BIAS_DOWN:BIAS_DOWN + 1] = spread(b_down[l:l + 1].astype(F32), 1)
-    units = [(gather_early if g in sum(LATE, ()) else gather_whole)(place, g[0], *g[2:], full[g[:2]], shards[g[0]].at[g[1]]) for g in GATHERS]
-    run([units[0], units[1], total_unit(place, value, total, slots)] + units[2:])
-
-
-def gather(attn, up, down, *small):
-    shards = [attn.reshape(LAYERS, MATRICES, PAIR, -1, WIDE).swapaxes(-3, -2), up.reshape(LAYERS, PAIR, -1, WIDE).swapaxes(-3, -2),
-              down.reshape(LAYERS, OCT, -1, WIDE).swapaxes(-3, -2)]
-    keys = [(k, l) for l in range(LAYERS) for k in KINDS]
+    units = units_of('gather', place, dict(zip(keys('gather'), full)), shards)
+    units.insert(PAIR, total_unit(place, value, total, slots))
+    run(units)
+
+
+def tiled_shards(attn, up, down):
+    return (attn.reshape(LAYERS, MATRICES, PAIR, -1, WIDE).swapaxes(-3, -2), up.reshape(LAYERS, PAIR, -1, WIDE).swapaxes(-3, -2),
+            down.reshape(LAYERS, OCT, -1, WIDE).swapaxes(-3, -2))
+
+
+def gather(shards, *small):
+    names = keys('gather')
     *full, total = pl.pallas_call(
         gather_kernel, name='gather',
-        in_specs=in_vmem(len(shards) + len(small)), out_specs=any_space(len(keys)) + in_vmem(1),
-        out_shape=[SD(fine_shape(k), BF) for k, _ in keys] + [SD((LAYERS, SMALL, DIM), F32)],
-        scratch_shapes=[pltpu.VMEM((LAYERS, SMALL, DIM), F32)] + total_buffers() + semaphores(200),
+        in_specs=in_vmem(len(shards) + len(small)), out_specs=any_space(len(names)) + in_vmem(1),
+        out_shape=[SD(fine_shape(k), BF) for k, _ in names] + [SD((LAYERS, SMALL, DIM), F32)],
+        scratch_shapes=[pltpu.VMEM((LAYERS, SMALL, DIM), F32)] + total_buffers(SMALL) + semaphores(200),
         compiler_params=pltpu.CompilerParams(collective_id=1, has_side_effects=True),
     )(*shards, *small)
-    return dict(zip(keys, full)), total
-
-
-def attn_fwd_kernel(late, len_ref, x_ref, w_ref, s_ref, cos_ref, sin_ref, *refs):
+    return dict(zip(names, full)), total
+
+
+def attn_fwd_kernel(name, len_ref, x_ref, w_ref, s_ref, cos_ref, sin_ref, *refs):
     h_ref, q_ref, k_ref, v_ref, ctx_ref, x1_ref, p_ref, *full = refs[:-2]
     t = pl.program_id(0)
     seq, j = lax.div(t, QUAD), lax.rem(t, QUAD)
-    place = Place(*refs[-2:])
-    full = dict(zip(sorted({g[:2] for g in late}), full))
-    gens = []
-
-    @pl.when(t == 0)
-    def _():
-        place.greet()
-        for g in late:
-            gens.append(gather_late(place, g[0], *g[2:], full[g[:2]]))
-            next(gens[-1])
+    proceed = host(name, Place(*refs[-2:]), t, dict(zip(keys(name), full)), {})
 
     @pl.when(j == 0)
     def _():
@@ -488,12 +524,7 @@
             rows = pl.ds(r, BLOCK)
             x1_ref[0, rows] = (x_ref[0, rows].astype(F32) + dot(ctx_ref[0, rows], w_ref[BIAS_OUT]) + row(s_ref, BIAS_OUT)).astype(BF)
 
-    for step, count in ((4, PAIR), (6, 1), (7, OCT)):
-        @pl.when(t == step)
-        def _():
-            for gen in gens if step == 7 else gens[:PAIR]:
-                for _ in range(count):
-                    next(gen, 0)
+    proceed()
 
 
 def mlp_fwd_kernel(x_ref, w1_ref, w2_ref, s_ref, h_ref, a_ref, g_ref, *y_ref):
@@ -505,9 +536,9 @@
     for j in range(CHUNKS):
         cols = slice(CHUNK * j, CHUNK * j + CHUNK)
         pre = dot(h, w1_ref[:, cols]) + row(s_ref, BIAS_UP + j)
-        cdf = 0.5 * (1.0 + lax.erf(pre * (1.0 / math.sqrt(2.0))))
-        pdf = jnp.exp(-0.5 * pre * pre) * (1.0 / math.sqrt(2.0 * math.pi))
-        g_ref[0, :, cols] = cdf + pre * pdf
+        z = pre * math.sqrt(0.5)
+        cdf = 0.5 + 0.5 * lax.erf(z)
+        g_ref[0, :, cols] = cdf + pre * math.sqrt(0.5 / math.pi) * jnp.exp2(z * z * -math.log2(math.e))
         a = (pre * cdf).astype(BF)
         a_ref[0, :, cols] = a
         if y_ref:
@@ -527,17 +558,14 @@
     saved.append(pl.BlockSpec((None, 1, PAIR, SEQ, SEQ), lambda t: (layer, lax.div(t, QUAD), lax.rem(t, QUAD), 0, 0)))
     inputs = [lengths, x, w, s, cos, sin]
     n, m = len(inputs), len(prev)
-
-    def body(*refs):
-        attn_fwd_kernel(LATE[layer], *refs[:n], *refs[n + m + len(late):])
     res = pl.pallas_call(
-        body, name='attn_fwd', grid=(OCT,),
+        lambda *refs: attn_fwd_kernel('attn%d' % layer, *refs[:n], *refs[n + m + len(late):]), name='attn_fwd', grid=(OCT,),
         in_specs=[pl.BlockSpec(memory_space=pltpu.SMEM), t, whole((MATRICES, DIM, DIM)), layer_small(layer), whole((SEQ, WIDE)), whole((SEQ, WIDE))] + any_space(m + len(late)),
         out_specs=saved + any_space(len(late)),
         out_shape=[SD((LAYERS, SEQS, SEQ, DIM), BF)] * 6 + [SD((LAYERS, SEQS, HEADS, SEQ, SEQ), BF)] + [SD(e.shape, BF) for e in late],
         input_output_aliases=dict([(n + i, i) for i in range(m)] + [(n + m + i, len(saved) + i) for i in range(len(late))]),
         scratch_shapes=semaphores(40),
-        compiler_params=pltpu.CompilerParams(collective_id=2 + layer, has_side_effects=True, vmem_limit_bytes=VM),
+        compiler_params=pltpu.CompilerParams(collective_id=PAIR + layer, has_side_effects=True, vmem_limit_bytes=VM),
     )(*inputs, *prev, *late)
     return res[:len(saved)], res[len(saved):]
 
@@ -547,13 +575,12 @@
     block = lambda n: pl.BlockSpec((None, 1, BLOCK, n), place)
     widths = [(DIM, BF), (FFN, BF), (FFN, F32)]
     outs = [block(w) for w, _ in widths] + [pl.BlockSpec((1, BLOCK, DIM), lambda t: place(t)[1:])] * (1 - layer)
-    shapes = [SD((LAYERS, SEQS, SEQ, w), d) for w, d in widths] + [SD((SEQS, SEQ, DIM), BF)] * (1 - layer)
     inputs = [x1, w1, w2, s]
     n, m = len(inputs), len(prev)
     return pl.pallas_call(
         lambda *refs: mlp_fwd_kernel(*refs[:n], *refs[n + m:]), name='mlp_fwd', grid=(QUAD,),
-        in_specs=[block(DIM), whole((DIM, FFN)), whole((FFN, DIM)), layer_small(layer)] + any_space(m),
-        out_specs=outs, out_shape=shapes,
+        in_specs=[block(DIM), whole((DIM, FFN)), whole((FFN, DIM)), layer_small(layer)] + any_space(m), out_specs=outs,
+        out_shape=[SD((LAYERS, SEQS, SEQ, w), d) for w, d in widths] + [SD((SEQS, SEQ, DIM), BF)] * (1 - layer),
         input_output_aliases={n + i: i for i in range(m)},
         compiler_params=pltpu.CompilerParams(vmem_limit_bytes=VM),
     )(*inputs, *prev)
@@ -566,7 +593,8 @@
     layer, r = 1 - lax.div(t, LAYER_STEPS), lax.rem(t, LAYER_STEPS)
     place = Place(*sems)
     me = place.me
-    slots, refs = refs[:len(total_buffers())], refs[len(total_buffers()):-4]
+    n = len(total_buffers(1))
+    slots, last_slots, refs = refs[:n], refs[n:n + n], refs[n + n:-4]
 
     def finish_of(name, l):
         def finish(core, part):
@@ -585,12 +613,13 @@
                     g_attn[l, PAIR * core + (name == 'third'), :, lane(PAIR + i)] = part[i]
         return finish
 
-    gens, grads = {}, {}
+    gens, grads = {(1, 'small'): total_unit(place, value.at[1], total.at[1], slots)}, {}
     for i, (name, kind, pieces) in enumerate(SETS):
-        m = len(unit_buffers(kind, 1)) - QUAD
-        shared, later, refs = refs[:QUAD], refs[QUAD:QUAD + LAYERS * m], refs[QUAD + LAYERS * m:]
+        shared, refs = refs[:QUAD], refs[QUAD:]
+        m = len(unit_buffers(kind)[1][0])
+        later, refs = (refs[:m], refs[m:m + m]), refs[m + m:]
         grads[name] = shared[0]
-        axis = UNITS[kind][0]
+        axis = UNITS[kind][0][0]
         groups = [[('c', 1)], [(axis, e) for e in place.peers(axis)]]
 
         def give(which, groups=groups, i=i):
@@ -601,7 +630,7 @@
             pl.semaphore_wait(credits.at[PAIR * i + which], len(groups[which]))
         nothing = lambda which: None
         for l in (1, 0):
-            gens[l, name] = reduce_unit(place, kind, [*shared, *later[m * l:m * l + m]], finish_of(name, l), pieces, give if l else nothing, nothing if l else take)
+            gens[l, name] = reduce_unit(place, kind, l, [*shared, *later[l]], finish_of(name, l), pieces, give if l else nothing, nothing if l else take)
 
     loads = dict(w2=(w2_0, w2_1, w2), w1=(w1_0, w1_1, w1), h2=(h2.at[0], h2.at[1], h2s), x1=(x1.at[0], x1.at[1], late), h1=(h1.at[0], h1.at[1], h1s),
                  wa=(wa_0, wa_1, wa), ctx=(ctx.at[0], ctx.at[1], late), xin=(x0, y0, late))
@@ -630,7 +659,7 @@
 
     def add_sums(rows, terms):
         for i, e in zip(rows, terms):
-            value[layer, i:i + 1] += jnp.sum(e, axis=0, keepdims=True)
+            value[layer, i // OCT, i % OCT:i % OCT + 1] += jnp.sum(e, axis=0, keepdims=True)
 
     @pl.when(r == 0)
     def _():
@@ -658,7 +687,7 @@
             @pl.when(r > 0)
             def _():
                 acc[rows] = acc[rows] + part
-        value[layer, pl.ds(BIAS_UP + r, 1)] = bias
+        value[layer, 1, pl.ds(r, 1)] = bias
         gw = dot(h2s[...], dpre[...], 0, 0)
         for i in range(QUAD):
             put(grads['up'], (i // PAIR, ALL, ALL, ALL, PAIR * r + i % PAIR), gw[:, lane(i)], (OCT, QUAD, PAIR))
@@ -724,13 +753,12 @@
                     put(grads[name], at + (ALL, ALL, ALL, j), gw[:, lane(j)], (OCT, QUAD, PAIR))
 
     def advance(when, cond):
-        for l in (1, 0):
-            due = [gens[l, name] for (n, name), letters in SCHEDULE.items() if n == l and when in letters]
-            if due:
-                @pl.when(cond)
-                def _():
-                    for gen in due:
-                        next(gen, 0)
+        due = [gens[key] for key, letters in SCHEDULE.items() if when in letters]
+        if due:
+            @pl.when(cond)
+            def _():
+                for gen in due:
+                    next(gen, 0)
 
     for step in range(STEPS):
         advance(chr(ord('A') + step), t == step)
@@ -756,23 +784,24 @@
         for i in range(QUAD):
             result(i).start()
         left = {name[0]: gens[0, name] for name, _, _ in SETS}
-        left['m'] = total_unit(place, value, total, slots)
+        left['l'] = total_unit(place, value.at[0], total.at[0], last_slots)
         for letter in ENDING:
             next(left[letter], 0)
         run(left.values())
         index = ((me['z'] * SIZES['y'] + me['y']) * SIZES['x'] + me['x']) * CORES + me['c']
-        lanes = lax.broadcasted_iota(jnp.int32, (QUAD, DIM), 1)
-        flat = lanes + DIM * lax.broadcasted_iota(jnp.int32, (QUAD, DIM), 0)
+        shape = (OCT, DIM)
+        lanes, rows = lax.broadcasted_iota(jnp.int32, shape, 1), lax.broadcasted_iota(jnp.int32, shape, 0)
+        diagonal = lax.broadcasted_iota(jnp.int32, (OCT, OCT), 0) == lax.broadcasted_iota(jnp.int32, (OCT, OCT), 1)
+
+        def across(e):
+            return jnp.sum(jnp.where(diagonal, jnp.sum(e, axis=-1, keepdims=True), 0.0), axis=0, keepdims=True)
         for l in range(LAYERS):
             for i in range(PAIR):
                 here = lanes == PAIR * index + i
-                pick = lambda e: jnp.sum(jnp.where(here[:e.shape[0]], e, 0.0), axis=-1, keepdims=True)
-                gb_attn[l, :, i:i + 1] = pick(total[l, :GAIN1])
-                g_ln[l, :, i:i + 1] = pick(total[l, GAIN1:BIAS_UP])
-                gb_down[l:l + 1, i:i + 1] = pick(total[l, BIAS_DOWN:BIAS_DOWN + 1])
-            for i in range(OCT):
-                e = jnp.where(flat == OCT * index + i, total[l, BIAS_UP:BIAS_DOWN], 0.0)
-                gb_up[l:l + 1, i:i + 1] = jnp.sum(jnp.sum(e, axis=0, keepdims=True), axis=-1, keepdims=True)
+                e = across(jnp.where(here, total[l, 0], 0.0))
+                gb_attn[l, i:i + 1], g_ln[l, i:i + 1] = e[:, :QUAD], e[:, QUAD:]
+                gb_down[l:l + 1, i:i + 1] = across(jnp.where(here, total[l, 1], 0.0))[:, QUAD:QUAD + 1]
+            gb_up[l:l + 1] = across(sum(jnp.where(lanes + DIM * n == OCT * index + rows, total[l, 1, n:n + 1], 0.0) for n in range(QUAD)))
         for i in range(QUAD):
             result(i).wait()
 
@@ -789,9 +818,9 @@
     cols = pl.BlockSpec((None, TOKENS, CHUNK), lambda t: (layer(t), 0, chunk(t)))
     head = pl.BlockSpec((None, None, SEQ, WIDE), lambda t: (layer(t), seq(t), 0, pair(t)))
     late = [flat(e) for e in (h2, x1, h1, ctx, x0, y0)] + [w for pair_of in wts for w in pair_of]
-    act, small = pltpu.VMEM((TOKENS, DIM), BF), pltpu.VMEM((LAYERS, SMALL, DIM), F32)
-    bufs = [e for _, kind, _ in SETS for e in unit_buffers(kind, LAYERS)]
-    shapes = [(LAYERS, MATRICES, PAIR, DIM), (LAYERS, PAIR, FFN), (LAYERS, OCT, DIM), (LAYERS, QUAD, PAIR), (LAYERS, QUAD, PAIR), (LAYERS, OCT), (LAYERS, PAIR)]
+    act, small = pltpu.VMEM((TOKENS, DIM), BF), pltpu.VMEM((LAYERS, CORES, OCT, DIM), F32)
+    bufs = [e for _, kind, _ in SETS for group in (unit_buffers(kind)[0], *unit_buffers(kind)[1]) for e in group]
+    shapes = [(LAYERS, MATRICES, PAIR, DIM), (LAYERS, PAIR, FFN), (LAYERS, OCT, DIM), (LAYERS, PAIR, QUAD), (LAYERS, PAIR, QUAD), (LAYERS, OCT), (LAYERS, PAIR)]
     return pl.pallas_call(
         backward_kernel, name='backward', grid=(STEPS,),
         in_specs=[whole((TOKENS, DIM), **once), cols, cols, head, head, head,
@@ -801,9 +830,18 @@
         out_shape=[SD((TOKENS, DIM), BF)] + [SD(e, F32) for e in shapes],
         scratch_shapes=[act, act, pltpu.VMEM((MATRICES - 1, TOKENS, DIM), BF), act, pltpu.VMEM((TOKENS, DIM), F32), small, small,
                         pltpu.VMEM((DIM, FFN), BF), pltpu.VMEM((FFN, DIM), BF), pltpu.VMEM((MATRICES, DIM, DIM), BF), act, act, act]
-        + total_buffers() + bufs + [pltpu.SemaphoreType.REGULAR((PAIR * len(SETS),)), pltpu.SemaphoreType.DMA((SMALL,))] + semaphores(200),
+        + total_buffers(OCT) * LAYERS + bufs + [pltpu.SemaphoreType.REGULAR((PAIR * len(SETS),)), pltpu.SemaphoreType.DMA((SMALL,))] + semaphores(240),
         compiler_params=pltpu.CompilerParams(collective_id=SMALL, has_side_effects=True, vmem_limit_bytes=67043328),
     )(flat(dy), flat(a), flat(g), q, k, v, p, s, cos, sin, *late)
+
+
+def deliver(*results):
+    n = len(results)
+
+    def body(*refs):
+        for src, dst in zip(refs[:n], refs[n:]):
+            dst[...] = src[...]
+    return pl.pallas_call(body, name='deliver', in_specs=in_vmem(n), out_specs=in_vmem(n), out_shape=[SD(e.shape, e.dtype) for e in results])(*results)
 
 
 def solution(mesh):
@@ -812,12 +850,13 @@
     weight_specs = (third, third, third, second, second, second, second)
 
     def device_step(x, lengths, d_y, w_attn, b_attn, ln_par, w_up, b_up, w_down, b_down):
-        full, small = gather(w_attn, w_up, w_down, b_attn, ln_par, b_up, b_down)
+        shards = tiled_shards(w_attn, w_up, w_down)
+        full, small = gather(shards, b_attn.swapaxes(1, PAIR), ln_par.swapaxes(1, PAIR), b_up, b_down)
         cos, sin = (jnp.asarray(t) for t in rotary_tables())
         attn_saved, mlp_saved, y, wts = [], [], x, {}
         for layer in range(LAYERS):
             inner = y
-            late = sorted({g[:2] for g in LATE[layer]})
+            late = keys('attn%d' % layer)
             wts['attn', layer] = natural('attn', full['attn', layer])
             attn_saved, done = attn_fwd(layer, lengths, inner, wts['attn', layer], small, cos, sin, attn_saved, [full[e] for e in late])
             full.update(zip(late, done))
@@ -826,7 +865,7 @@
             *mlp_saved, y = list(mlp_fwd(layer, attn_saved[5], wts['up', layer], wts['down', layer], small, mlp_saved)) + [x] * layer
         by_layer = [[wts[kind, layer] for layer in range(LAYERS)] for kind in ('up', 'down', 'attn')]
         d_x, *grads = backward(d_y, list(attn_saved) + mlp_saved, x, inner, by_layer, small, cos, sin)
-        g_attn, g_up, g_down, gb_attn, g_ln, gb_up, gb_down = grads
-        return d_x.reshape(x.shape), g_attn, gb_attn, g_ln, g_up, gb_up, g_down, gb_down
+        d_x, g_attn, g_up, g_down, gb_attn, g_ln, gb_up, gb_down = deliver(d_x, *grads)
+        return d_x.reshape(x.shape), g_attn, gb_attn.swapaxes(1, PAIR), g_ln.swapaxes(1, PAIR), g_up, gb_up, g_down, gb_down
 
     return jax.shard_map(device_step, mesh=grid, in_specs=(first,) * 3 + weight_specs, out_specs=(first,) + weight_specs, check_vma=False)

time: 287 us -> 259 us (0.902)
  Pallas kernels: 276 us -> 258 us
  local copies, waits for them, and re-layouts: 10.6 us -> 0 us
    pallas_call x1, Pallas kernels: 158 us -> 139 us  [backward(): pl.pallas_call(backward_kernel, name='backward', grid=(STEPS,), in_specs=...]
    unnamed x20 -> x0, local copies, waits for them, and re-layouts: 10.6 us -> none
    pallas_call x2 -> x3, Pallas kernels: 54.4 us -> 55.6 us  [the longest x2 53.3 us: attn_fwd(): pl.pallas_call(lambda *refs: attn_fwd_kernel('attn%d' % layer, *refs[:n],...]
where the time goes in v3:
time: 259 us
  Pallas kernels  258 us (100%)
    pallas_call x1, Pallas kernels, backward(): pl.pallas_call(backward_kernel, name='backward', grid=(STEPS,), in_specs=...  139 us
    pallas_call x2, Pallas kernels, attn_fwd(): pl.pallas_call(lambda *refs: attn_fwd_kernel('attn%d' % layer, *refs[:n],...  53.3 us
    pallas_call x1, Pallas kernels, gather(): pl.pallas_call(gather_kernel, name='gather', in_specs=in_vmem(len(shards)...  40.6 us
    pallas_call x2, Pallas kernels, mlp_fwd(): pl.pallas_call(lambda *refs: mlp_fwd_kernel(*refs[:n], *refs[n + m:]), na...  23.4 us

profile of v3, /device:TPU:1, one launch (start us, length us, event | category | flops | bytes accessed | tf_op | source)
XLA Modules:
  0.0 259.1 jit_solution(5669179332189956403)
XLA Ops:
  0.6 40.6 %gather.1 = (bf16[4,8,4,2,4,2,2,2,128]{8,7,6,5,4,3,2,1,0:T(2,128)(2,1)}, bf16[4,8,4,2,4,2,2,2,128]{8,7,6,5,4,3,2,1,0:T(2,128)(2,1)}, bf16[8,4,4,2,4,8,128]{6,5,4...) custom-call(bf16[2,4,4,2,128]{4,3,2,1,0:T(2,128)(2,1)} %bitcast.74, ...), custom_call_target="tpu_custom_call" | custom-call | tf_op jit(solution)/shard_map/gather/pallas_call | solution.py:464
  41.3 30.0 %attn_fwd.2 = (bf16[2,2,512,512]{3,2,1,0:T(8,128)(2,1)}, bf16[2,2,512,512]{3,2,1,0:T(8,128)(2,1)}, bf16[2,2,512,512]{3,2,1,0:T(8,128)(2,1)}, bf16[2,2,512,512]{3...) custom-call(s32[2]{0:T(128)} %refs_0_.3, ...), custom_call_target="tpu_custom_call", output_to_operand_aliasing={{7}: (6, {}), {8}: (7, {}), {9}: (8, {})} | custom-call | tf_op jit(solution)/shard_map/attn_fwd/pallas_call | solution.py:561
  71.3 13.5 %mlp_fwd.2 = (bf16[2,2,512,512]{3,2,1,0:T(8,128)(2,1)}, bf16[2,2,512,2048]{3,2,1,0:T(8,128)(2,1)}, f32[2,2,512,2048]{3,2,1,0:T(8,128)}, bf16[2,512,512]{2,1,0:T(8,128)(2,1)}) custom-call(bf16[2,2,512,512]{3,2,1,0:T(8,128)(2,1)} %get-tuple-element.62.refs_0_.refs_11_, bf16[512,2048]{1,0:T(8,128)(2,1)} %bitcast.64, bf16[2048,512]{1,0:T(8,128)(2,1)} %bitcast.62, ...), custom_call_target="tpu_custom_call" | custom-call | tf_op jit(solution)/shard_map/mlp_fwd/pallas_call | solution.py:580
  84.8 23.3 %attn_fwd.3 = (bf16[2,2,512,512]{3,2,1,0:T(8,128)(2,1)}, bf16[2,2,512,512]{3,2,1,0:T(8,128)(2,1)}, bf16[2,2,512,512]{3,2,1,0:T(8,128)(2,1)}, bf16[2,2,512,512]{3...) custom-call(s32[2]{0:T(128)} %refs_0_.3, ...), custom_call_target="tpu_custom_call", output_to_operand_aliasing={{0}: (6, {}), {1}: (7, {}), {2}: (8, {}), {3}: (9, {}), {4}... | custom-call | tf_op jit(solution)/shard_map/attn_fwd/pallas_call | solution.py:561
  108.1 10.0 %mlp_fwd.3 = (bf16[2,2,512,512]{3,2,1,0:T(8,128)(2,1)}, bf16[2,2,512,2048]{3,2,1,0:T(8,128)(2,1)}, f32[2,2,512,2048]{3,2,1,0:T(8,128)}) custom-call(bf16[2,2,512,512]{3,2,1,0:T(8,128)(2,1)} %get-tuple-element.75.refs_0_, bf16[512,2048]{1,0:T(8,128)(2,1)} %bitcast.58, ...), custom_call_target="tpu_custom_call", output_to_operand_aliasing={{0}: (4, {}), {1}: (5, {}), {2}: (6, {})} | custom-call | tf_op jit(solution)/shard_map/mlp_fwd/pallas_call | solution.py:580
  118.0 138.6 %backward.1 = (bf16[1024,512]{1,0:T(8,128)(2,1)}, f32[2,4,2,512]{3,2,1,0:T(2,128)}, f32[2,2,2048]{2,1,0:T(2,128)}, f32[2,8,512]{2,1,0:T(8,128)}, f32[2,2,4]{2,1,...) custom-call(bf16[1024,512]{1,0:T(8,128)(2,1)} %bitcast.73, bf16[2,1024,2048]{2,1,0:T(8,128)(2,1)} %bitcast.54, ...), custom_call_target="tpu_custom_call" | custom-call | tf_op jit(solution)/shard_map/backward/pallas_call | solution.py:824
  256.6 2.3 deliver.1

commit v4 on v3

--- a/solution.py
+++ b/solution.py
@@ -29,9 +29,9 @@
 LAYER_STEPS = MLP_STEPS + ATTN_STEPS
 STEPS = LAYERS * LAYER_STEPS
 SETS = (('up', 'up', ('t', PAIR, CHUNKS)), ('down', 'down', ('z', PAIR, CHUNKS)), ('first', 'part', ('z', OCT, 1)), ('second', 'slim', ('z', OCT, 1)), ('third', 'pair', ('z', OCT, 1)))
-SCHEDULE = {(1, 'small'): 'MNOPST', (1, 'second'): 'LMQUXb', (1, 'third'): 'LMPTWac', (1, 'first'): 'HJNSUWX', (1, 'up'): 'ABCDEJNQU', (1, 'down'): 'ABCDEJMOP',
-            (0, 'up'): 'MNOPQVb', (0, 'down'): 'MNOPQVXc', (0, 'first'): 'TVb', (0, 'second'): 'Xa', (0, 'third'): 'Xa'}
-ENDING = 'lsdltufsldtsfltsftlft'
+SCHEDULE = {(1, 'small'): 'MNOPTU', (1, 'second'): 'LMQUb', (1, 'third'): 'LMPUXd', (1, 'first'): 'HJNSUX', (1, 'up'): 'ABCDEJNU', (1, 'down'): 'ABCDEJMOP',
+            (0, 'up'): 'MNOPQV', (0, 'down'): 'MNOPQVa', (0, 'first'): 'TV', (0, 'second'): 'Xa', (0, 'third'): 'Xa'}
+ENDING = 'lulsftldtusfltdsftlftl'
 VM = 56 << 20
 
 
@@ -58,23 +58,28 @@
             at['x'] = SIZES['l'] * at['h'] + at['l']
         return spot(at)
 
-    def device(self, axis, s):
+    def device(self, axis, s, core=0):
         at = self.shifted(axis, s)
+        if core:
+            at['c'] = other(at)
         return tuple(at[a] for a in AXES)
 
     def peers(self, axis):
         n = SIZES[axis]
         return sorted(range(1, n), key=lambda s: min(s, n - s))
 
-    def signal(self, sem, axis, s):
-        pl.semaphore_signal(sem, inc=1, device_id=self.device(axis, s), device_id_type=pl.DeviceIdType.MESH)
-
-    def greet(self):
-        bar = pltpu.get_barrier_semaphore()
-        everyone = [(a, s) for a in AXES for s in self.peers(a)]
-        for a, s in everyone:
-            self.signal(bar, a, s)
-        pl.semaphore_wait(bar, len(everyone))
+    def signal(self, sem, *to):
+        pl.semaphore_signal(sem, inc=1, device_id=self.device(*to), device_id_type=pl.DeviceIdType.MESH)
+
+    def hello(self, partners=()):
+        everyone = [(a, s, 0) for a in AXES for s in self.peers(a)] + [(a, s, 1) for a in partners for s in self.peers(a)]
+        for e in everyone:
+            self.signal(pltpu.get_barrier_semaphore(), *e)
+        return len(everyone)
+
+    def greet(self, said=None):
+        n = self.hello() if said is None else said
+        pl.semaphore_wait(pltpu.get_barrier_semaphore(), n)
 
     def begin(self, build):
         self.used += 1
@@ -82,12 +87,12 @@
         build().start()
         return lambda: build().wait()
 
-    def copy(self, axis, s, refs):
+    def copy(self, axis, s, refs, core=0):
         i = self.used
 
         def build():
             src, dst = refs()
-            return pltpu.make_async_remote_copy(src, dst, self.send.at[i], self.recv.at[i], device_id=self.device(axis, s), device_id_type=pl.DeviceIdType.MESH)
+            return pltpu.make_async_remote_copy(src, dst, self.send.at[i], self.recv.at[i], device_id=self.device(axis, s, core), device_id_type=pl.DeviceIdType.MESH)
         return self.begin(build)
 
     def local(self, refs):
@@ -171,14 +176,14 @@
     lax.fori_loop(0, math.prod(shape), step, 0)
 
 
-def total_unit(place, value, out, slots):
+def total_unit(place, value, out, slots, axes='xyz'):
     me = place.me
     keep, slot, *slots = slots
     wait = place.copy('c', 1, lambda: (value.at[other(me)], slot.at[0]))
     yield
     wait()
     keep[...] = value[me['c']] + slot[0]
-    for axis, slot in zip('xyz', slots):
+    for axis, slot in zip(axes, slots):
         last = SIZES[axis] - 1
         slot[last] = keep[...]
         waits = [place.copy(axis, s, lambda s=s: (slot.at[last], slot.at[s - 1])) for s in place.peers(axis)]
@@ -196,7 +201,7 @@
 
 
 def total_buffers(n):
-    return [pltpu.VMEM((n, DIM), F32)] + [pltpu.VMEM((SIZES[a], n, DIM), F32) for a in 'cxyz']
+    return [pltpu.VMEM((n, DIM), F32)] + [pltpu.VMEM((OCT, n, DIM), F32)] * QUAD
 
 
 def run(units):
@@ -223,8 +228,12 @@
     later = []
     for layer in range(LAYERS):
         slots = [(SIZES[axis] - 1,) + free_sizes(kind, left) for axis, _, left in plan(kind, layer)]
-        *_, (_, _, left) = plan(kind, layer)
-        later.append([pltpu.VMEM(s, F32) for s in slots[1:] + [free_sizes(kind, left.replace('c', ''))]])
+        *_, (axis, _, left) = plan(kind, layer)
+        if kind == 'down':
+            slots.append(free_sizes(kind, left.replace('c', '')))
+        else:
+            slots[-1] = (PAIR * SIZES[axis],) + free_sizes(kind, left)
+        later.append([pltpu.VMEM(s, F32) for s in slots[1:]])
     return [pltpu.VMEM(s, F32) for s in shapes + slots[:1]], later
 
 
@@ -288,6 +297,21 @@
     grad, names, pick = first, left, {}
     for axis, d, left in later:
         slots, *rest = rest
+        if not rest:
+            far = [(s, core) for s in range(SIZES[axis]) for core in range(CORES) if s or core]
+            waits = [place.copy(axis, s, lambda s=s, core=core: (view(first, names, dict(pick, **only(place.shifted(axis, s), d))), slots.at[PAIR * s + core]), core) for s, core in far]
+            yield
+            for w in waits:
+                w()
+            pick = dict(pick, **only(me, d))
+            rows = pl.ds((me['l'] * PAIR + me['c']) * PAIR, PAIR)
+            mine, away = first[tuple(pick.get(n, ALL) for n in names) + (rows,)], 0
+            for s in range(SIZES[axis]):
+                mine = mine + slots.at[PAIR * s][..., rows, :] if s else mine
+                away = away + slots.at[PAIR * s + 1][..., rows, :]
+            finish(own(me), mine)
+            finish(other(me), away)
+            return
         waits = [place.copy(axis, s, lambda s=s: (view(first, names, dict(pick, **only(place.shifted(axis, s), d))), slots.at[s - 1])) for s in place.peers(axis)]
         yield
         for w in waits:
@@ -295,13 +319,12 @@
         pick = dict(pick, **only(me, d))
         accumulate([slots.at[s] for s in range(SIZES[axis] - 1)], pick, first)
     away, = rest
-    last = (lambda core: dict(pick, c=core(me))) if 'c' in left else (lambda core: pick)
+    last = lambda core: dict(pick, c=core(me))
     wait = place.copy('c', 1, lambda: (view(first, names, last(other)), away))
     yield
     wait()
-    rows = ALL if kind == 'down' else pl.ds((me['l'] * PAIR + me['c']) * PAIR, PAIR)
-    finish(own(me), first[tuple(last(own).get(n, ALL) for n in names) + (rows,)])
-    finish(other(me), away[..., rows, :])
+    finish(own(me), first[tuple(last(own).get(n, ALL) for n in names)])
+    finish(other(me), away[...])
 
 
 def blocks(n):
@@ -404,11 +427,14 @@
 
 
 def host(name, place, t, full, shards):
-    units = []
+    units, said = [], []
 
     @pl.when(t == 0)
     def _():
-        place.greet()
+        said.append(place.hello())
+
+    def start():
+        place.greet(*said)
         units.extend(units_of(name, place, full, shards))
         for u in units:
             next(u)
@@ -423,7 +449,7 @@
         @pl.when(t == pl.num_programs(0) - 1)
         def _():
             run(units)
-    return proceed
+    return start, proceed
 
 
 def gather_kernel(sa, su, sd, b_attn, ln, b_up, b_down, *refs):
@@ -475,7 +501,7 @@
     h_ref, q_ref, k_ref, v_ref, ctx_ref, x1_ref, p_ref, *full = refs[:-2]
     t = pl.program_id(0)
     seq, j = lax.div(t, QUAD), lax.rem(t, QUAD)
-    proceed = host(name, Place(*refs[-2:]), t, dict(zip(keys(name), full)), {})
+    start, proceed = host(name, Place(*refs[-2:]), t, dict(zip(keys(name), full)), {})
 
     @pl.when(j == 0)
     def _():
@@ -497,6 +523,7 @@
                             e = e * cos + swap_halves(e) * sin
                         dst[0, rows, c + WIDE * i:c + WIDE * i + WIDE] = e.astype(BF)
 
+    pl.when(t == 0)(start)
     valid = lax.broadcasted_iota(jnp.int32, (1, SEQ), 1) < len_ref[seq]
     lanes = pl.ds(pl.multiple_of(j * WIDE, WIDE), WIDE)
     masks = [half_mask((SEQ, WIDE), 1, h) for h in range(PAIR)]
@@ -587,14 +614,17 @@
 
 
 def backward_kernel(dy, a, g, q, k, v, p, s, cos_ref, sin_ref, h2, x1, h1, ctx, x0, y0, w1_0, w1_1, w2_0, w2_1, wa_0, wa_1,
-                    d_x, g_attn, g_up, g_down, gb_attn, g_ln, gb_up, gb_down, dx, dmid, dproj, dpre, acc, value, total, w1, w2, wa, h2s, h1s, late, *refs):
-    credits, fetched, *sems = refs[-4:]
+                    d_x, *refs):
+    (g_attn, g_up, g_down, gb_attn, g_ln, gb_up, gb_down), outs, refs = refs[RESULTS:RESULTS + RESULTS], refs[:RESULTS], refs[RESULTS + RESULTS:]
+    made = (g_attn, g_up, g_down, gb_attn, g_ln, gb_up, gb_down)
+    (dx, dmid, dproj, dpre, acc, value, total, w1, w2, wa, h2s, h1s, late, *refs) = refs
+    credits, fetched, written, *sems = refs[-5:]
     t = pl.program_id(0)
     layer, r = 1 - lax.div(t, LAYER_STEPS), lax.rem(t, LAYER_STEPS)
     place = Place(*sems)
     me = place.me
     n = len(total_buffers(1))
-    slots, last_slots, refs = refs[:n], refs[n:n + n], refs[n + n:-4]
+    slots, last_slots, refs = refs[:n], refs[n:n + n], refs[n + n:-5]
 
     def finish_of(name, l):
         def finish(core, part):
@@ -640,9 +670,11 @@
     def load(name, l):
         return pltpu.make_async_copy(loads[name][l], loads[name][-1], fetched.at[list(loads).index(name)])
 
+    said = []
+
     @pl.when(t == 0)
     def _():
-        place.greet()
+        said.append(place.hello('xl'))
         dx[...] = dy[...]
         value[...] = jnp.zeros_like(value)
 
@@ -661,16 +693,16 @@
         for i, e in zip(rows, terms):
             value[layer, i // OCT, i % OCT:i % OCT + 1] += jnp.sum(e, axis=0, keepdims=True)
 
-    @pl.when(r == 0)
-    def _():
-        for name in ('w2', 'w1', 'h2'):
-            load(name, 0).wait()
-
     @pl.when(r < MLP_STEPS)
     def _():
         gw = dot(a[...], dx[...], 0, 0)
         for i in range(QUAD):
             put(grads['down'], (i // PAIR, pl.ds(PAIR * r, PAIR), ALL, ALL, ALL, i % PAIR), gw[:, lane(i)], (PAIR, QUAD, QUAD, CORES))
+
+        @pl.when(r == 0)
+        def _():
+            for name in ('w2', 'w1', 'h2'):
+                load(name, 0).wait()
         chunk = pl.ds(pl.multiple_of(r * CHUNK, CHUNK), CHUNK)
         bias = jnp.zeros((1, DIM), F32)
         for e in blocks(TOKENS):
@@ -760,6 +792,10 @@
                 for gen in due:
                     next(gen, 0)
 
+    @pl.when(t == 0)
+    def _():
+        place.greet(*said)
+
     for step in range(STEPS):
         advance(chr(ord('A') + step), t == step)
 
@@ -784,7 +820,7 @@
         for i in range(QUAD):
             result(i).start()
         left = {name[0]: gens[0, name] for name, _, _ in SETS}
-        left['l'] = total_unit(place, value.at[0], total.at[0], last_slots)
+        left['l'] = total_unit(place, value.at[0], total.at[0], last_slots, 'zyx')
         for letter in ENDING:
             next(left[letter], 0)
         run(left.values())
@@ -802,8 +838,14 @@
                 gb_attn[l, i:i + 1], g_ln[l, i:i + 1] = e[:, :QUAD], e[:, QUAD:]
                 gb_down[l:l + 1, i:i + 1] = across(jnp.where(here, total[l, 1], 0.0))[:, QUAD:QUAD + 1]
             gb_up[l:l + 1] = across(sum(jnp.where(lanes + DIM * n == OCT * index + rows, total[l, 1, n:n + 1], 0.0) for n in range(QUAD)))
-        for i in range(QUAD):
-            result(i).wait()
+        copies = [pltpu.make_async_copy(src, dst, written.at[i]) for i, (src, dst) in enumerate(zip(made, outs))]
+        for e in copies:
+            e.start()
+        for e in copies + [result(i) for i in range(QUAD)]:
+            e.wait()
+
+
+RESULTS = 7
 
 
 def backward(dy, saved, x0, y0, wts, s, cos, sin):
@@ -826,11 +868,11 @@
         in_specs=[whole((TOKENS, DIM), **once), cols, cols, head, head, head,
                   pl.BlockSpec((None, None, PAIR, SEQ, SEQ), lambda t: (layer(t), seq(t), pair(t), 0, 0)),
                   pl.BlockSpec((None, SMALL, DIM), lambda t: (layer(t), 0, 0)), whole((SEQ, WIDE), **once), whole((SEQ, WIDE), **once)] + any_space(len(late)),
-        out_specs=any_space(1) + in_vmem(len(shapes)),
+        out_specs=any_space(1 + len(shapes)),
         out_shape=[SD((TOKENS, DIM), BF)] + [SD(e, F32) for e in shapes],
-        scratch_shapes=[act, act, pltpu.VMEM((MATRICES - 1, TOKENS, DIM), BF), act, pltpu.VMEM((TOKENS, DIM), F32), small, small,
+        scratch_shapes=[pltpu.VMEM(e, F32) for e in shapes] + [act, act, pltpu.VMEM((MATRICES - 1, TOKENS, DIM), BF), act, pltpu.VMEM((TOKENS, DIM), F32), small, small,
                         pltpu.VMEM((DIM, FFN), BF), pltpu.VMEM((FFN, DIM), BF), pltpu.VMEM((MATRICES, DIM, DIM), BF), act, act, act]
-        + total_buffers(OCT) * LAYERS + bufs + [pltpu.SemaphoreType.REGULAR((PAIR * len(SETS),)), pltpu.SemaphoreType.DMA((SMALL,))] + semaphores(240),
+        + total_buffers(OCT) * LAYERS + bufs + [pltpu.SemaphoreType.REGULAR((PAIR * len(SETS),)), pltpu.SemaphoreType.DMA((SMALL,)), pltpu.SemaphoreType.DMA((RESULTS,))] + semaphores(260),
         compiler_params=pltpu.CompilerParams(collective_id=SMALL, has_side_effects=True, vmem_limit_bytes=67043328),
     )(flat(dy), flat(a), flat(g), q, k, v, p, s, cos, sin, *late)
 

time: 259 us -> 252 us (0.973)
  Pallas kernels: 258 us -> 251 us
    pallas_call x1, Pallas kernels: 139 us -> 132 us  [backward(): pl.pallas_call(backward_kernel, name='backward', grid=(STEPS,), in_specs=...]
where the time goes in v4:
time: 252 us; the launch traced here: 251 us
  Pallas kernels  251 us (100%)
    pallas_call x1, Pallas kernels, backward(): pl.pallas_call(backward_kernel, name='backward', grid=(STEPS,), in_specs=...  132 us
    pallas_call x2, Pallas kernels, attn_fwd(): pl.pallas_call(lambda *refs: attn_fwd_kernel('attn%d' % layer, *refs[:n],...  52.3 us
    pallas_call x1, Pallas kernels, gather(): pl.pallas_call(gather_kernel, name='gather', in_specs=in_vmem(len(shards)...  40.6 us
    pallas_call x2, Pallas kernels, mlp_fwd(): pl.pallas_call(lambda *refs: mlp_fwd_kernel(*refs[:n], *refs[n + m:]), na...  23.4 us

profile of v4, /device:TPU:1, one launch (start us, length us, event | category | flops | bytes accessed | tf_op | source)
XLA Modules:
  0.0 251.5 jit_solution(2452251507228682651)
XLA Ops:
  0.6 40.6 %gather.1 = (bf16[4,8,4,2,4,2,2,2,128]{8,7,6,5,4,3,2,1,0:T(2,128)(2,1)}, bf16[4,8,4,2,4,2,2,2,128]{8,7,6,5,4,3,2,1,0:T(2,128)(2,1)}, bf16[8,4,4,2,4,8,128]{6,5,4...) custom-call(bf16[2,4,4,2,128]{4,3,2,1,0:T(2,128)(2,1)} %bitcast.74, ...), custom_call_target="tpu_custom_call" | custom-call | tf_op jit(solution)/shard_map/gather/pallas_call | solution.py:490
  41.3 30.0 %attn_fwd.2 = (bf16[2,2,512,512]{3,2,1,0:T(8,128)(2,1)}, bf16[2,2,512,512]{3,2,1,0:T(8,128)(2,1)}, bf16[2,2,512,512]{3,2,1,0:T(8,128)(2,1)}, bf16[2,2,512,512]{3...) custom-call(s32[2]{0:T(128)} %refs_0_.3, ...), custom_call_target="tpu_custom_call", output_to_operand_aliasing={{7}: (6, {}), {8}: (7, {}), {9}: (8, {})} | custom-call | tf_op jit(solution)/shard_map/attn_fwd/pallas_call | solution.py:588
  71.3 13.5 %mlp_fwd.2 = (bf16[2,2,512,512]{3,2,1,0:T(8,128)(2,1)}, bf16[2,2,512,2048]{3,2,1,0:T(8,128)(2,1)}, f32[2,2,512,2048]{3,2,1,0:T(8,128)}, bf16[2,512,512]{2,1,0:T(8,128)(2,1)}) custom-call(bf16[2,2,512,512]{3,2,1,0:T(8,128)(2,1)} %get-tuple-element.62.refs_0_.refs_11_, bf16[512,2048]{1,0:T(8,128)(2,1)} %bitcast.64, bf16[2048,512]{1,0:T(8,128)(2,1)} %bitcast.62, ...), custom_call_target="tpu_custom_call" | custom-call | tf_op jit(solution)/shard_map/mlp_fwd/pallas_call | solution.py:607
  84.8 22.3 %attn_fwd.3 = (bf16[2,2,512,512]{3,2,1,0:T(8,128)(2,1)}, bf16[2,2,512,512]{3,2,1,0:T(8,128)(2,1)}, bf16[2,2,512,512]{3,2,1,0:T(8,128)(2,1)}, bf16[2,2,512,512]{3...) custom-call(s32[2]{0:T(128)} %refs_0_.3, ...), custom_call_target="tpu_custom_call", output_to_operand_aliasing={{0}: (6, {}), {1}: (7, {}), {2}: (8, {}), {3}: (9, {}), {4}... | custom-call | tf_op jit(solution)/shard_map/attn_fwd/pallas_call | solution.py:588
  107.1 10.0 %mlp_fwd.3 = (bf16[2,2,512,512]{3,2,1,0:T(8,128)(2,1)}, bf16[2,2,512,2048]{3,2,1,0:T(8,128)(2,1)}, f32[2,2,512,2048]{3,2,1,0:T(8,128)}) custom-call(bf16[2,2,512,512]{3,2,1,0:T(8,128)(2,1)} %get-tuple-element.75.refs_0_, bf16[512,2048]{1,0:T(8,128)(2,1)} %bitcast.58, ...), custom_call_target="tpu_custom_call", output_to_operand_aliasing={{0}: (4, {}), {1}: (5, {}), {2}: (6, {})} | custom-call | tf_op jit(solution)/shard_map/mlp_fwd/pallas_call | solution.py:607
  117.1 131.9 %backward.1 = (bf16[1024,512]{1,0:T(8,128)(2,1)}, f32[2,4,2,512]{3,2,1,0:T(2,128)}, f32[2,2,2048]{2,1,0:T(2,128)}, f32[2,8,512]{2,1,0:T(8,128)}, f32[2,2,4]{2,1,...) custom-call(bf16[1024,512]{1,0:T(8,128)(2,1)} %bitcast.73, bf16[2,1024,2048]{2,1,0:T(8,128)(2,1)} %bitcast.54, ...), custom_call_target="tpu_custom_call" | custom-call | tf_op jit(solution)/shard_map/backward/pallas_call | solution.py:866
  249.0 2.3 deliver.1

commit v5 on v4

--- a/solution.py
+++ b/solution.py
@@ -29,9 +29,9 @@
 LAYER_STEPS = MLP_STEPS + ATTN_STEPS
 STEPS = LAYERS * LAYER_STEPS
 SETS = (('up', 'up', ('t', PAIR, CHUNKS)), ('down', 'down', ('z', PAIR, CHUNKS)), ('first', 'part', ('z', OCT, 1)), ('second', 'slim', ('z', OCT, 1)), ('third', 'pair', ('z', OCT, 1)))
-SCHEDULE = {(1, 'small'): 'MNOPTU', (1, 'second'): 'LMQUb', (1, 'third'): 'LMPUXd', (1, 'first'): 'HJNSUX', (1, 'up'): 'ABCDEJNU', (1, 'down'): 'ABCDEJMOP',
-            (0, 'up'): 'MNOPQV', (0, 'down'): 'MNOPQVa', (0, 'first'): 'TV', (0, 'second'): 'Xa', (0, 'third'): 'Xa'}
-ENDING = 'lulsftldtusfltdsftlftl'
+SCHEDULE = {(1, 'small'): 'MNOPTU', (1, 'second'): 'LMQUb', (1, 'third'): 'LMPUX', (1, 'first'): 'HJNSUX', (1, 'up'): 'ABCDEJNU', (1, 'down'): 'ABCDEJMOP',
+            (0, 'up'): 'MNOPQV', (0, 'down'): 'MNOPQW', (0, 'first'): 'TVc', (0, 'second'): 'Xa', (0, 'third'): 'Xa'}
+ENDING = 'lduls3tfldtsufltdsftlftl'
 VM = 56 << 20
 
 
@@ -446,7 +446,7 @@
                 for i in digits:
                     next(units[int(i)], 0)
 
-        @pl.when(t == pl.num_programs(0) - 1)
+        @pl.when(t == OCT - 1)
         def _():
             run(units)
     return start, proceed
@@ -499,8 +499,8 @@
 
 def attn_fwd_kernel(name, len_ref, x_ref, w_ref, s_ref, cos_ref, sin_ref, *refs):
     h_ref, q_ref, k_ref, v_ref, ctx_ref, x1_ref, p_ref, *full = refs[:-2]
-    t = pl.program_id(0)
-    seq, j = lax.div(t, QUAD), lax.rem(t, QUAD)
+    seq, j = pl.program_id(0), pl.program_id(1)
+    t = seq * QUAD + j
     start, proceed = host(name, Place(*refs[-2:]), t, dict(zip(keys(name), full)), {})
 
     @pl.when(j == 0)
@@ -533,11 +533,11 @@
 
     def score(r, h):
         return dot(q_ref[0, pl.ds(r, BLOCK), lanes], ks[h], 1, 1)
-    ahead, ctx = score(*chains[0]), 0
+    ahead, ctx = [score(*c) for c in chains[:PAIR]], 0
     for i, (r, h) in enumerate(chains):
-        s = jnp.where(valid, ahead, NEG_BIG)
-        if i + 1 < len(chains):
-            ahead = score(*chains[i + 1])
+        s = jnp.where(valid, ahead.pop(0), NEG_BIG)
+        if i + PAIR < len(chains):
+            ahead.append(score(*chains[i + PAIR]))
         e = jnp.exp(s - jnp.max(s, axis=-1, keepdims=True))
         p = (e * (1.0 / jnp.sum(e, axis=-1, keepdims=True))).astype(BF)
         p_ref[0, h, pl.ds(r, BLOCK)] = p
@@ -579,14 +579,13 @@
 
 
 def attn_fwd(layer, lengths, x, w, s, cos, sin, prev, late):
-    seq = lambda t: (lax.div(t, QUAD), 0, 0)
-    t = pl.BlockSpec((1, SEQ, DIM), seq)
-    saved = [pl.BlockSpec((None, 1, SEQ, DIM), lambda t: (layer,) + seq(t))] * 6
-    saved.append(pl.BlockSpec((None, 1, PAIR, SEQ, SEQ), lambda t: (layer, lax.div(t, QUAD), lax.rem(t, QUAD), 0, 0)))
+    t = pl.BlockSpec((1, SEQ, DIM), lambda i, j: (i, 0, 0))
+    saved = [pl.BlockSpec((None, 1, SEQ, DIM), lambda i, j: (layer, i, 0, 0))] * 6
+    saved.append(pl.BlockSpec((None, 1, PAIR, SEQ, SEQ), lambda i, j: (layer, i, j, 0, 0)))
     inputs = [lengths, x, w, s, cos, sin]
     n, m = len(inputs), len(prev)
     res = pl.pallas_call(
-        lambda *refs: attn_fwd_kernel('attn%d' % layer, *refs[:n], *refs[n + m + len(late):]), name='attn_fwd', grid=(OCT,),
+        lambda *refs: attn_fwd_kernel('attn%d' % layer, *refs[:n], *refs[n + m + len(late):]), name='attn_fwd', grid=(SEQS, QUAD),
         in_specs=[pl.BlockSpec(memory_space=pltpu.SMEM), t, whole((MATRICES, DIM, DIM)), layer_small(layer), whole((SEQ, WIDE)), whole((SEQ, WIDE))] + any_space(m + len(late)),
         out_specs=saved + any_space(len(late)),
         out_shape=[SD((LAYERS, SEQS, SEQ, DIM), BF)] * 6 + [SD((LAYERS, SEQS, HEADS, SEQ, SEQ), BF)] + [SD(e.shape, BF) for e in late],
@@ -598,14 +597,13 @@
 
 
 def mlp_fwd(layer, x1, w1, w2, s, prev):
-    place = lambda t: (layer, lax.div(t, PAIR), lax.rem(t, PAIR), 0)
-    block = lambda n: pl.BlockSpec((None, 1, BLOCK, n), place)
+    block = lambda n: pl.BlockSpec((None, 1, BLOCK, n), lambda i, j: (layer, i, j, 0))
     widths = [(DIM, BF), (FFN, BF), (FFN, F32)]
-    outs = [block(w) for w, _ in widths] + [pl.BlockSpec((1, BLOCK, DIM), lambda t: place(t)[1:])] * (1 - layer)
+    outs = [block(w) for w, _ in widths] + [pl.BlockSpec((1, BLOCK, DIM), lambda i, j: (i, j, 0))] * (1 - layer)
     inputs = [x1, w1, w2, s]
     n, m = len(inputs), len(prev)
     return pl.pallas_call(
-        lambda *refs: mlp_fwd_kernel(*refs[:n], *refs[n + m:]), name='mlp_fwd', grid=(QUAD,),
+        lambda *refs: mlp_fwd_kernel(*refs[:n], *refs[n + m:]), name='mlp_fwd', grid=(SEQS, PAIR),
         in_specs=[block(DIM), whole((DIM, FFN)), whole((FFN, DIM)), layer_small(layer)] + any_space(m), out_specs=outs,
         out_shape=[SD((LAYERS, SEQS, SEQ, w), d) for w, d in widths] + [SD((SEQS, SEQ, DIM), BF)] * (1 - layer),
         input_output_aliases={n + i: i for i in range(m)},
@@ -619,8 +617,8 @@
     made = (g_attn, g_up, g_down, gb_attn, g_ln, gb_up, gb_down)
     (dx, dmid, dproj, dpre, acc, value, total, w1, w2, wa, h2s, h1s, late, *refs) = refs
     credits, fetched, written, *sems = refs[-5:]
-    t = pl.program_id(0)
-    layer, r = 1 - lax.div(t, LAYER_STEPS), lax.rem(t, LAYER_STEPS)
+    layer, r = 1 - pl.program_id(0), pl.program_id(1)
+    t = (1 - layer) * LAYER_STEPS + r
     place = Place(*sems)
     me = place.me
     n = len(total_buffers(1))
@@ -748,19 +746,26 @@
         dc = dot(dmid[rows], wa[BIAS_OUT, lanes], 1, 1).astype(BF)
         qt, dct = qv.T, dc.T
         dq, dkt, dvt = 0, 0, 0
-        for h in range(PAIR):
-            m = half_mask((SEQ, WIDE), 1, h)
-            mt = half_mask((WIDE, SEQ), 0, h)
-            kh, vh = jnp.where(m, kv, 0), jnp.where(m, vv, 0)
-            dvt = dvt + dot(jnp.where(mt, dct, 0), p[h])
-            ds = []
-            for b in blocks(SEQ):
-                pf = p[h, pl.ds(b, BLOCK)].astype(F32)
-                dp = dot(dc[b:b + BLOCK], vh, 1, 1)
-                ds.append((pf * (dp - jnp.sum(dp * pf, axis=-1, keepdims=True))).astype(BF))
-            ds = jnp.concatenate(ds, axis=0)
-            dq = dq + dot(ds, kh)
-            dkt = dkt + dot(jnp.where(mt, qt, 0), ds)
+        masks = [half_mask((SEQ, WIDE), 1, h) for h in range(PAIR)]
+        ks, vs = ([jnp.where(m, e, 0) for m in masks] for e in (kv, vv))
+        chains = [(h, b) for h in range(PAIR) for b in blocks(SEQ)]
+
+        def slope(h, b):
+            return dot(dc[b:b + BLOCK], vs[h], 1, 1)
+        ahead, ds = [slope(*c) for c in chains[:PAIR]], []
+        for i, (h, b) in enumerate(chains):
+            dp = ahead.pop(0)
+            if i + PAIR < len(chains):
+                ahead.append(slope(*chains[i + PAIR]))
+            pf = p[h, pl.ds(b, BLOCK)].astype(F32)
+            ds.append((pf * (dp - jnp.sum(dp * pf, axis=-1, keepdims=True))).astype(BF))
+            if len(ds) == SEQ // BLOCK:
+                mt = half_mask((WIDE, SEQ), 0, h)
+                dvt = dvt + dot(jnp.where(mt, dct, 0), p[h])
+                whole_ds = jnp.concatenate(ds, axis=0)
+                dq = dq + dot(whole_ds, ks[h])
+                dkt = dkt + dot(jnp.where(mt, qt, 0), whole_ds)
+                ds = []
         cos, sin = cos_ref[...], sin_ref[...]
         dk = dkt.T
         dproj[0, rows, lanes] = ((dq * cos - swap_halves(dq) * sin) * (HEAD_DIM ** -0.5)).astype(BF)
@@ -820,6 +825,7 @@
         for i in range(QUAD):
             result(i).start()
         left = {name[0]: gens[0, name] for name, _, _ in SETS}
+        left['3'] = gens[1, 'third']
         left['l'] = total_unit(place, value.at[0], total.at[0], last_slots, 'zyx')
         for letter in ENDING:
             next(left[letter], 0)
@@ -851,23 +857,21 @@
 def backward(dy, saved, x0, y0, wts, s, cos, sin):
     h1, q, k, v, ctx, x1, p, h2, a, g = saved
     once = dict(pipeline_mode=pl.Buffered(1))
-    layer = lambda t: 1 - lax.div(t, LAYER_STEPS)
-    chunk = lambda t: jnp.minimum(lax.rem(t, LAYER_STEPS), CHUNKS - 1)
-    head_of = lambda t: jnp.maximum(lax.rem(t, LAYER_STEPS) - MLP_STEPS, 0)
-    seq = lambda t: lax.rem(head_of(t), SEQS)
-    pair = lambda t: lax.div(head_of(t), SEQS)
+    chunk = lambda r: jnp.minimum(r, CHUNKS - 1)
+    seq = lambda r: lax.rem(jnp.maximum(r - MLP_STEPS, 0), SEQS)
+    pair = lambda r: lax.div(jnp.maximum(r - MLP_STEPS, 0), SEQS)
     flat = lambda e: e.reshape(*e.shape[:-3], TOKENS, e.shape[-1])
-    cols = pl.BlockSpec((None, TOKENS, CHUNK), lambda t: (layer(t), 0, chunk(t)))
-    head = pl.BlockSpec((None, None, SEQ, WIDE), lambda t: (layer(t), seq(t), 0, pair(t)))
+    cols = pl.BlockSpec((None, TOKENS, CHUNK), lambda i, r: (1 - i, 0, chunk(r)))
+    head = pl.BlockSpec((None, None, SEQ, WIDE), lambda i, r: (1 - i, seq(r), 0, pair(r)))
     late = [flat(e) for e in (h2, x1, h1, ctx, x0, y0)] + [w for pair_of in wts for w in pair_of]
     act, small = pltpu.VMEM((TOKENS, DIM), BF), pltpu.VMEM((LAYERS, CORES, OCT, DIM), F32)
     bufs = [e for _, kind, _ in SETS for group in (unit_buffers(kind)[0], *unit_buffers(kind)[1]) for e in group]
     shapes = [(LAYERS, MATRICES, PAIR, DIM), (LAYERS, PAIR, FFN), (LAYERS, OCT, DIM), (LAYERS, PAIR, QUAD), (LAYERS, PAIR, QUAD), (LAYERS, OCT), (LAYERS, PAIR)]
     return pl.pallas_call(
-        backward_kernel, name='backward', grid=(STEPS,),
+        backward_kernel, name='backward', grid=(LAYERS, LAYER_STEPS),
         in_specs=[whole((TOKENS, DIM), **once), cols, cols, head, head, head,
-                  pl.BlockSpec((None, None, PAIR, SEQ, SEQ), lambda t: (layer(t), seq(t), pair(t), 0, 0)),
-                  pl.BlockSpec((None, SMALL, DIM), lambda t: (layer(t), 0, 0)), whole((SEQ, WIDE), **once), whole((SEQ, WIDE), **once)] + any_space(len(late)),
+                  pl.BlockSpec((None, None, PAIR, SEQ, SEQ), lambda i, r: (1 - i, seq(r), pair(r), 0, 0)),
+                  pl.BlockSpec((None, SMALL, DIM), lambda i, r: (1 - i, 0, 0)), whole((SEQ, WIDE), **once), whole((SEQ, WIDE), **once)] + any_space(len(late)),
         out_specs=any_space(1 + len(shapes)),
         out_shape=[SD((TOKENS, DIM), BF)] + [SD(e, F32) for e in shapes],
         scratch_shapes=[pltpu.VMEM(e, F32) for e in shapes] + [act, act, pltpu.VMEM((MATRICES - 1, TOKENS, DIM), BF), act, pltpu.VMEM((TOKENS, DIM), F32), small, small,

time: 252 us -> 250 us (level)
  no operation moved by 1% of the time
where the time goes in v5:
time: 250 us; the launch traced here: 249 us
  Pallas kernels  249 us (100%)
    pallas_call x1, Pallas kernels, backward(): pl.pallas_call(backward_kernel, name='backward', grid=(LAYERS, LAYER_STEP...  130 us
    pallas_call x2, Pallas kernels, attn_fwd(): pl.pallas_call(lambda *refs: attn_fwd_kernel('attn%d' % layer, *refs[:n],...  52.4 us
    pallas_call x1, Pallas kernels, gather(): pl.pallas_call(gather_kernel, name='gather', in_specs=in_vmem(len(shards)...  40.6 us
    pallas_call x2, Pallas kernels, mlp_fwd(): pl.pallas_call(lambda *refs: mlp_fwd_kernel(*refs[:n], *refs[n + m:]), na...  23.4 us

profile of v5, /device:TPU:1, one launch (start us, length us, event | category | flops | bytes accessed | tf_op | source)
XLA Modules:
  0.0 249.4 jit_solution(14847431657980603860)
XLA Ops:
  0.6 40.6 %gather.1 = (bf16[4,8,4,2,4,2,2,2,128]{8,7,6,5,4,3,2,1,0:T(2,128)(2,1)}, bf16[4,8,4,2,4,2,2,2,128]{8,7,6,5,4,3,2,1,0:T(2,128)(2,1)}, bf16[8,4,4,2,4,8,128]{6,5,4...) custom-call(bf16[2,4,4,2,128]{4,3,2,1,0:T(2,128)(2,1)} %bitcast.74, ...), custom_call_target="tpu_custom_call" | custom-call | tf_op jit(solution)/shard_map/gather/pallas_call | solution.py:490
  41.3 30.2 %attn_fwd.2 = (bf16[2,2,512,512]{3,2,1,0:T(8,128)(2,1)}, bf16[2,2,512,512]{3,2,1,0:T(8,128)(2,1)}, bf16[2,2,512,512]{3,2,1,0:T(8,128)(2,1)}, bf16[2,2,512,512]{3...) custom-call(s32[2]{0:T(128)} %refs_0_.3, ...), custom_call_target="tpu_custom_call", output_to_operand_aliasing={{7}: (6, {}), {8}: (7, {}), {9}: (8, {})} | custom-call | tf_op jit(solution)/shard_map/attn_fwd/pallas_call | solution.py:587
  71.4 13.5 %mlp_fwd.2 = (bf16[2,2,512,512]{3,2,1,0:T(8,128)(2,1)}, bf16[2,2,512,2048]{3,2,1,0:T(8,128)(2,1)}, f32[2,2,512,2048]{3,2,1,0:T(8,128)}, bf16[2,512,512]{2,1,0:T(8,128)(2,1)}) custom-call(bf16[2,2,512,512]{3,2,1,0:T(8,128)(2,1)} %get-tuple-element.62.refs_0_.refs_11_, bf16[512,2048]{1,0:T(8,128)(2,1)} %bitcast.64, bf16[2048,512]{1,0:T(8,128)(2,1)} %bitcast.62, ...), custom_call_target="tpu_custom_call" | custom-call | tf_op jit(solution)/shard_map/mlp_fwd/pallas_call | solution.py:605
  84.9 22.3 %attn_fwd.3 = (bf16[2,2,512,512]{3,2,1,0:T(8,128)(2,1)}, bf16[2,2,512,512]{3,2,1,0:T(8,128)(2,1)}, bf16[2,2,512,512]{3,2,1,0:T(8,128)(2,1)}, bf16[2,2,512,512]{3...) custom-call(s32[2]{0:T(128)} %refs_0_.3, ...), custom_call_target="tpu_custom_call", output_to_operand_aliasing={{0}: (6, {}), {1}: (7, {}), {2}: (8, {}), {3}: (9, {}), {4}... | custom-call | tf_op jit(solution)/shard_map/attn_fwd/pallas_call | solution.py:587
  107.2 10.0 %mlp_fwd.3 = (bf16[2,2,512,512]{3,2,1,0:T(8,128)(2,1)}, bf16[2,2,512,2048]{3,2,1,0:T(8,128)(2,1)}, f32[2,2,512,2048]{3,2,1,0:T(8,128)}) custom-call(bf16[2,2,512,512]{3,2,1,0:T(8,128)(2,1)} %get-tuple-element.75.refs_0_, bf16[512,2048]{1,0:T(8,128)(2,1)} %bitcast.58, ...), custom_call_target="tpu_custom_call", output_to_operand_aliasing={{0}: (4, {}), {1}: (5, {}), {2}: (6, {})} | custom-call | tf_op jit(solution)/shard_map/mlp_fwd/pallas_call | solution.py:605
  117.2 129.8 %backward.1 = (bf16[1024,512]{1,0:T(8,128)(2,1)}, f32[2,4,2,512]{3,2,1,0:T(2,128)}, f32[2,2,2048]{2,1,0:T(2,128)}, f32[2,8,512]{2,1,0:T(8,128)}, f32[2,2,4]{2,1,...) custom-call(bf16[1024,512]{1,0:T(8,128)(2,1)} %bitcast.73, bf16[2,1024,2048]{2,1,0:T(8,128)(2,1)} %bitcast.54, ...), custom_call_target="tpu_custom_call" | custom-call | tf_op jit(solution)/shard_map/backward/pallas_call | solution.py:870
  247.0 2.3 deliver.1
